TPU v7x, 32 devices: a whole 2x2x4 slice. The times are simulated.
32 devices in a mesh: cfg: 2 (over x), seq: 16 (over z, y, core).
Axes of the slice: x: 2, y: 2, z: 4, core: 2. Of those that a mesh axis runs over, the one named last changes fastest.
Arguments:
- hidden: bfloat16 [2, 2048, 1920], P('cfg', 'seq'), may hold values from -6 to 6
- modulation: float32 [6, 1920], replicated, may hold values from -3 to 3
- w_qkv: bfloat16 [3, 1920, 1024], replicated, may hold values from -0.125 to 0.125
- q_gain: float32 [64], replicated, may hold values from 1 to 13, as said below
- k_gain: float32 [64], replicated, may hold values from 1 to 13, as said below
- w_out: bfloat16 [1024, 1920], replicated, may hold values from -0.1875 to 0.1875
- text_count: int32 [2], P('cfg'), may hold values from 1 to 226
- block_order: int32 [16], P('seq'), may hold values from 0 to 15, each once
Outputs:
- guided: float32 [2048, 1920], P('seq', 'cfg')
Inputs may be any that keep to these rules, and one draw needn't show every extreme that they name: text_count[b] is how many of the 226 text positions of branch b (0 conditional, 1 unconditional) hold prompt tokens; keys at the other text positions are masked. Seq index j holds positions block_order[j] * 128 to block_order[j] * 128 + 127; every block appears once. `q_gain`: one gain for each of the 64 entries of a head, shared by all heads. `k_gain`: one gain for each of the 64 entries of a head, shared by all heads.
All inputs are finite; a program needn't handle non-finite values.
Results may differ from a plain program's by a relative error of at most 0.015.
The roundings to bfloat16 on the way count: a program that leaves them out, or rounds other values in their place, can miss the bound.
Values may be sent and summed in bfloat16 or wider, within the bound.
No kernel may reach another device: no remote copies, remote signals or barrier semaphores. Data moves between devices by JAX's collectives and lax.ppermute only.
A program may use at most 256 MiB of HBM per device.

v0:
```python
import jax
import jax.numpy as jnp
from jax import lax
from jax.sharding import PartitionSpec as P

HEAD = 64
HEADS = 16
TXT = 226


GUIDANCE = 6.0
EPSILON = 1e-05
MASKED = -1000000000.0


def swapped(block, axis, apart):
    count = lax.axis_size(axis)
    route = []
    for low in range(count):
        high = low | 1 << apart
        if high != low and high < count:
            route += [(low, high), (high, low)]
    return lax.ppermute(block, axis, route)


def layer_normal(values_in):
    average = jnp.mean(values_in, axis=-1, keepdims=True)
    centred = values_in - average
    spread = jnp.mean(centred * centred, axis=-1, keepdims=True)
    return centred * lax.rsqrt(spread + EPSILON)


def modulated(states, is_text, modulation):
    normed = layer_normal(states.astype(jnp.float32))
    shift = jnp.where(is_text[:, None], modulation[3][None, :], modulation[0][None, :])
    scale = jnp.where(is_text[:, None], modulation[4][None, :], modulation[1][None, :])
    return (normed * (1.0 + scale) + shift).astype(jnp.bfloat16)


def head_normal(projected, gain):
    rows = projected.shape[0]
    heads_view = projected.reshape(rows, HEADS, HEAD)
    return (layer_normal(heads_view) * gain).reshape(rows, HEADS * HEAD).astype(jnp.bfloat16)


def projections(states, is_text, modulation, w_qkv, q_gain, k_gain):
    modded = modulated(states, is_text, modulation)
    query = head_normal(jnp.dot(modded, w_qkv[0], preferred_element_type=jnp.float32), q_gain)
    keys = head_normal(jnp.dot(modded, w_qkv[1], preferred_element_type=jnp.float32), k_gain)
    values = jnp.dot(modded, w_qkv[2], preferred_element_type=jnp.float32).astype(jnp.bfloat16)
    return (query, keys, values)


def fold_block(query_heads, carry, piece):
    highest, total, numer = carry
    keys_piece, values_piece, bias_piece = piece
    count = keys_piece.shape[0]
    key_heads = keys_piece.reshape(count, HEADS, HEAD)
    value_heads = values_piece.reshape(count, HEADS, HEAD)
    scores = jnp.einsum("qhd,khd->hqk", query_heads, key_heads, preferred_element_type=jnp.float32)
    scores = scores * HEAD ** (-0.5) + bias_piece.astype(jnp.float32)[None, None, :]
    new_high = jnp.maximum(highest, jnp.max(scores, axis=-1))
    expo = jnp.exp(scores - new_high[:, :, None])
    rescale = jnp.exp(highest - new_high)
    total = jnp.sum(expo, axis=-1)
    numer = numer * rescale.T[:, :, None] + jnp.einsum(
        "hqk,khd->qhd", expo.astype(jnp.bfloat16), value_heads, preferred_element_type=jnp.float32
    )
    return (new_high, total, numer)


def shards(hidden, modulation, w_qkv, q_gain, k_gain, w_out, text_count, block_order):
    states = hidden[0]
    tok_rows = states.shape[0]
    within = jnp.arange(tok_rows, dtype=jnp.int32)
    position = block_order[0] * tok_rows + within
    is_text = position < TXT
    keep = jnp.logical_or(position >= TXT, position < text_count[0])
    key_bias = jnp.where(keep, 0.0, MASKED).astype(jnp.bfloat16)
    query, keys, values = projections(states, is_text, modulation, w_qkv, q_gain, k_gain)
    query_heads = query.reshape(tok_rows, HEADS, HEAD)
    start_state = (
        jnp.full((HEADS, tok_rows), -1e30, jnp.float32),
        jnp.zeros((HEADS, tok_rows), jnp.float32),
        jnp.zeros((tok_rows, HEADS, HEAD), jnp.float32),
    )
    carry = fold_block(
        query_heads,
        start_state,
        (
            lax.all_gather(keys, "seq", axis=0, tiled=True),
            lax.all_gather(values, "seq", axis=0, tiled=True),
            lax.all_gather(key_bias, "seq", axis=0, tiled=True),
        ),
    )
    highest, total, numer = carry
    attended = (numer / total.T[:, :, None]).reshape(tok_rows, HEADS * HEAD).astype(jnp.bfloat16)
    gate = jnp.where(is_text[:, None], modulation[5][None, :], modulation[2][None, :])
    cfg_index = lax.axis_index("cfg")
    half_width = w_out.shape[1] // 2
    w_half = lax.dynamic_slice_in_dim(w_out, cfg_index * half_width, half_width, 1)
    gate_half = lax.dynamic_slice_in_dim(gate, cfg_index * half_width, half_width, 1)
    partner = swapped(attended, "cfg", 0)
    own_update = gate_half * jnp.dot(attended, w_half, preferred_element_type=jnp.float32)
    other_update = gate_half * jnp.dot(partner, w_half, preferred_element_type=jnp.float32)
    is_first = cfg_index == 0
    cond = jnp.where(is_first, own_update, other_update)
    uncond = jnp.where(is_first, other_update, own_update)
    return uncond + GUIDANCE * (cond - uncond)


def solution(mesh):
    in_specs = (P("cfg", "seq", None), P(), P(), P(), P(), P(), P("cfg"), P("seq"))
    out_specs = P("seq", "cfg")
    return jax.shard_map(shards, mesh=mesh, in_specs=in_specs, out_specs=out_specs, check_vma=False)
```

profile of v0, /device:TPU:0, one launch (start us, length us, event | category | flops | bytes accessed | tf_op | source)
XLA Modules:
  0.0 170.8 jit_solution(8093386982138254050)
XLA Ops:
  6.5 0.0 all-gather.4.cloned.1.call-start
  6.5 1.2 slice_reduce_fusion.5
  7.8 1.2 convert_reduce_fusion
  8.9 1.3 fusion.39
  10.9 5.6 %slice_bitcast_fusion.1 = (bf16[1024,1920]{0,1:T(8,128)(2,1)}, bf16[1024,1920]{0,1:T(8,128)(2,1)}) fusion(bf16[3,1920,1024]{2,1,0:T(8,128)(2,1)} %param.10), kind=kLoop, calls=%fused_computation.10 | loop fusion | bytes 15728640 | tf_op jit(solution)/shard_map/dot_general | solution.py:48
  16.6 6.3 %copy.16 = bf16[1024,1920]{1,0:T(8,128)(2,1)} copy(bf16[1024,1920]{0,1:T(8,128)(2,1)} %get-tuple-element.12) | data formatting | bytes 7864320 | tf_op jit(solution)/shard_map/dot_general | solution.py:49
  22.8 0.0 copy-done.1
  22.9 3.5 %fusion.60 = (f32[128,16]{0,1:T(8,128)S(1)}, f32[128,16,64]{0,2,1:T(8,128)S(1)}) fusion(bf16[16,64,1920]{2,1,0:T(8,128)(2,1)} %bitcast.65, f32[1920]{0:T(1024)S(1)} %get-tuple-element.9, f32[1920]{0:T(1024)S(1)} %get-tuple-element.10, f32[1920]{0:T(1024)S(1)} %get-tuple-element.6, f32[1920]{0:T(1024)S(1)} %get-tuple-element.7, ...), kind=kOutput, calls=%fused_computation.68 | convolution fusion | flops 505657344 | bytes 4988032 | tf_op jit(solution)/shard_map/dot_general | solution.py:49
  26.3 0.1 multiply_reduce_fusion
  26.4 0.8 multiply_convert_fusion
  27.3 0.0 all-gather.4.cloned.1.call-update
  27.3 0.0 all-gather.6.cloned.1.call-start
  27.3 3.7 %fusion.24 = bf16[128,1024]{1,0:T(8,128)(2,1)} fusion(bf16[3,1920,1024]{2,1,0:T(8,128)(2,1)} %param.10, bf16[1,128,1920]{2,1,0:T(8,128)(2,1)S(1)} %copy-done.1, f32[1920]{0:T(1024)S(1)} %get-tuple-element.9, f32[1920]{0:T(1024)S(1)} %get-tuple-element.10, f32[1920]{0:T(1024)S(1)} %get-tuple-element.6, f32[1920]{0:T(1024)S(1)} %get-tuple-element.7, ...), kind=kOutput, calls=%fused_computation.22 | convolution fusion | flops 505659392 | bytes 4717696 | tf_op jit(solution)/shard_map/dot_general | solution.py:50
  31.0 0.0 all-gather.6.cloned.1.call-update
  31.1 6.2 %copy.15 = bf16[1024,1920]{1,0:T(8,128)(2,1)} copy(bf16[1024,1920]{0,1:T(8,128)(2,1)} %get-tuple-element.11) | data formatting | bytes 7864320 | tf_op jit(solution)/shard_map/dot_general | solution.py:48
  38.0 23.4 %all-gather = bf16[16,1,128]{2,1,0:T(2,128)(2,1)S(1)} all-gather(bf16[1,1,128]{2,1,0:T(2,128)(2,1)S(1)} %fusion.52), channel_id=1, replica_groups=mesh['cfg'=2,'seq'=16] {'seq'}, dimensions={0}, use_global_device_ids=true | all-gather | bytes 4352 | tf_op jit(solution)/shard_map/all_gather | solution.py:93
  61.3 0.0 copy-start.2
  61.4 3.4 %fusion.61 = (f32[128,16]{0,1:T(8,128)S(1)}, f32[128,16,64]{0,2,1:T(8,128)S(1)}) fusion(bf16[16,64,1920]{2,1,0:T(8,128)(2,1)} %bitcast.64, f32[1920]{0:T(1024)S(1)} %get-tuple-element.9, f32[1920]{0:T(1024)S(1)} %get-tuple-element.10, f32[1920]{0:T(1024)S(1)} %get-tuple-element.6, f32[1920]{0:T(1024)S(1)} %get-tuple-element.7, ...), kind=kOutput, calls=%fused_computation.69 | convolution fusion | flops 505657344 | bytes 4988032 | tf_op jit(solution)/shard_map/dot_general | solution.py:48
  64.8 0.1 multiply_reduce_fusion.1
  64.9 17.7 %all-gather.4.cloned.1.call-done = bf16[2048,1024]{0,1:T(8,128)(2,1)} async-done(((bf16[128,1024]{0,1:T(8,128)(2,1)}), bf16[2048,1024]{0,1:T(8,128)(2,1)}) %all-gather.4.cloned.1.call-update) | async-done | bytes 4194320 | tf_op jit(solution)/shard_map/all_gather | solution.py:91
  82.6 4.5 %fusion = (f32[16,128]{1,0:T(8,128)S(1)}, f32[16,128,2048]{2,1,0:T(8,128)S(1)}) fusion(f32[2048]{0:T(1024)S(1)} %bitcast.69, bf16[2048,16,64]{0,2,1:T(8,128)(2,1)} %bitcast.62, f32[128,16,64]{0,2,1:T(8,128)S(1)} %get-tuple-element.18, f32[64]{0:T(128)S(1)} %copy-done.2, f32[128,16]{0,1:T(8,128)S(1)} %add_rsqrt_fusion.1, ...), kind=kOutput, calls=%fused_computation.2 | convolution fusion | flops 549976064 | bytes 21528832 | tf_op jit(solution)/shard_map/qhd,khd->hqk/dot_general | solution.py:60
  87.2 5.8 %copy-done = f32[16,128,2048]{2,1,0:T(8,128)} copy-done((f32[16,128,2048]{2,1,0:T(8,128)}, f32[16,128,2048]{2,1,0:T(8,128)S(1)}, u32[]{:S(2)}) %copy-start) | copy-done | bytes 16777240
  93.0 3.8 %fusion.1 = f32[16,128]{1,0:T(8,128)S(1)} fusion(f32[16,128,2048]{2,1,0:T(8,128)S(1)} %get-tuple-element.20, f32[16,128]{1,0:T(8,128)S(1)} %get-tuple-element.14, f32[2048]{0:T(1024)S(1)} %bitcast.70), kind=kLoop, calls=%fused_computation.3 | loop fusion | flops 16775168 | bytes 16801792 | tf_op jit(solution)/shard_map/reduce_sum | solution.py:65
  96.8 36.6 %all-gather.6.cloned.1.call-done = bf16[2048,1024]{1,0:T(8,128)(2,1)} async-done(((bf16[128,1024]{1,0:T(8,128)(2,1)}), bf16[2048,1024]{1,0:T(8,128)(2,1)}) %all-gather.6.cloned.1.call-update) | async-done | bytes 4194320 | tf_op jit(solution)/shard_map/all_gather | solution.py:92
  133.4 6.5 %copy.17 = bf16[2048,1024]{0,1:T(8,128)(2,1)} copy(bf16[2048,1024]{1,0:T(8,128)(2,1)} %all-gather.6.cloned.1.call-done) | data formatting | bytes 8388608 | tf_op jit(solution)/shard_map/all_gather | solution.py:92
  139.9 11.1 %fusion.30 = bf16[128,16,64]{0,2,1:T(8,128)(2,1)S(1)} fusion(bf16[2048,16,64]{0,2,1:T(8,128)(2,1)} %bitcast.63, f32[16,128,2048]{2,1,0:T(8,128)} %copy-done, f32[16,128]{1,0:T(8,128)S(1)} %get-tuple-element.14, f32[2048]{0:T(1024)S(1)} %bitcast.71, f32[128,16]{0,1:T(8,128)S(1)} %bitcast.72, f32[128,16]{0,1:T(8,128)S(1)} %get-tuple-element.13), kind=kOutput, calls=%fused_computation.24 | convolution fusion | flops 554041344 | bytes 21266432 | tf_op jit(solution)/shard_map/hqk,khd->qhd/dot_general | solution.py:66
  151.0 1.5 collective-permute-start
  152.5 0.1 dynamic-slice
  152.6 0.1 dynamic-slice.1
  152.7 3.7 %fusion.18 = f32[128,960]{0,1:T(8,128)S(1)} fusion(bf16[128,1024]{0,1:T(8,128)(2,1)S(1)} %bitcast.68, bf16[1024,1920]{1,0:T(8,128)(2,1)} %param.13, s32[]{:T(128)S(6)} %select_n.50, f32[960]{0:T(1024)S(1)} %dynamic-slice.1, f32[960]{0:T(1024)S(1)} %dynamic-slice, pred[128]{0:T(512)(128)(4,1)S(1)} %fusion.53), kind=kOutput, calls=%fused_computation.20 | convolution fusion | flops 251904000 | bytes 2858628 | tf_op jit(solution)/shard_map/dot_general | solution.py:104
  156.4 3.2 %collective-permute-done = bf16[128,1024]{0,1:T(8,128)(2,1)S(1)} collective-permute-done((bf16[128,1024]{0,1:T(8,128)(2,1)S(1)}, bf16[128,1024]{0,1:T(8,128)(2,1)S(1)}, u32[]{:S(2)}, u32[]{:S(2)}) %collective-permute-start) | collective-permute-done | bytes 262176 | tf_op jit(solution)/shard_map/ppermute | solution.py:23
  159.5 4.5 %multiply_add_fusion.1 = f32[128,960]{0,1:T(8,128)} fusion(f32[128,960]{0,1:T(8,128)S(1)} %fusion.18, bf16[128,1024]{0,1:T(8,128)(2,1)S(1)} %collective-permute-done, bf16[1024,1920]{1,0:T(8,128)(2,1)} %param.13, s32[]{:T(128)S(6)} %select_n.50, f32[960]{0:T(1024)S(1)} %dynamic-slice.1, f32[960]{0:T(1024)S(1)} %dynamic-slice, ...), kind=kOutput, calls=%fused_computation.41 | convolution fusion | flops 252518400 | bytes 3350149 | tf_op jit(solution)/shard_map/dot_general | solution.py:105
  (15 shorter events, 0.1 us)
Async XLA Ops:
  6.5 76.1 %all-gather.4.cloned.1.call-start = ((), (), s32[]{:S(2)}) async-start(), calls=%async_computation | async-start | bytes 4456448 | tf_op jit(solution)/shard_map/all_gather | solution.py:91
  16.6 6.3 %copy-start.1 = (bf16[1,128,1920]{2,1,0:T(8,128)(2,1)S(1)}, bf16[1,128,1920]{2,1,0:T(8,128)(2,1)}, u32[]{:S(2)}) copy-start(bf16[1,128,1920]{2,1,0:T(8,128)(2,1)} %param.8) | copy-start | bytes 1474564
  22.9 3.6 %copy-start.3 = (f32[64]{0:T(128)S(1)}, f32[64]{0:T(128)}, u32[]{:S(2)}) copy-start(f32[64]{0:T(128)} %param.12) | copy-start | bytes 772
  27.3 106.1 %all-gather.6.cloned.1.call-start = ((), (), s32[]{:S(2)}) async-start(), calls=%async_computation.1 | async-start | bytes 4456448 | tf_op jit(solution)/shard_map/all_gather | solution.py:92
  61.3 21.3 %copy-start.2 = (f32[64]{0:T(128)S(1)}, f32[64]{0:T(128)}, u32[]{:S(2)}) copy-start(f32[64]{0:T(128)} %param.11) | copy-start | bytes 772
  87.2 5.8 %copy-start = (f32[16,128,2048]{2,1,0:T(8,128)}, f32[16,128,2048]{2,1,0:T(8,128)S(1)}, u32[]{:S(2)}) copy-start(f32[16,128,2048]{2,1,0:T(8,128)S(1)} %get-tuple-element.20) | copy-start | bytes 50331652
  151.0 8.5 %collective-permute-start = (bf16[128,1024]{0,1:T(8,128)(2,1)S(1)}, bf16[128,1024]{0,1:T(8,128)(2,1)S(1)}, u32[]{:S(2)}, u32[]{:S(2)}) collective-permute-start(bf16[128,1024]{0,1:T(8,128)(2,1)S(1)} %bitcast.67), channel_id=1, source_target_pairs={{0,16},{16,0},{1,17},{17,1},{2,18},{18,2},{3,19},{19,3},{4,20},{20... | collective-permute-start | bytes 786440 | tf_op jit(solution)/shard_map/ppermute | solution.py:23
Sparse Core Ops, SparseCore 0:
  27.4 55.1 all-gather.3
  84.8 48.5 all-gather.5
where the time goes:
time: 172 us; the launch traced here: 171 us
  waiting for transfers between devices  57.5 us (33%)
  matrix products  34.4 us (20%)
  local copies, waits for them, and re-layouts  31.8 us (18%)
  blocking collectives  23.4 us (14%)
  between operations  14.8 us (9%)
  other arithmetic  7.31 us (4%)
    all_gather x1, waiting for transfers between devices, shards(): lax.all_gather(values, 'seq', axis=0, tiled=True)  36.6 us
    all_gather x1, blocking collectives, shards(): lax.all_gather(key_bias, 'seq', axis=0, tiled=True)  23.4 us
    all_gather x1, waiting for transfers between devices, shards(): lax.all_gather(keys, 'seq', axis=0, tiled=True)  17.7 us
    dot_general x2, local copies, waits for them, and re-layouts, projections(): jnp.dot(modded, w_qkv[0], preferred_element_type=jnp.float32)  11.9 us
    dot_general x1, matrix products, fold_block(): jnp.einsum('hqk,khd->qhd', expo.astype(jnp.bfloat16), value_heads, prefer...  11.1 us
    all_gather x1, local copies, waits for them, and re-layouts, shards(): lax.all_gather(values, 'seq', axis=0, tiled=True)  6.51 us
    dot_general x1, local copies, waits for them, and re-layouts, projections(): jnp.dot(modded, w_qkv[1], preferred_element_type=jnp.float32)  6.29 us
    unnamed x8, local copies, waits for them, and re-layouts  5.81 us
  transfers between devices with their start and end apart: 3, of which 3 were waited for; matrix products, arithmetic and copies ran while one was open for 15% of the time, Pallas kernels for 0%

commit v1 on v0

v1 whole, which is shorter than its diff:
```python
import functools

import jax
import jax.numpy as jnp
from jax import lax
from jax.experimental import pallas as pl
from jax.experimental.pallas import tpu as pltpu
from jax.sharding import PartitionSpec as P

TXT = 226
GUIDANCE = 6.0
EPSILON = 1e-05
MASKED = -1000000000.0
WAYS = 4
LANES = 128
EXTRA = 16


def text_rows(block, rows):
    within = lax.broadcasted_iota(jnp.int32, (rows, 1), 0)
    return block * rows + within < TXT


def modulate(block, states, modulation_ref):
    average = jnp.mean(states, axis=-1, keepdims=True)
    centred = states - average
    spread = jnp.mean(centred * centred, axis=-1, keepdims=True)
    normed = centred * lax.rsqrt(spread + EPSILON)
    is_text = text_rows(block, states.shape[0])
    table = modulation_ref[...]
    shift = jnp.where(is_text, table[3:4, :], table[0:1, :])
    scale = jnp.where(is_text, table[4:5, :], table[1:2, :])
    return (normed * (1.0 + scale) + shift).astype(jnp.bfloat16)


def head_normal(tile, gain, head):
    lane = lax.broadcasted_iota(jnp.int32, (1, LANES), 1)

    def average(x):
        mean = jnp.zeros(x.shape, jnp.float32)
        for first in range(0, LANES, head):
            inside = (lane >= first) & (lane < first + head)
            total = jnp.sum(jnp.where(inside, x, 0.0), axis=-1, keepdims=True)
            mean = jnp.where(inside, total * (1.0 / head), mean)
        return mean

    centred = tile - average(tile)
    return centred * lax.rsqrt(average(centred * centred) + EPSILON) * gain


def wide(gain):
    return jnp.concatenate([gain] * (LANES // gain.shape[1]), axis=-1)


def key_value_kernel(block_ref, count_ref, hidden_ref, modulation_ref, w_ref, gain_ref, *refs, head, groups):
    slots, (modded_ref, w_all, sems) = refs[:WAYS], refs[WAYS:]
    copies = [pltpu.make_async_copy(w_ref.at[1 + i], w_all.at[i], sems.at[i]) for i in range(2)]
    for copy in copies:
        copy.start()
    block = block_ref[0]
    modded_ref[...] = modulate(block, hidden_ref[...].astype(jnp.float32), modulation_ref)
    rows = modded_ref.shape[0]
    width = w_all.shape[2] // WAYS
    gain = wide(gain_ref[...])
    way = lax.axis_index("seq") // groups
    position = block * rows + lax.broadcasted_iota(jnp.int32, (EXTRA, rows), 1)
    keep = (position >= TXT) | (position < count_ref[0])
    bias = jnp.where(keep, 0.0, MASKED).astype(jnp.bfloat16)
    starts = [pl.multiple_of((way ^ slot) * width, width) for slot in range(WAYS)]
    copies[0].wait()
    for slot in range(WAYS):
        w = w_all[0, :, pl.ds(starts[slot], width)]
        keys = jnp.dot(modded_ref[...], w, preferred_element_type=jnp.float32)
        for tile in range(width // LANES):
            normed = head_normal(keys[:, tile * LANES : (tile + 1) * LANES], gain, head)
            slots[slot][tile * rows : (tile + 1) * rows, :] = normed.astype(jnp.bfloat16)
        at = rows * (width // LANES)
        slots[slot][at : at + EXTRA, :] = bias
    copies[1].wait()
    for slot in range(WAYS):
        w = w_all[1, :, pl.ds(starts[slot], width)]
        values = jnp.dot(modded_ref[...], w, preferred_element_type=jnp.float32)
        slots[slot][at + EXTRA :, :] = values.T.astype(jnp.bfloat16)


def query_kernel(modded_ref, w_ref, gain_ref, *refs, head, groups):
    slots, (w_all, sem) = refs[:WAYS], refs[WAYS:]
    copy = pltpu.make_async_copy(w_ref.at[0], w_all, sem)
    copy.start()
    width = w_all.shape[1] // WAYS
    gain = wide(gain_ref[...])
    way = lax.axis_index("seq") // groups
    copy.wait()
    for slot in range(WAYS):
        start = pl.multiple_of((way ^ slot) * width, width)
        query = jnp.dot(modded_ref[...], w_all[:, pl.ds(start, width)], preferred_element_type=jnp.float32)
        for tile in range(width // LANES):
            at = slice(tile * LANES, (tile + 1) * LANES)
            normed = head_normal(query[:, at], gain, head).astype(jnp.bfloat16)
            slots[slot][:, at] = normed * jnp.asarray(head ** (-0.5), jnp.bfloat16)


def attention_kernel(*refs, held, head):
    queries, refs = refs[:WAYS], refs[WAYS:]
    pieces, refs = refs[:held], refs[held:]
    outs, (k_all, v_all, b_all, q_all, o_all) = refs[:WAYS], refs[WAYS:]
    rows, width = queries[0].shape
    heads = width // head
    tiles = width // LANES
    deep = head + EXTRA
    size = tiles * rows + EXTRA + width
    each = pieces[0].shape[0] // size
    biases = []
    for g in range(held):
        for p in range(each):
            to, at = (g * each + p) * rows, p * size
            for tile in range(tiles):
                k_all[to : to + rows, tile * LANES : (tile + 1) * LANES] = pieces[g][at + tile * rows : at + (tile + 1) * rows, :]
            at += tiles * rows
            biases.append(pieces[g][at : at + EXTRA, :].astype(jnp.float32)[0:1, :])
            at += EXTRA
            for h in range(heads):
                v_all[h, :head, to : to + rows] = pieces[g][at + h * head : at + (h + 1) * head, :]
    for h in range(heads):
        v_all[h, head:, :] = jnp.ones((EXTRA, v_all.shape[2]), jnp.bfloat16)
    for first in range(0, len(biases), LANES):
        some = biases[first : first + LANES]
        fill = [jnp.zeros((LANES - len(some), LANES), jnp.float32)] if len(some) < LANES else []
        columns = jnp.concatenate(some + fill, axis=0).T
        for i in range(len(some)):
            to = (first + i) * rows
            b_all[to : to + rows, :] = jnp.broadcast_to(columns[:, i : i + 1], (rows, LANES))
    for slot in range(WAYS):
        q_all[slot * rows : (slot + 1) * rows, :] = queries[slot][...]
    lane = lax.broadcasted_iota(jnp.int32, (1, width), 1)
    span = 2 * rows

    def one_block(index, _):
        query = q_all[pl.ds(pl.multiple_of(index * span, span), span), :]
        columns = []
        for h in range(heads):
            inside = (lane >= h * head) & (lane < (h + 1) * head)
            masked = jnp.where(inside, query, jnp.zeros_like(query))
            scores = lax.dot_general(k_all[...], masked, (((1,), (1,)), ((), ())), preferred_element_type=jnp.float32)
            bias = b_all[...]
            scores = scores + jnp.concatenate([bias] * (span // LANES), axis=-1)
            expo = jnp.exp(scores - jnp.max(scores, axis=0, keepdims=True)).astype(jnp.bfloat16)
            numer = jnp.dot(v_all[h], expo, preferred_element_type=jnp.float32)
            columns.append(numer[:head, :] / numer[head : head + 1, :])
        o_all[index] = jnp.concatenate(columns, axis=0)
        return 0

    lax.fori_loop(0, WAYS // 2, one_block, 0)
    for slot in range(WAYS):
        at = (slot % 2) * rows
        outs[slot][...] = o_all[slot // 2, :, at : at + rows].T.astype(jnp.bfloat16)


def project(pieces_ref, w_ref, way, start, span):
    width = pieces_ref.shape[1]
    rows = pieces_ref.shape[0] // WAYS
    total = jnp.zeros((rows, span), jnp.float32)
    for slot in range(WAYS):
        at = pl.multiple_of((way ^ slot) * width, width)
        w = w_ref[pl.ds(at, width), pl.ds(start, span)]
        total += jnp.dot(pieces_ref[slot * rows : (slot + 1) * rows, :], w, preferred_element_type=jnp.float32)
    return total


def half_of(total):
    half = total // 2
    spare = half % LANES
    span = half + spare
    start = pl.multiple_of(lax.axis_index("cfg") * (half - spare), LANES)
    return half, spare, span, start


def own_kernel(pieces_ref, w_ref, out_ref, *, groups):
    _, _, span, start = half_of(w_ref.shape[1])
    out_ref[...] = project(pieces_ref, w_ref, lax.axis_index("seq") // groups, start, span)


def final_kernel(block_ref, pieces_ref, own_ref, w_ref, modulation_ref, out_ref, *, groups):
    half, spare, span, start = half_of(w_ref.shape[1])
    total = project(pieces_ref, w_ref, lax.axis_index("seq") // groups, start, span)
    is_text = text_rows(block_ref[0], total.shape[0])
    table = modulation_ref[:, pl.ds(start, span)]
    gate = jnp.where(is_text, table[5:6, :], table[2:3, :])
    other = gate * total
    own = gate * own_ref[...]
    is_first = lax.axis_index("cfg") == 0
    cond = jnp.where(is_first, own, other)
    uncond = jnp.where(is_first, other, own)
    guided = (uncond + GUIDANCE * (cond - uncond)).T
    out_ref[...] = jnp.where(is_first, guided[:half, :], guided[spare:, :])


def shards(hidden, modulation, w_qkv, q_gain, k_gain, w_out, text_count, block_order):
    states = hidden[0]
    rows, features = states.shape
    head = q_gain.shape[0]
    inner = w_qkv.shape[2]
    width = inner // WAYS
    count = lax.axis_size("seq")
    groups = count // WAYS
    bf16 = jnp.bfloat16
    smem = pl.BlockSpec(memory_space=pltpu.SMEM)
    vmem = pl.BlockSpec(memory_space=pltpu.VMEM)
    hbm = pl.BlockSpec(memory_space=pl.ANY)

    def exchange(block, bits):
        return lax.ppermute(block, "seq", [(i, i ^ bits) for i in range(count)])

    def spread(slots):
        far = {s: exchange(slots[s], s * groups) for s in reversed(range(1, WAYS))}
        return [slots[0]] + [far[s] for s in range(1, WAYS)]

    size = (width // LANES) * rows + EXTRA + width
    kv_piece = jax.ShapeDtypeStruct((size, LANES), bf16)
    piece = jax.ShapeDtypeStruct((rows, width), bf16)
    *kv_slots, modded = pl.pallas_call(
        functools.partial(key_value_kernel, head=head, groups=groups),
        in_specs=[smem, smem, vmem, vmem, hbm, vmem],
        out_shape=[kv_piece] * WAYS + [jax.ShapeDtypeStruct((rows, features), bf16)],
        scratch_shapes=[pltpu.VMEM((2, features, inner), bf16), pltpu.SemaphoreType.DMA((2,))],
    )(block_order, text_count, states, modulation, w_qkv, k_gain[None, :])
    kv = spread(kv_slots)
    q_slots = pl.pallas_call(
        functools.partial(query_kernel, head=head, groups=groups),
        in_specs=[vmem, hbm, vmem],
        out_shape=[piece] * WAYS,
        scratch_shapes=[pltpu.VMEM((features, inner), bf16), pltpu.SemaphoreType.DMA],
    )(modded, w_qkv, q_gain[None, :])
    queries = spread(q_slots)
    held = [jnp.concatenate(kv[i : i + 2], axis=0) for i in range(0, WAYS, 2)]
    bit = groups // 2
    while bit:
        held = held + [exchange(x, bit) for x in held]
        bit //= 2

    keys = count * rows
    o_slots = pl.pallas_call(
        functools.partial(attention_kernel, held=len(held), head=head),
        in_specs=[vmem] * (WAYS + len(held)),
        out_shape=[piece] * WAYS,
        scratch_shapes=[
            pltpu.VMEM((keys, width), bf16),
            pltpu.VMEM((width // head, head + EXTRA, keys), bf16),
            pltpu.VMEM((keys, LANES), jnp.float32),
            pltpu.VMEM((WAYS * rows, width), bf16),
            pltpu.VMEM((WAYS // 2, width, 2 * rows), jnp.float32),
        ],
    )(*queries, *held)
    attended = jnp.concatenate(spread(o_slots), axis=0)
    cfg_count = lax.axis_size("cfg")
    partner = lax.ppermute(attended, "cfg", [(i, i ^ 1) for i in range(cfg_count)])

    half = w_out.shape[1] // 2
    span = half + half % LANES
    own = pl.pallas_call(
        functools.partial(own_kernel, groups=groups),
        in_specs=[vmem] * 2,
        out_shape=jax.ShapeDtypeStruct((rows, span), jnp.float32),
    )(attended, w_out)
    guided = pl.pallas_call(
        functools.partial(final_kernel, groups=groups),
        in_specs=[smem] + [vmem] * 4,
        out_shape=jax.ShapeDtypeStruct((half, rows), jnp.float32),
    )(block_order, partner, own, w_out, modulation)
    return guided.T


def solution(mesh):
    in_specs = (P("cfg", "seq", None), P(), P(), P(), P(), P(), P("cfg"), P("seq"))
    out_specs = P("seq", "cfg")
    return jax.shard_map(shards, mesh=mesh, in_specs=in_specs, out_specs=out_specs, check_vma=False)
```

time: 172 us -> 87.5 us (0.51)
  matrix products: 34.4 us -> 0 us
  Pallas kernels: 0 us -> 30.8 us
  waiting for transfers between devices: 57.5 us -> 27.4 us
  local copies, waits for them, and re-layouts: 31.8 us -> 3.44 us
  blocking collectives: 23.4 us -> 0 us
  starting transfers between devices: 1.58 us -> 24 us
  between operations: 14.8 us -> 1.48 us
  other arithmetic: 7.31 us -> 0 us
    all_gather x2 -> x0, waiting for transfers between devices: 54.3 us -> none  [the longest x1 36.6 us: shards(): lax.all_gather(values, 'seq', axis=0, tiled=True)]
    dot_general x7 -> x0, matrix products: 34.4 us -> none  [the longest x1 11.1 us: fold_block(): jnp.einsum('hqk,khd->qhd', expo.astype(jnp.bfloat16), value_heads, prefer...]
    pallas_call x0 -> x5, Pallas kernels: none -> 30.8 us  [the longest x1 12.5 us: shards(): pl.pallas_call(functools.partial(attention_kernel, held=len(held), head=h...]
    ppermute x1 -> x16, waiting for transfers between devices: 3.16 us -> 27.4 us  [the longest x15 26 us: exchange(): return lax.ppermute(block, 'seq', [(i, i ^ bits) for i in range(count)])]
    all_gather x1 -> x0, blocking collectives: 23.4 us -> none  [shards(): lax.all_gather(key_bias, 'seq', axis=0, tiled=True)]
    ppermute x1 -> x16, starting transfers between devices: 1.53 us -> 24 us  [the longest x15 22.4 us: exchange(): return lax.ppermute(block, 'seq', [(i, i ^ bits) for i in range(count)])]
    dot_general x3 -> x0, local copies, waits for them, and re-layouts: 18.1 us -> none  [the longest x2 11.9 us: projections(): jnp.dot(modded, w_qkv[0], preferred_element_type=jnp.float32)]
    all_gather x1 -> x0, local copies, waits for them, and re-layouts: 6.51 us -> none  [shards(): lax.all_gather(values, 'seq', axis=0, tiled=True)]
  transfers between devices with their start and end apart: 3 -> 16, of which waited for: 3 -> 9; matrix products, arithmetic and copies ran while one was open for 15% -> 2% of each run, Pallas kernels for 0% -> 10%
where the time goes in v1:
time: 87.5 us; the launch traced here: 87.2 us
  Pallas kernels  30.8 us (35%)
  waiting for transfers between devices  27.4 us (31%)
  starting transfers between devices  24 us (27%)
  local copies, waits for them, and re-layouts  3.44 us (4%)
  between operations  1.48 us (2%)
    ppermute x15, waiting for transfers between devices, exchange(): return lax.ppermute(block, 'seq', [(i, i ^ bits) for i in range(count)])  26 us
    ppermute x15, starting transfers between devices, exchange(): return lax.ppermute(block, 'seq', [(i, i ^ bits) for i in range(count)])  22.4 us
    pallas_call x1, Pallas kernels, shards(): pl.pallas_call(functools.partial(attention_kernel, held=len(held), head=h...  12.5 us
    pallas_call x1, Pallas kernels, shards(): pl.pallas_call(functools.partial(key_value_kernel, head=head, groups=grou...  6.12 us
    pallas_call x1, Pallas kernels, shards(): pl.pallas_call(functools.partial(query_kernel, head=head, groups=groups),...  5 us
    pallas_call x1, Pallas kernels, shards(): pl.pallas_call(functools.partial(final_kernel, groups=groups), in_specs=[...  3.73 us
    pallas_call x1, Pallas kernels, shards(): pl.pallas_call(functools.partial(own_kernel, groups=groups), in_specs=[vm...  3.47 us
    unnamed x31, local copies, waits for them, and re-layouts  3.4 us
  transfers between devices with their start and end apart: 16, of which 9 were waited for; matrix products, arithmetic and copies ran while one was open for 2% of the time, Pallas kernels for 10%

profile of v1, /device:TPU:0, one launch (start us, length us, event | category | flops | bytes accessed | tf_op | source)
XLA Modules:
  0.0 87.2 jit_solution(802696132180906707)
XLA Ops:
  1.3 6.1 %shard_map.82 = (bf16[528,128]{1,0:T(8,128)(2,1)}, bf16[528,128]{1,0:T(8,128)(2,1)}, bf16[528,128]{1,0:T(8,128)(2,1)}, bf16[528,128]{1,0:T(8,128)(2,1)}, bf16[128,1920]{1,0:T(8,128)(2,1)}) custom-call(s32[1]{0:T(128)S(6)} %copy.15.block_ref, s32[1]{0:T(128)S(6)} %copy.14.count_ref, bf16[128,1920]{1,0:T(8,128)(2,1)} %bitcast.4, f32[6,1920]{1,0:T(8,128)} %modulation_ref.3, ...), custom_call_target="tpu_custom_call" | custom-call | tf_op jit(solution)/shard_map/pallas_call | solution.py:221
  7.4 3.1 %collective-permute-start.3 = (bf16[528,128]{1,0:T(8,128)(2,1)}, bf16[528,128]{1,0:T(8,128)(2,1)S(1)}, u32[]{:S(2)}, u32[]{:S(2)}) collective-permute-start(bf16[528,128]{1,0:T(8,128)(2,1)} %get-tuple-element.24), channel_id=1, source_target_pairs={{0,4},{1,5},{2,6},{3,7},{4,0},{5,1},{6,2},{7,3},{8,12},{9,13},{10,... | collective-permute-start | bytes 405512 | tf_op jit(solution)/shard_map/ppermute | solution.py:212
  10.5 2.6 %collective-permute-start.4 = (bf16[528,128]{1,0:T(8,128)(2,1)}, bf16[528,128]{1,0:T(8,128)(2,1)S(1)}, u32[]{:S(2)}, u32[]{:S(2)}) collective-permute-start(bf16[528,128]{1,0:T(8,128)(2,1)} %get-tuple-element.25), channel_id=1, source_target_pairs={{0,8},{1,9},{2,10},{3,11},{4,12},{5,13},{6,14},{7,15},{8,0},{9,1},... | collective-permute-start | bytes 405512 | tf_op jit(solution)/shard_map/ppermute | solution.py:212
  13.1 0.9 %constant_dynamic-update-slice_fusion.1 = bf16[1056,128]{1,0:T(8,128)(2,1)S(1)} fusion(bf16[528,128]{1,0:T(8,128)(2,1)} %get-tuple-element.23), kind=kLoop, calls=%fused_computation.1 | loop fusion | bytes 270336
  14.0 2.0 %collective-permute-done.3 = bf16[528,128]{1,0:T(8,128)(2,1)S(1)} collective-permute-done((bf16[528,128]{1,0:T(8,128)(2,1)}, bf16[528,128]{1,0:T(8,128)(2,1)S(1)}, u32[]{:S(2)}, u32[]{:S(2)}) %collective-permute-start.3) | collective-permute-done | bytes 135200 | tf_op jit(solution)/shard_map/ppermute | solution.py:212
  16.1 1.8 %collective-permute-start.6 = (bf16[1056,128]{1,0:T(8,128)(2,1)S(1)}, bf16[1056,128]{1,0:T(8,128)(2,1)S(1)}, u32[]{:S(2)}, u32[]{:S(2)}) collective-permute-start(bf16[1056,128]{1,0:T(8,128)(2,1)S(1)} %constant_dynamic-update-slice_fusion.refs_4_), channel_id=1, source_target_pairs={{0,2},{1,3},{2,0},{3,1},{4,6},{5,7},{6,4},{7,5},{8,10},{9,11},{10,... | collective-permute-start | bytes 811016 | tf_op jit(solution)/shard_map/ppermute | solution.py:212
  17.9 6.0 %collective-permute-done.4 = bf16[528,128]{1,0:T(8,128)(2,1)S(1)} collective-permute-done((bf16[528,128]{1,0:T(8,128)(2,1)}, bf16[528,128]{1,0:T(8,128)(2,1)S(1)}, u32[]{:S(2)}, u32[]{:S(2)}) %collective-permute-start.4) | collective-permute-done | bytes 135200 | tf_op jit(solution)/shard_map/ppermute | solution.py:212
  24.0 1.6 %collective-permute-start.7 = (bf16[1056,128]{1,0:T(8,128)(2,1)S(1)}, bf16[1056,128]{1,0:T(8,128)(2,1)S(1)}, u32[]{:S(2)}, u32[]{:S(2)}) collective-permute-start(bf16[1056,128]{1,0:T(8,128)(2,1)S(1)} %constant_dynamic-update-slice_fusion.2.refs_5_), channel_id=1, source_target_pairs={{0,2},{1,3},{2,0},{3,1},{4,6},{5,7},{6,4},{7,5},{8,10},{9,11},{10,... | collective-permute-start | bytes 811016 | tf_op jit(solution)/shard_map/ppermute | solution.py:212
  25.5 0.5 collective-permute-start.9
  26.1 4.4 %collective-permute-done.7.refs_7_ = bf16[1056,128]{1,0:T(8,128)(2,1)S(1)} collective-permute-done((bf16[1056,128]{1,0:T(8,128)(2,1)S(1)}, bf16[1056,128]{1,0:T(8,128)(2,1)S(1)}, u32[]{:S(2)}, u32[]{:S(2)}) %collective-permute-start.7) | collective-permute-done | bytes 270368 | tf_op jit(solution)/shard_map/ppermute | solution.py:212
  30.5 5.0 %shard_map.83 = (bf16[128,256]{1,0:T(8,128)(2,1)}, bf16[128,256]{1,0:T(8,128)(2,1)}, bf16[128,256]{1,0:T(8,128)(2,1)}, bf16[128,256]{1,0:T(8,128)(2,1)}) custom-call(bf16[128,1920]{1,0:T(8,128)(2,1)} %get-tuple-element.18.modded_ref, bf16[3,1920,1024]{2,1,0:T(8,128)(2,1)} %w_ref.5, f32[1,64]{1,0:T(1,128)} %bitcast.6), custom_call_target="tpu_custom_call" | custom-call | tf_op jit(solution)/shard_map/pallas_call | solution.py:228
  35.5 2.8 %collective-permute-start = (bf16[128,256]{1,0:T(8,128)(2,1)}, bf16[128,256]{1,0:T(8,128)(2,1)S(1)}, u32[]{:S(2)}, u32[]{:S(2)}) collective-permute-start(bf16[128,256]{1,0:T(8,128)(2,1)} %get-tuple-element.20), channel_id=1, source_target_pairs={{0,4},{1,5},{2,6},{3,7},{4,0},{5,1},{6,2},{7,3},{8,12},{9,13},{10,... | collective-permute-start | bytes 196616 | tf_op jit(solution)/shard_map/ppermute | solution.py:212
  38.3 2.9 %collective-permute-done.refs_1_ = bf16[128,256]{1,0:T(8,128)(2,1)S(1)} collective-permute-done((bf16[128,256]{1,0:T(8,128)(2,1)}, bf16[128,256]{1,0:T(8,128)(2,1)S(1)}, u32[]{:S(2)}, u32[]{:S(2)}) %collective-permute-start) | collective-permute-done | bytes 65568 | tf_op jit(solution)/shard_map/ppermute | solution.py:212
  41.2 2.9 %collective-permute-start.1 = (bf16[128,256]{1,0:T(8,128)(2,1)}, bf16[128,256]{1,0:T(8,128)(2,1)S(1)}, u32[]{:S(2)}, u32[]{:S(2)}) collective-permute-start(bf16[128,256]{1,0:T(8,128)(2,1)} %get-tuple-element.21), channel_id=1, source_target_pairs={{0,8},{1,9},{2,10},{3,11},{4,12},{5,13},{6,14},{7,15},{8,0},{9,1},... | collective-permute-start | bytes 196616 | tf_op jit(solution)/shard_map/ppermute | solution.py:212
  44.1 2.9 %collective-permute-done.1.refs_2_ = bf16[128,256]{1,0:T(8,128)(2,1)S(1)} collective-permute-done((bf16[128,256]{1,0:T(8,128)(2,1)}, bf16[128,256]{1,0:T(8,128)(2,1)S(1)}, u32[]{:S(2)}, u32[]{:S(2)}) %collective-permute-start.1) | collective-permute-done | bytes 65568 | tf_op jit(solution)/shard_map/ppermute | solution.py:212
  47.0 2.7 %collective-permute-start.2 = (bf16[128,256]{1,0:T(8,128)(2,1)}, bf16[128,256]{1,0:T(8,128)(2,1)S(1)}, u32[]{:S(2)}, u32[]{:S(2)}) collective-permute-start(bf16[128,256]{1,0:T(8,128)(2,1)} %get-tuple-element.22), channel_id=1, source_target_pairs={{0,12},{1,13},{2,14},{3,15},{4,8},{5,9},{6,10},{7,11},{8,4},{9,5},... | collective-permute-start | bytes 196616 | tf_op jit(solution)/shard_map/ppermute | solution.py:212
  49.7 3.6 %collective-permute-done.2.refs_3_ = bf16[128,256]{1,0:T(8,128)(2,1)S(1)} collective-permute-done((bf16[128,256]{1,0:T(8,128)(2,1)}, bf16[128,256]{1,0:T(8,128)(2,1)S(1)}, u32[]{:S(2)}, u32[]{:S(2)}) %collective-permute-start.2) | collective-permute-done | bytes 65568 | tf_op jit(solution)/shard_map/ppermute | solution.py:212
  53.4 0.5 copy-done.12
  53.9 0.1 copy-done.5
  54.0 0.1 copy-done.6
  54.2 0.1 copy-done.8
  54.3 12.5 %shard_map.84 = (bf16[128,256]{1,0:T(8,128)(2,1)}, bf16[128,256]{1,0:T(8,128)(2,1)}, bf16[128,256]{1,0:T(8,128)(2,1)}, bf16[128,256]{1,0:T(8,128)(2,1)}) custom-call(bf16[128,256]{1,0:T(8,128)(2,1)} %get-tuple-element.19.refs_0_, bf16[128,256]{1,0:T(8,128)(2,1)} %copy-done.10, bf16[128,256]{1,0:T(8,128)(2,1)} %copy-done.11, bf16[128,256]{1,0:T(8,128)(2,1)} %copy-done.12, ...), custom_call_target="tpu_custom_call" | custom-call | tf_op jit(solution)/shard_map/pallas_call | solution.py:242
  66.8 3.2 %collective-permute-start.13 = (bf16[128,256]{1,0:T(8,128)(2,1)}, bf16[128,256]{1,0:T(8,128)(2,1)S(1)}, u32[]{:S(2)}, u32[]{:S(2)}) collective-permute-start(bf16[128,256]{1,0:T(8,128)(2,1)} %get-tuple-element.29), channel_id=1, source_target_pairs={{0,8},{1,9},{2,10},{3,11},{4,12},{5,13},{6,14},{7,15},{8,0},{9,1},... | collective-permute-start | bytes 196616 | tf_op jit(solution)/shard_map/ppermute | solution.py:212
  70.0 1.2 %collective-permute-start.14 = (bf16[128,256]{1,0:T(8,128)(2,1)}, bf16[128,256]{1,0:T(8,128)(2,1)S(1)}, u32[]{:S(2)}, u32[]{:S(2)}) collective-permute-start(bf16[128,256]{1,0:T(8,128)(2,1)} %get-tuple-element.30), channel_id=1, source_target_pairs={{0,12},{1,13},{2,14},{3,15},{4,8},{5,9},{6,10},{7,11},{8,4},{9,5},... | collective-permute-start | bytes 196616 | tf_op jit(solution)/shard_map/ppermute | solution.py:212
  71.2 0.8 constant_dynamic-update-slice_fusion.7
  72.0 0.8 collective-permute-done.13
  72.8 3.5 %collective-permute-done.14 = bf16[128,256]{1,0:T(8,128)(2,1)S(1)} collective-permute-done((bf16[128,256]{1,0:T(8,128)(2,1)}, bf16[128,256]{1,0:T(8,128)(2,1)S(1)}, u32[]{:S(2)}, u32[]{:S(2)}) %collective-permute-start.14) | collective-permute-done | bytes 65568 | tf_op jit(solution)/shard_map/ppermute | solution.py:212
  76.3 1.6 %collective-permute-start.15 = (bf16[512,256]{1,0:T(8,128)(2,1)S(1)}, bf16[512,256]{1,0:T(8,128)(2,1)S(1)}, u32[]{:S(2)}, u32[]{:S(2)}) collective-permute-start(bf16[512,256]{1,0:T(8,128)(2,1)S(1)} %constant_dynamic-update-slice_fusion.4.pieces_ref), channel_id=1, source_target_pairs={{0,16},{16,0},{1,17},{17,1},{2,18},{18,2},{3,19},{19,3},{4,20},{20... | collective-permute-start | bytes 786440 | tf_op jit(solution)/shard_map/ppermute | solution.py:256
  77.9 3.5 %shard_map.85.own_ref = f32[128,1024]{1,0:T(8,128)} custom-call(bf16[512,256]{1,0:T(8,128)(2,1)} %copy-done.2, bf16[1024,1920]{1,0:T(8,128)(2,1)} %w_ref.7), custom_call_target="tpu_custom_call" | custom-call | tf_op jit(solution)/shard_map/pallas_call | solution.py:260
  81.3 1.4 %collective-permute-done.15.pieces_ref = bf16[512,256]{1,0:T(8,128)(2,1)S(1)} collective-permute-done((bf16[512,256]{1,0:T(8,128)(2,1)S(1)}, bf16[512,256]{1,0:T(8,128)(2,1)S(1)}, u32[]{:S(2)}, u32[]{:S(2)}) %collective-permute-start.15) | collective-permute-done | bytes 262176 | tf_op jit(solution)/shard_map/ppermute | solution.py:256
  82.7 0.7 copy-done.9
  83.5 3.7 %shard_map.86 = f32[960,128]{1,0:T(8,128)} custom-call(s32[1]{0:T(128)S(6)} %copy.15.block_ref, bf16[512,256]{1,0:T(8,128)(2,1)} %copy-done.9, f32[128,1024]{1,0:T(8,128)} %shard_map.85.own_ref, bf16[1024,1920]{1,0:T(8,128)(2,1)} %w_ref.7, f32[6,1920]{1,0:T(8,128)} %modulation_ref.3), custom_call_target="tpu_custom_call" | custom-call | tf_op jit(solution)/shard_map/pallas_call | solution.py:265
  (39 shorter events, 0.3 us)
Async XLA Ops:
  7.4 8.6 %collective-permute-start.3 = (bf16[528,128]{1,0:T(8,128)(2,1)}, bf16[528,128]{1,0:T(8,128)(2,1)S(1)}, u32[]{:S(2)}, u32[]{:S(2)}) collective-permute-start(bf16[528,128]{1,0:T(8,128)(2,1)} %get-tuple-element.24), channel_id=1, source_target_pairs={{0,4},{1,5},{2,6},{3,7},{4,0},{5,1},{6,2},{7,3},{8,12},{9,13},{10,... | collective-permute-start | bytes 405512 | tf_op jit(solution)/shard_map/ppermute | solution.py:212
  10.5 13.4 %collective-permute-start.4 = (bf16[528,128]{1,0:T(8,128)(2,1)}, bf16[528,128]{1,0:T(8,128)(2,1)S(1)}, u32[]{:S(2)}, u32[]{:S(2)}) collective-permute-start(bf16[528,128]{1,0:T(8,128)(2,1)} %get-tuple-element.25), channel_id=1, source_target_pairs={{0,8},{1,9},{2,10},{3,11},{4,12},{5,13},{6,14},{7,15},{8,0},{9,1},... | collective-permute-start | bytes 405512 | tf_op jit(solution)/shard_map/ppermute | solution.py:212
  13.1 10.8 %collective-permute-start.5 = (bf16[528,128]{1,0:T(8,128)(2,1)}, bf16[528,128]{1,0:T(8,128)(2,1)S(1)}, u32[]{:S(2)}, u32[]{:S(2)}) collective-permute-start(bf16[528,128]{1,0:T(8,128)(2,1)} %get-tuple-element.26), channel_id=1, source_target_pairs={{0,12},{1,13},{2,14},{3,15},{4,8},{5,9},{6,10},{7,11},{8,4},{9,5},... | collective-permute-start | bytes 405512 | tf_op jit(solution)/shard_map/ppermute | solution.py:212
  16.1 37.3 %copy-start = (bf16[1056,128]{1,0:T(8,128)(2,1)}, bf16[1056,128]{1,0:T(8,128)(2,1)S(1)}, u32[]{:S(2)}) copy-start(bf16[1056,128]{1,0:T(8,128)(2,1)S(1)} %constant_dynamic-update-slice_fusion.refs_4_) | copy-start | bytes 811012
  16.1 10.0 %collective-permute-start.6 = (bf16[1056,128]{1,0:T(8,128)(2,1)S(1)}, bf16[1056,128]{1,0:T(8,128)(2,1)S(1)}, u32[]{:S(2)}, u32[]{:S(2)}) collective-permute-start(bf16[1056,128]{1,0:T(8,128)(2,1)S(1)} %constant_dynamic-update-slice_fusion.refs_4_), channel_id=1, source_target_pairs={{0,2},{1,3},{2,0},{3,1},{4,6},{5,7},{6,4},{7,5},{8,10},{9,11},{10,... | collective-permute-start | bytes 811016 | tf_op jit(solution)/shard_map/ppermute | solution.py:212
  24.0 29.4 %copy-start.1 = (bf16[1056,128]{1,0:T(8,128)(2,1)}, bf16[1056,128]{1,0:T(8,128)(2,1)S(1)}, u32[]{:S(2)}) copy-start(bf16[1056,128]{1,0:T(8,128)(2,1)S(1)} %constant_dynamic-update-slice_fusion.2.refs_5_) | copy-start | bytes 811012
  24.0 6.5 %collective-permute-start.7 = (bf16[1056,128]{1,0:T(8,128)(2,1)S(1)}, bf16[1056,128]{1,0:T(8,128)(2,1)S(1)}, u32[]{:S(2)}, u32[]{:S(2)}) collective-permute-start(bf16[1056,128]{1,0:T(8,128)(2,1)S(1)} %constant_dynamic-update-slice_fusion.2.refs_5_), channel_id=1, source_target_pairs={{0,2},{1,3},{2,0},{3,1},{4,6},{5,7},{6,4},{7,5},{8,10},{9,11},{10,... | collective-permute-start | bytes 811016 | tf_op jit(solution)/shard_map/ppermute | solution.py:212
  25.5 27.7 %collective-permute-start.8 = (bf16[1056,128]{1,0:T(8,128)(2,1)S(1)}, bf16[1056,128]{1,0:T(8,128)(2,1)S(1)}, u32[]{:S(2)}, u32[]{:S(2)}) collective-permute-start(bf16[1056,128]{1,0:T(8,128)(2,1)S(1)} %constant_dynamic-update-slice_fusion.refs_4_), channel_id=1, source_target_pairs={{0,1},{1,0},{2,3},{3,2},{4,5},{5,4},{6,7},{7,6},{8,9},{9,8},{10,11... | collective-permute-start | bytes 811016 | tf_op jit(solution)/shard_map/ppermute | solution.py:212
  25.5 27.7 %collective-permute-start.9 = (bf16[1056,128]{1,0:T(8,128)(2,1)S(1)}, bf16[1056,128]{1,0:T(8,128)(2,1)S(1)}, u32[]{:S(2)}, u32[]{:S(2)}) collective-permute-start(bf16[1056,128]{1,0:T(8,128)(2,1)S(1)} %constant_dynamic-update-slice_fusion.2.refs_5_), channel_id=1, source_target_pairs={{0,1},{1,0},{2,3},{3,2},{4,5},{5,4},{6,7},{7,6},{8,9},{9,8},{10,11... | collective-permute-start | bytes 811016 | tf_op jit(solution)/shard_map/ppermute | solution.py:212
  26.1 27.3 %copy-start.3 = (bf16[1056,128]{1,0:T(8,128)(2,1)}, bf16[1056,128]{1,0:T(8,128)(2,1)S(1)}, u32[]{:S(2)}) copy-start(bf16[1056,128]{1,0:T(8,128)(2,1)S(1)} %collective-permute-done.6.refs_6_) | copy-start | bytes 811012
  26.1 27.2 %collective-permute-start.10 = (bf16[1056,128]{1,0:T(8,128)(2,1)S(1)}, bf16[1056,128]{1,0:T(8,128)(2,1)S(1)}, u32[]{:S(2)}, u32[]{:S(2)}) collective-permute-start(bf16[1056,128]{1,0:T(8,128)(2,1)S(1)} %collective-permute-done.6.refs_6_), channel_id=1, source_target_pairs={{0,1},{1,0},{2,3},{3,2},{4,5},{5,4},{6,7},{7,6},{8,9},{9,8},{10,11... | collective-permute-start | bytes 811016 | tf_op jit(solution)/shard_map/ppermute | solution.py:212
  30.5 22.9 %copy-start.4 = (bf16[1056,128]{1,0:T(8,128)(2,1)}, bf16[1056,128]{1,0:T(8,128)(2,1)S(1)}, u32[]{:S(2)}) copy-start(bf16[1056,128]{1,0:T(8,128)(2,1)S(1)} %collective-permute-done.7.refs_7_) | copy-start | bytes 811012
  30.5 22.8 %collective-permute-start.11 = (bf16[1056,128]{1,0:T(8,128)(2,1)S(1)}, bf16[1056,128]{1,0:T(8,128)(2,1)S(1)}, u32[]{:S(2)}, u32[]{:S(2)}) collective-permute-start(bf16[1056,128]{1,0:T(8,128)(2,1)S(1)} %collective-permute-done.7.refs_7_), channel_id=1, source_target_pairs={{0,1},{1,0},{2,3},{3,2},{4,5},{5,4},{6,7},{7,6},{8,9},{9,8},{10,11... | collective-permute-start | bytes 811016 | tf_op jit(solution)/shard_map/ppermute | solution.py:212
  35.5 5.7 %collective-permute-start = (bf16[128,256]{1,0:T(8,128)(2,1)}, bf16[128,256]{1,0:T(8,128)(2,1)S(1)}, u32[]{:S(2)}, u32[]{:S(2)}) collective-permute-start(bf16[128,256]{1,0:T(8,128)(2,1)} %get-tuple-element.20), channel_id=1, source_target_pairs={{0,4},{1,5},{2,6},{3,7},{4,0},{5,1},{6,2},{7,3},{8,12},{9,13},{10,... | collective-permute-start | bytes 196616 | tf_op jit(solution)/shard_map/ppermute | solution.py:212
  41.2 12.2 %copy-start.10 = (bf16[128,256]{1,0:T(8,128)(2,1)}, bf16[128,256]{1,0:T(8,128)(2,1)S(1)}, u32[]{:S(2)}) copy-start(bf16[128,256]{1,0:T(8,128)(2,1)S(1)} %collective-permute-done.refs_1_) | copy-start | bytes 196612
  41.2 5.8 %collective-permute-start.1 = (bf16[128,256]{1,0:T(8,128)(2,1)}, bf16[128,256]{1,0:T(8,128)(2,1)S(1)}, u32[]{:S(2)}, u32[]{:S(2)}) collective-permute-start(bf16[128,256]{1,0:T(8,128)(2,1)} %get-tuple-element.21), channel_id=1, source_target_pairs={{0,8},{1,9},{2,10},{3,11},{4,12},{5,13},{6,14},{7,15},{8,0},{9,1},... | collective-permute-start | bytes 196616 | tf_op jit(solution)/shard_map/ppermute | solution.py:212
  47.0 6.4 %copy-start.11 = (bf16[128,256]{1,0:T(8,128)(2,1)}, bf16[128,256]{1,0:T(8,128)(2,1)S(1)}, u32[]{:S(2)}) copy-start(bf16[128,256]{1,0:T(8,128)(2,1)S(1)} %collective-permute-done.1.refs_2_) | copy-start | bytes 196612
  47.0 6.3 %collective-permute-start.2 = (bf16[128,256]{1,0:T(8,128)(2,1)}, bf16[128,256]{1,0:T(8,128)(2,1)S(1)}, u32[]{:S(2)}, u32[]{:S(2)}) collective-permute-start(bf16[128,256]{1,0:T(8,128)(2,1)} %get-tuple-element.22), channel_id=1, source_target_pairs={{0,12},{1,13},{2,14},{3,15},{4,8},{5,9},{6,10},{7,11},{8,4},{9,5},... | collective-permute-start | bytes 196616 | tf_op jit(solution)/shard_map/ppermute | solution.py:212
  53.3 0.6 copy-start.12
  53.3 0.7 copy-start.5
  53.3 0.8 copy-start.6
  53.3 0.9 copy-start.7
  53.3 0.9 %copy-start.8 = (bf16[1056,128]{1,0:T(8,128)(2,1)}, bf16[1056,128]{1,0:T(8,128)(2,1)S(1)}, u32[]{:S(2)}) copy-start(bf16[1056,128]{1,0:T(8,128)(2,1)S(1)} %collective-permute-done.11.refs_11_) | copy-start | bytes 811012
  66.8 5.2 %collective-permute-start.12 = (bf16[128,256]{1,0:T(8,128)(2,1)}, bf16[128,256]{1,0:T(8,128)(2,1)S(1)}, u32[]{:S(2)}, u32[]{:S(2)}) collective-permute-start(bf16[128,256]{1,0:T(8,128)(2,1)} %get-tuple-element.28), channel_id=1, source_target_pairs={{0,4},{1,5},{2,6},{3,7},{4,0},{5,1},{6,2},{7,3},{8,12},{9,13},{10,... | collective-permute-start | bytes 196616 | tf_op jit(solution)/shard_map/ppermute | solution.py:212
  66.8 6.0 %collective-permute-start.13 = (bf16[128,256]{1,0:T(8,128)(2,1)}, bf16[128,256]{1,0:T(8,128)(2,1)S(1)}, u32[]{:S(2)}, u32[]{:S(2)}) collective-permute-start(bf16[128,256]{1,0:T(8,128)(2,1)} %get-tuple-element.29), channel_id=1, source_target_pairs={{0,8},{1,9},{2,10},{3,11},{4,12},{5,13},{6,14},{7,15},{8,0},{9,1},... | collective-permute-start | bytes 196616 | tf_op jit(solution)/shard_map/ppermute | solution.py:212
  70.0 6.3 %collective-permute-start.14 = (bf16[128,256]{1,0:T(8,128)(2,1)}, bf16[128,256]{1,0:T(8,128)(2,1)S(1)}, u32[]{:S(2)}, u32[]{:S(2)}) collective-permute-start(bf16[128,256]{1,0:T(8,128)(2,1)} %get-tuple-element.30), channel_id=1, source_target_pairs={{0,12},{1,13},{2,14},{3,15},{4,8},{5,9},{6,10},{7,11},{8,4},{9,5},... | collective-permute-start | bytes 196616 | tf_op jit(solution)/shard_map/ppermute | solution.py:212
  76.3 1.6 %copy-start.2 = (bf16[512,256]{1,0:T(8,128)(2,1)}, bf16[512,256]{1,0:T(8,128)(2,1)S(1)}, u32[]{:S(2)}) copy-start(bf16[512,256]{1,0:T(8,128)(2,1)S(1)} %constant_dynamic-update-slice_fusion.4.pieces_ref) | copy-start | bytes 786436
  76.3 6.4 %collective-permute-start.15 = (bf16[512,256]{1,0:T(8,128)(2,1)S(1)}, bf16[512,256]{1,0:T(8,128)(2,1)S(1)}, u32[]{:S(2)}, u32[]{:S(2)}) collective-permute-start(bf16[512,256]{1,0:T(8,128)(2,1)S(1)} %constant_dynamic-update-slice_fusion.4.pieces_ref), channel_id=1, source_target_pairs={{0,16},{16,0},{1,17},{17,1},{2,18},{18,2},{3,19},{19,3},{4,20},{20... | collective-permute-start | bytes 786440 | tf_op jit(solution)/shard_map/ppermute | solution.py:256
  82.7 0.7 copy-start.9

commit v2 on v1

--- a/solution.py
+++ b/solution.py
@@ -6,6 +6,7 @@
 from jax.experimental import pallas as pl
 from jax.experimental.pallas import tpu as pltpu
 from jax.sharding import PartitionSpec as P
+
 
 TXT = 226
 GUIDANCE = 6.0
@@ -53,12 +54,18 @@
 
 
 def key_value_kernel(block_ref, count_ref, hidden_ref, modulation_ref, w_ref, gain_ref, *refs, head, groups):
-    slots, (modded_ref, w_all, sems) = refs[:WAYS], refs[WAYS:]
+    slots, (modded_ref, states, table, w_all, sems) = refs[:WAYS], refs[WAYS:]
+    first = [
+        pltpu.make_async_copy(hidden_ref, states, sems.at[2]),
+        pltpu.make_async_copy(modulation_ref, table, sems.at[3]),
+    ]
     copies = [pltpu.make_async_copy(w_ref.at[1 + i], w_all.at[i], sems.at[i]) for i in range(2)]
-    for copy in copies:
+    for copy in first + copies:
         copy.start()
+    for copy in first:
+        copy.wait()
     block = block_ref[0]
-    modded_ref[...] = modulate(block, hidden_ref[...].astype(jnp.float32), modulation_ref)
+    modded_ref[...] = modulate(block, states[...].astype(jnp.float32), table)
     rows = modded_ref.shape[0]
     width = w_all.shape[2] // WAYS
     gain = wide(gain_ref[...])
@@ -107,13 +114,11 @@
     rows, width = queries[0].shape
     heads = width // head
     tiles = width // LANES
-    deep = head + EXTRA
     size = tiles * rows + EXTRA + width
-    each = pieces[0].shape[0] // size
     biases = []
     for g in range(held):
-        for p in range(each):
-            to, at = (g * each + p) * rows, p * size
+        for p in range(pieces[g].shape[0] // size):
+            to, at = len(biases) * rows, p * size
             for tile in range(tiles):
                 k_all[to : to + rows, tile * LANES : (tile + 1) * LANES] = pieces[g][at + tile * rows : at + (tile + 1) * rows, :]
             at += tiles * rows
@@ -167,22 +172,36 @@
     return total
 
 
-def half_of(total):
-    half = total // 2
+def half_of(half):
     spare = half % LANES
     span = half + spare
-    start = pl.multiple_of(lax.axis_index("cfg") * (half - spare), LANES)
-    return half, spare, span, start
+    return spare, span, pl.multiple_of(lax.axis_index("cfg") * (half - spare), LANES)
+
+
+def fetch_kernel(w_ref, out_ref, sem):
+    _, span, start = half_of(w_ref.shape[1] // 2)
+    copy = pltpu.make_async_copy(w_ref.at[:, pl.ds(start, span)], out_ref, sem)
+    copy.start()
+    copy.wait()
+
+
+def project(pieces_ref, w_ref, way):
+    width = pieces_ref.shape[1]
+    rows = pieces_ref.shape[0] // WAYS
+    total = jnp.zeros((rows, w_ref.shape[1]), jnp.float32)
+    for slot in range(WAYS):
+        w = w_ref[pl.ds(pl.multiple_of((way ^ slot) * width, width), width), :]
+        total += jnp.dot(pieces_ref[slot * rows : (slot + 1) * rows, :], w, preferred_element_type=jnp.float32)
+    return total
 
 
 def own_kernel(pieces_ref, w_ref, out_ref, *, groups):
-    _, _, span, start = half_of(w_ref.shape[1])
-    out_ref[...] = project(pieces_ref, w_ref, lax.axis_index("seq") // groups, start, span)
-
-
-def final_kernel(block_ref, pieces_ref, own_ref, w_ref, modulation_ref, out_ref, *, groups):
-    half, spare, span, start = half_of(w_ref.shape[1])
-    total = project(pieces_ref, w_ref, lax.axis_index("seq") // groups, start, span)
+    out_ref[...] = project(pieces_ref, w_ref, lax.axis_index("seq") // groups)
+
+
+def final_kernel(block_ref, pieces_ref, own_ref, w_ref, modulation_ref, out_ref, *, groups, half):
+    spare, span, start = half_of(half)
+    total = project(pieces_ref, w_ref, lax.axis_index("seq") // groups)
     is_text = text_rows(block_ref[0], total.shape[0])
     table = modulation_ref[:, pl.ds(start, span)]
     gate = jnp.where(is_text, table[5:6, :], table[2:3, :])
@@ -195,7 +214,7 @@
     out_ref[...] = jnp.where(is_first, guided[:half, :], guided[spare:, :])
 
 
-def shards(hidden, modulation, w_qkv, q_gain, k_gain, w_out, text_count, block_order):
+def block(hidden, modulation, w_qkv, q_gain, k_gain, w_out, text_count, block_order):
     states = hidden[0]
     rows, features = states.shape
     head = q_gain.shape[0]
@@ -207,9 +226,10 @@
     smem = pl.BlockSpec(memory_space=pltpu.SMEM)
     vmem = pl.BlockSpec(memory_space=pltpu.VMEM)
     hbm = pl.BlockSpec(memory_space=pl.ANY)
-
-    def exchange(block, bits):
-        return lax.ppermute(block, "seq", [(i, i ^ bits) for i in range(count)])
+    held_in = functools.partial(pltpu.with_memory_space_constraint, memory_space=pltpu.VMEM)
+
+    def exchange(x, bits):
+        return lax.ppermute(x, "seq", [(i, i ^ bits) for i in range(count)])
 
     def spread(slots):
         far = {s: exchange(slots[s], s * groups) for s in reversed(range(1, WAYS))}
@@ -220,9 +240,14 @@
     piece = jax.ShapeDtypeStruct((rows, width), bf16)
     *kv_slots, modded = pl.pallas_call(
         functools.partial(key_value_kernel, head=head, groups=groups),
-        in_specs=[smem, smem, vmem, vmem, hbm, vmem],
-        out_shape=[kv_piece] * WAYS + [jax.ShapeDtypeStruct((rows, features), bf16)],
-        scratch_shapes=[pltpu.VMEM((2, features, inner), bf16), pltpu.SemaphoreType.DMA((2,))],
+        in_specs=[smem, smem, hbm, hbm, hbm, vmem],
+        out_shape=[kv_piece] * WAYS + [pltpu.VMEM((rows, features), bf16)],
+        scratch_shapes=[
+            pltpu.VMEM((rows, features), bf16),
+            pltpu.VMEM(modulation.shape, jnp.float32),
+            pltpu.VMEM((2, features, inner), bf16),
+            pltpu.SemaphoreType.DMA((4,)),
+        ],
     )(block_order, text_count, states, modulation, w_qkv, k_gain[None, :])
     kv = spread(kv_slots)
     q_slots = pl.pallas_call(
@@ -230,9 +255,17 @@
         in_specs=[vmem, hbm, vmem],
         out_shape=[piece] * WAYS,
         scratch_shapes=[pltpu.VMEM((features, inner), bf16), pltpu.SemaphoreType.DMA],
-    )(modded, w_qkv, q_gain[None, :])
+    )(held_in(modded), w_qkv, q_gain[None, :])
     queries = spread(q_slots)
-    held = [jnp.concatenate(kv[i : i + 2], axis=0) for i in range(0, WAYS, 2)]
+    half = w_out.shape[1] // 2
+    span = half + half % LANES
+    w_half = pl.pallas_call(
+        fetch_kernel,
+        in_specs=[hbm],
+        out_shape=pltpu.VMEM((inner, span), bf16),
+        scratch_shapes=[pltpu.SemaphoreType.DMA],
+    )(w_out)
+    held = [kv[0], kv[1], jnp.concatenate(kv[2:], axis=0)]
     bit = groups // 2
     while bit:
         held = held + [exchange(x, bit) for x in held]
@@ -254,23 +287,20 @@
     attended = jnp.concatenate(spread(o_slots), axis=0)
     cfg_count = lax.axis_size("cfg")
     partner = lax.ppermute(attended, "cfg", [(i, i ^ 1) for i in range(cfg_count)])
-
-    half = w_out.shape[1] // 2
-    span = half + half % LANES
     own = pl.pallas_call(
         functools.partial(own_kernel, groups=groups),
         in_specs=[vmem] * 2,
-        out_shape=jax.ShapeDtypeStruct((rows, span), jnp.float32),
-    )(attended, w_out)
+        out_shape=pltpu.VMEM((rows, span), jnp.float32),
+    )(attended, held_in(w_half))
     guided = pl.pallas_call(
-        functools.partial(final_kernel, groups=groups),
+        functools.partial(final_kernel, groups=groups, half=half),
         in_specs=[smem] + [vmem] * 4,
         out_shape=jax.ShapeDtypeStruct((half, rows), jnp.float32),
-    )(block_order, partner, own, w_out, modulation)
+    )(block_order, partner, held_in(own), held_in(w_half), modulation)
     return guided.T
 
 
 def solution(mesh):
     in_specs = (P("cfg", "seq", None), P(), P(), P(), P(), P(), P("cfg"), P("seq"))
     out_specs = P("seq", "cfg")
-    return jax.shard_map(shards, mesh=mesh, in_specs=in_specs, out_specs=out_specs, check_vma=False)
+    return jax.shard_map(block, mesh=mesh, in_specs=in_specs, out_specs=out_specs, check_vma=False)

time: 87.5 us -> 80.5 us (0.920)
  Pallas kernels: 30.8 us -> 28.2 us
  waiting for transfers between devices: 27.4 us -> 25 us
  local copies, waits for them, and re-layouts: 3.44 us -> 2.39 us
  starting transfers between devices: 24 us -> 23 us
    pallas_call x5 -> x6, Pallas kernels: 30.8 us -> 28.2 us  [the longest x1 12.6 us: block(): pl.pallas_call(functools.partial(attention_kernel, held=len(held), head=h...]
    ppermute x16 -> x19, waiting for transfers between devices: 27.4 us -> 25 us  [the longest x18 22.9 us: exchange(): return lax.ppermute(x, 'seq', [(i, i ^ bits) for i in range(count)])]
    unnamed x31 -> x38, local copies, waits for them, and re-layouts: 3.4 us -> 2.36 us
    ppermute x16 -> x19, starting transfers between devices: 24 us -> 23 us  [the longest x18 21.4 us: exchange(): return lax.ppermute(x, 'seq', [(i, i ^ bits) for i in range(count)])]
  transfers between devices with their start and end apart: 16 -> 19, of which waited for: 9 -> 9; matrix products, arithmetic and copies ran while one was open for 2% -> 1% of each run, Pallas kernels for 10% -> 9%
where the time goes in v2:
time: 80.5 us; the launch traced here: 80.1 us
  Pallas kernels  28.2 us (35%)
  waiting for transfers between devices  25 us (31%)
  starting transfers between devices  23 us (29%)
  local copies, waits for them, and re-layouts  2.39 us (3%)
  between operations  1.55 us (2%)
    ppermute x18, waiting for transfers between devices, exchange(): return lax.ppermute(x, 'seq', [(i, i ^ bits) for i in range(count)])  22.9 us
    ppermute x18, starting transfers between devices, exchange(): return lax.ppermute(x, 'seq', [(i, i ^ bits) for i in range(count)])  21.4 us
    pallas_call x1, Pallas kernels, block(): pl.pallas_call(functools.partial(attention_kernel, held=len(held), head=h...  12.6 us
    pallas_call x1, Pallas kernels, block(): pl.pallas_call(functools.partial(key_value_kernel, head=head, groups=grou...  5.73 us
    pallas_call x1, Pallas kernels, block(): pl.pallas_call(functools.partial(query_kernel, head=head, groups=groups),...  4.57 us
    unnamed x38, local copies, waits for them, and re-layouts  2.36 us
    pallas_call x1, Pallas kernels, block(): pl.pallas_call(functools.partial(final_kernel, groups=groups, half=half),...  2.33 us
    ppermute x1, waiting for transfers between devices, block(): lax.ppermute(attended, 'cfg', [(i, i ^ 1) for i in range(cfg_count)])  2.14 us
  transfers between devices with their start and end apart: 19, of which 9 were waited for; matrix products, arithmetic and copies ran while one was open for 1% of the time, Pallas kernels for 9%

profile of v2, /device:TPU:0, one launch (start us, length us, event | category | flops | bytes accessed | tf_op | source)
XLA Modules:
  0.0 80.1 jit_solution(11809478463482781477)
XLA Ops:
  1.3 5.7 %shard_map.82 = (bf16[528,128]{1,0:T(8,128)(2,1)}, bf16[528,128]{1,0:T(8,128)(2,1)}, bf16[528,128]{1,0:T(8,128)(2,1)}, bf16[528,128]{1,0:T(8,128)(2,1)}, bf16[128,1920]{1,0:T(8,128)(2,1)S(1)}) custom-call(s32[1]{0:T(128)S(6)} %copy.14.block_ref, s32[1]{0:T(128)S(6)} %copy.13.count_ref, bf16[128,1920]{1,0:T(8,128)(2,1)} %bitcast.4, f32[6,1920]{1,0:T(8,128)} %modulation_ref.3, ...), custom_call_target="tpu_custom_call" | custom-call | tf_op jit(solution)/shard_map/pallas_call | solution.py:241
  7.0 4.1 %collective-permute-start.4 = (bf16[528,128]{1,0:T(8,128)(2,1)}, bf16[528,128]{1,0:T(8,128)(2,1)S(1)}, u32[]{:S(2)}, u32[]{:S(2)}) collective-permute-start(bf16[528,128]{1,0:T(8,128)(2,1)} %get-tuple-element.25), channel_id=1, source_target_pairs={{0,8},{1,9},{2,10},{3,11},{4,12},{5,13},{6,14},{7,15},{8,0},{9,1},... | collective-permute-start | bytes 405512 | tf_op jit(solution)/shard_map/ppermute | solution.py:232
  11.2 1.3 %collective-permute-start.5 = (bf16[528,128]{1,0:T(8,128)(2,1)}, bf16[528,128]{1,0:T(8,128)(2,1)S(1)}, u32[]{:S(2)}, u32[]{:S(2)}) collective-permute-start(bf16[528,128]{1,0:T(8,128)(2,1)} %get-tuple-element.26), channel_id=1, source_target_pairs={{0,12},{1,13},{2,14},{3,15},{4,8},{5,9},{6,10},{7,11},{8,4},{9,5},... | collective-permute-start | bytes 405512 | tf_op jit(solution)/shard_map/ppermute | solution.py:232
  12.5 9.1 %collective-permute-done.4 = bf16[528,128]{1,0:T(8,128)(2,1)S(1)} collective-permute-done((bf16[528,128]{1,0:T(8,128)(2,1)}, bf16[528,128]{1,0:T(8,128)(2,1)S(1)}, u32[]{:S(2)}, u32[]{:S(2)}) %collective-permute-start.4) | collective-permute-done | bytes 135200 | tf_op jit(solution)/shard_map/ppermute | solution.py:232
  21.7 1.9 %collective-permute-start.8 = (bf16[1056,128]{1,0:T(8,128)(2,1)S(1)}, bf16[1056,128]{1,0:T(8,128)(2,1)S(1)}, u32[]{:S(2)}, u32[]{:S(2)}) collective-permute-start(bf16[1056,128]{1,0:T(8,128)(2,1)S(1)} %constant_dynamic-update-slice_fusion.refs_6_), channel_id=1, source_target_pairs={{0,2},{1,3},{2,0},{3,1},{4,6},{5,7},{6,4},{7,5},{8,10},{9,11},{10,... | collective-permute-start | bytes 811016 | tf_op jit(solution)/shard_map/ppermute | solution.py:232
  23.6 2.5 %collective-permute-start.3 = (bf16[528,128]{1,0:T(8,128)(2,1)}, bf16[528,128]{1,0:T(8,128)(2,1)S(1)}, u32[]{:S(2)}, u32[]{:S(2)}) collective-permute-start(bf16[528,128]{1,0:T(8,128)(2,1)} %get-tuple-element.24), channel_id=1, source_target_pairs={{0,4},{1,5},{2,6},{3,7},{4,0},{5,1},{6,2},{7,3},{8,12},{9,13},{10,... | collective-permute-start | bytes 405512 | tf_op jit(solution)/shard_map/ppermute | solution.py:232
  26.1 4.6 %shard_map.83 = (bf16[128,256]{1,0:T(8,128)(2,1)}, bf16[128,256]{1,0:T(8,128)(2,1)}, bf16[128,256]{1,0:T(8,128)(2,1)}, bf16[128,256]{1,0:T(8,128)(2,1)}) custom-call(bf16[128,1920]{1,0:T(8,128)(2,1)S(1)} %get-tuple-element.18.modded_ref, bf16[3,1920,1024]{2,1,0:T(8,128)(2,1)} %w_ref.4, f32[1,64]{1,0:T(1,128)} %bitcast.6), custom_call_target="tpu_custom_call" | custom-call | tf_op jit(solution)/shard_map/pallas_call | solution.py:253
  30.8 3.8 %collective-permute-start.1 = (bf16[128,256]{1,0:T(8,128)(2,1)}, bf16[128,256]{1,0:T(8,128)(2,1)S(1)}, u32[]{:S(2)}, u32[]{:S(2)}) collective-permute-start(bf16[128,256]{1,0:T(8,128)(2,1)} %get-tuple-element.21), channel_id=1, source_target_pairs={{0,8},{1,9},{2,10},{3,11},{4,12},{5,13},{6,14},{7,15},{8,0},{9,1},... | collective-permute-start | bytes 196616 | tf_op jit(solution)/shard_map/ppermute | solution.py:232
  34.6 0.6 collective-permute-start.2
  35.1 0.6 collective-permute-done.refs_1_
  35.8 3.3 %collective-permute-done.1.refs_2_ = bf16[128,256]{1,0:T(8,128)(2,1)S(1)} collective-permute-done((bf16[128,256]{1,0:T(8,128)(2,1)}, bf16[128,256]{1,0:T(8,128)(2,1)S(1)}, u32[]{:S(2)}, u32[]{:S(2)}) %collective-permute-start.1) | collective-permute-done | bytes 65568 | tf_op jit(solution)/shard_map/ppermute | solution.py:232
  39.0 0.5 collective-permute-start.6
  39.5 1.5 %collective-permute-start.7 = (bf16[528,128]{1,0:T(8,128)(2,1)S(1)}, bf16[528,128]{1,0:T(8,128)(2,1)S(1)}, u32[]{:S(2)}, u32[]{:S(2)}) collective-permute-start(bf16[528,128]{1,0:T(8,128)(2,1)S(1)} %collective-permute-done.3.refs_5_), channel_id=1, source_target_pairs={{0,2},{1,3},{2,0},{3,1},{4,6},{5,7},{6,4},{7,5},{8,10},{9,11},{10,... | collective-permute-start | bytes 405512 | tf_op jit(solution)/shard_map/ppermute | solution.py:232
  41.2 0.5 collective-permute-start.14
  41.7 2.3 %collective-permute-done.6.refs_7_ = bf16[528,128]{1,0:T(8,128)(2,1)S(1)} collective-permute-done((bf16[528,128]{1,0:T(8,128)(2,1)S(1)}, bf16[528,128]{1,0:T(8,128)(2,1)S(1)}, u32[]{:S(2)}, u32[]{:S(2)}) %collective-permute-start.6) | collective-permute-done | bytes 135200 | tf_op jit(solution)/shard_map/ppermute | solution.py:232
  44.0 1.4 %collective-permute-done.7.refs_8_ = bf16[528,128]{1,0:T(8,128)(2,1)S(1)} collective-permute-done((bf16[528,128]{1,0:T(8,128)(2,1)S(1)}, bf16[528,128]{1,0:T(8,128)(2,1)S(1)}, u32[]{:S(2)}, u32[]{:S(2)}) %collective-permute-start.7) | collective-permute-done | bytes 135200 | tf_op jit(solution)/shard_map/ppermute | solution.py:232
  45.5 1.3 %collective-permute-done.13.refs_14_ = bf16[528,128]{1,0:T(8,128)(2,1)S(1)} collective-permute-done((bf16[528,128]{1,0:T(8,128)(2,1)S(1)}, bf16[528,128]{1,0:T(8,128)(2,1)S(1)}, u32[]{:S(2)}, u32[]{:S(2)}) %collective-permute-start.13) | collective-permute-done | bytes 135200 | tf_op jit(solution)/shard_map/ppermute | solution.py:232
  47.0 0.5 copy-done.13
  47.6 0.1 copy-done.4
  47.7 12.6 %shard_map.84 = (bf16[128,256]{1,0:T(8,128)(2,1)}, bf16[128,256]{1,0:T(8,128)(2,1)}, bf16[128,256]{1,0:T(8,128)(2,1)}, bf16[128,256]{1,0:T(8,128)(2,1)}) custom-call(bf16[128,256]{1,0:T(8,128)(2,1)} %get-tuple-element.19.refs_0_, bf16[128,256]{1,0:T(8,128)(2,1)} %copy-done.14, bf16[128,256]{1,0:T(8,128)(2,1)} %copy-done.15, bf16[128,256]{1,0:T(8,128)(2,1)} %copy-done.16, ...), custom_call_target="tpu_custom_call" | custom-call | tf_op jit(solution)/shard_map/pallas_call | solution.py:275
  60.3 0.5 collective-permute-start.15
  60.8 3.2 %collective-permute-start.16 = (bf16[128,256]{1,0:T(8,128)(2,1)}, bf16[128,256]{1,0:T(8,128)(2,1)S(1)}, u32[]{:S(2)}, u32[]{:S(2)}) collective-permute-start(bf16[128,256]{1,0:T(8,128)(2,1)} %get-tuple-element.29), channel_id=1, source_target_pairs={{0,8},{1,9},{2,10},{3,11},{4,12},{5,13},{6,14},{7,15},{8,0},{9,1},... | collective-permute-start | bytes 196616 | tf_op jit(solution)/shard_map/ppermute | solution.py:232
  64.0 0.7 collective-permute-start.17
  64.7 0.8 %constant_dynamic-update-slice_fusion.5 = bf16[512,256]{1,0:T(8,128)(2,1)S(1)} fusion(bf16[128,256]{1,0:T(8,128)(2,1)} %get-tuple-element.27), kind=kLoop, calls=%fused_computation.5 | loop fusion | bytes 131072
  65.6 2.7 %collective-permute-done.16 = bf16[128,256]{1,0:T(8,128)(2,1)S(1)} collective-permute-done((bf16[128,256]{1,0:T(8,128)(2,1)}, bf16[128,256]{1,0:T(8,128)(2,1)S(1)}, u32[]{:S(2)}, u32[]{:S(2)}) %collective-permute-start.16) | collective-permute-done | bytes 65568 | tf_op jit(solution)/shard_map/ppermute | solution.py:232
  68.2 2.1 %collective-permute-done.17 = bf16[128,256]{1,0:T(8,128)(2,1)S(1)} collective-permute-done((bf16[128,256]{1,0:T(8,128)(2,1)}, bf16[128,256]{1,0:T(8,128)(2,1)S(1)}, u32[]{:S(2)}, u32[]{:S(2)}) %collective-permute-start.17) | collective-permute-done | bytes 65568 | tf_op jit(solution)/shard_map/ppermute | solution.py:232
  70.4 1.6 %collective-permute-start.18 = (bf16[512,256]{1,0:T(8,128)(2,1)S(1)}, bf16[512,256]{1,0:T(8,128)(2,1)S(1)}, u32[]{:S(2)}, u32[]{:S(2)}) collective-permute-start(bf16[512,256]{1,0:T(8,128)(2,1)S(1)} %constant_dynamic-update-slice_fusion.2.pieces_ref), channel_id=1, source_target_pairs={{0,16},{16,0},{1,17},{17,1},{2,18},{18,2},{3,19},{19,3},{4,20},{20... | collective-permute-start | bytes 786440 | tf_op jit(solution)/shard_map/ppermute | solution.py:289
  72.0 1.6 %shard_map.85.w_ref = bf16[1024,1024]{1,0:T(8,128)(2,1)S(1)} custom-call(bf16[1024,1920]{1,0:T(8,128)(2,1)} %w_ref.5), custom_call_target="tpu_custom_call" | custom-call | tf_op jit(solution)/shard_map/pallas_call | solution.py:262
  73.6 1.4 %shard_map.86.own_ref = f32[128,1024]{1,0:T(8,128)S(1)} custom-call(bf16[512,256]{1,0:T(8,128)(2,1)} %copy-done.1, bf16[1024,1024]{1,0:T(8,128)(2,1)S(1)} %shard_map.85.w_ref), custom_call_target="tpu_custom_call" | custom-call | tf_op jit(solution)/shard_map/pallas_call | solution.py:290
  75.0 2.1 %collective-permute-done.18.pieces_ref = bf16[512,256]{1,0:T(8,128)(2,1)S(1)} collective-permute-done((bf16[512,256]{1,0:T(8,128)(2,1)S(1)}, bf16[512,256]{1,0:T(8,128)(2,1)S(1)}, u32[]{:S(2)}, u32[]{:S(2)}) %collective-permute-start.18) | collective-permute-done | bytes 262176 | tf_op jit(solution)/shard_map/ppermute | solution.py:289
  77.1 0.7 copy-done.5
  77.8 2.3 %shard_map.87 = f32[960,128]{1,0:T(8,128)} custom-call(s32[1]{0:T(128)S(6)} %copy.14.block_ref, bf16[512,256]{1,0:T(8,128)(2,1)} %copy-done.5, f32[128,1024]{1,0:T(8,128)S(1)} %shard_map.86.own_ref, bf16[1024,1024]{1,0:T(8,128)(2,1)S(1)} %shard_map.85.w_ref, f32[6,1920]{1,0:T(8,128)} %modulation_ref.3), custom_call_target="tpu_custom_call" | custom-call | tf_op jit(solution)/shard_map/pallas_call | solution.py:295
  (52 shorter events, 0.5 us)
Async XLA Ops:
  7.0 14.6 %collective-permute-start.4 = (bf16[528,128]{1,0:T(8,128)(2,1)}, bf16[528,128]{1,0:T(8,128)(2,1)S(1)}, u32[]{:S(2)}, u32[]{:S(2)}) collective-permute-start(bf16[528,128]{1,0:T(8,128)(2,1)} %get-tuple-element.25), channel_id=1, source_target_pairs={{0,8},{1,9},{2,10},{3,11},{4,12},{5,13},{6,14},{7,15},{8,0},{9,1},... | collective-permute-start | bytes 405512 | tf_op jit(solution)/shard_map/ppermute | solution.py:232
  11.2 10.5 %collective-permute-start.5 = (bf16[528,128]{1,0:T(8,128)(2,1)}, bf16[528,128]{1,0:T(8,128)(2,1)S(1)}, u32[]{:S(2)}, u32[]{:S(2)}) collective-permute-start(bf16[528,128]{1,0:T(8,128)(2,1)} %get-tuple-element.26), channel_id=1, source_target_pairs={{0,12},{1,13},{2,14},{3,15},{4,8},{5,9},{6,10},{7,11},{8,4},{9,5},... | collective-permute-start | bytes 405512 | tf_op jit(solution)/shard_map/ppermute | solution.py:232
  21.7 19.4 %copy-start = (bf16[1056,128]{1,0:T(8,128)(2,1)}, bf16[1056,128]{1,0:T(8,128)(2,1)S(1)}, u32[]{:S(2)}) copy-start(bf16[1056,128]{1,0:T(8,128)(2,1)S(1)} %constant_dynamic-update-slice_fusion.refs_6_) | copy-start | bytes 811012
  21.7 19.5 %collective-permute-start.8 = (bf16[1056,128]{1,0:T(8,128)(2,1)S(1)}, bf16[1056,128]{1,0:T(8,128)(2,1)S(1)}, u32[]{:S(2)}, u32[]{:S(2)}) collective-permute-start(bf16[1056,128]{1,0:T(8,128)(2,1)S(1)} %constant_dynamic-update-slice_fusion.refs_6_), channel_id=1, source_target_pairs={{0,2},{1,3},{2,0},{3,1},{4,6},{5,7},{6,4},{7,5},{8,10},{9,11},{10,... | collective-permute-start | bytes 811016 | tf_op jit(solution)/shard_map/ppermute | solution.py:232
  23.6 16.0 %collective-permute-start.3 = (bf16[528,128]{1,0:T(8,128)(2,1)}, bf16[528,128]{1,0:T(8,128)(2,1)S(1)}, u32[]{:S(2)}, u32[]{:S(2)}) collective-permute-start(bf16[528,128]{1,0:T(8,128)(2,1)} %get-tuple-element.24), channel_id=1, source_target_pairs={{0,4},{1,5},{2,6},{3,7},{4,0},{5,1},{6,2},{7,3},{8,12},{9,13},{10,... | collective-permute-start | bytes 405512 | tf_op jit(solution)/shard_map/ppermute | solution.py:232
  26.1 9.6 %copy-start.6 = (bf16[528,128]{1,0:T(8,128)(2,1)S(1)}, bf16[528,128]{1,0:T(8,128)(2,1)}, u32[]{:S(2)}) copy-start(bf16[528,128]{1,0:T(8,128)(2,1)} %get-tuple-element.23.refs_4_) | copy-start | bytes 405508
  30.7 5.1 %collective-permute-start = (bf16[128,256]{1,0:T(8,128)(2,1)}, bf16[128,256]{1,0:T(8,128)(2,1)S(1)}, u32[]{:S(2)}, u32[]{:S(2)}) collective-permute-start(bf16[128,256]{1,0:T(8,128)(2,1)} %get-tuple-element.20), channel_id=1, source_target_pairs={{0,4},{1,5},{2,6},{3,7},{4,0},{5,1},{6,2},{7,3},{8,12},{9,13},{10,... | collective-permute-start | bytes 196616 | tf_op jit(solution)/shard_map/ppermute | solution.py:232
  30.8 8.3 %collective-permute-start.1 = (bf16[128,256]{1,0:T(8,128)(2,1)}, bf16[128,256]{1,0:T(8,128)(2,1)S(1)}, u32[]{:S(2)}, u32[]{:S(2)}) collective-permute-start(bf16[128,256]{1,0:T(8,128)(2,1)} %get-tuple-element.21), channel_id=1, source_target_pairs={{0,8},{1,9},{2,10},{3,11},{4,12},{5,13},{6,14},{7,15},{8,0},{9,1},... | collective-permute-start | bytes 196616 | tf_op jit(solution)/shard_map/ppermute | solution.py:232
  34.6 6.5 %collective-permute-start.2 = (bf16[128,256]{1,0:T(8,128)(2,1)}, bf16[128,256]{1,0:T(8,128)(2,1)S(1)}, u32[]{:S(2)}, u32[]{:S(2)}) collective-permute-start(bf16[128,256]{1,0:T(8,128)(2,1)} %get-tuple-element.22), channel_id=1, source_target_pairs={{0,12},{1,13},{2,14},{3,15},{4,8},{5,9},{6,10},{7,11},{8,4},{9,5},... | collective-permute-start | bytes 196616 | tf_op jit(solution)/shard_map/ppermute | solution.py:232
  35.7 11.1 %copy-start.14 = (bf16[128,256]{1,0:T(8,128)(2,1)}, bf16[128,256]{1,0:T(8,128)(2,1)S(1)}, u32[]{:S(2)}) copy-start(bf16[128,256]{1,0:T(8,128)(2,1)S(1)} %collective-permute-done.refs_1_) | copy-start | bytes 196612
  35.7 5.9 %collective-permute-start.9 = (bf16[528,128]{1,0:T(8,128)(2,1)S(1)}, bf16[528,128]{1,0:T(8,128)(2,1)S(1)}, u32[]{:S(2)}, u32[]{:S(2)}) collective-permute-start(bf16[528,128]{1,0:T(8,128)(2,1)S(1)} %copy-done.6), channel_id=1, source_target_pairs={{0,1},{1,0},{2,3},{3,2},{4,5},{5,4},{6,7},{7,6},{8,9},{9,8},{10,11... | collective-permute-start | bytes 405512 | tf_op jit(solution)/shard_map/ppermute | solution.py:232
  39.0 7.9 %copy-start.15 = (bf16[128,256]{1,0:T(8,128)(2,1)}, bf16[128,256]{1,0:T(8,128)(2,1)S(1)}, u32[]{:S(2)}) copy-start(bf16[128,256]{1,0:T(8,128)(2,1)S(1)} %collective-permute-done.1.refs_2_) | copy-start | bytes 196612
  39.0 5.0 %collective-permute-start.6 = (bf16[528,128]{1,0:T(8,128)(2,1)S(1)}, bf16[528,128]{1,0:T(8,128)(2,1)S(1)}, u32[]{:S(2)}, u32[]{:S(2)}) collective-permute-start(bf16[528,128]{1,0:T(8,128)(2,1)S(1)} %copy-done.6), channel_id=1, source_target_pairs={{0,2},{1,3},{2,0},{3,1},{4,6},{5,7},{6,4},{7,5},{8,10},{9,11},{10,... | collective-permute-start | bytes 405512 | tf_op jit(solution)/shard_map/ppermute | solution.py:232
  39.5 7.4 %copy-start.7 = (bf16[528,128]{1,0:T(8,128)(2,1)}, bf16[528,128]{1,0:T(8,128)(2,1)S(1)}, u32[]{:S(2)}) copy-start(bf16[528,128]{1,0:T(8,128)(2,1)S(1)} %collective-permute-done.3.refs_5_) | copy-start | bytes 405508
  39.5 5.9 %collective-permute-start.7 = (bf16[528,128]{1,0:T(8,128)(2,1)S(1)}, bf16[528,128]{1,0:T(8,128)(2,1)S(1)}, u32[]{:S(2)}, u32[]{:S(2)}) collective-permute-start(bf16[528,128]{1,0:T(8,128)(2,1)S(1)} %collective-permute-done.3.refs_5_), channel_id=1, source_target_pairs={{0,2},{1,3},{2,0},{3,1},{4,6},{5,7},{6,4},{7,5},{8,10},{9,11},{10,... | collective-permute-start | bytes 405512 | tf_op jit(solution)/shard_map/ppermute | solution.py:232
  41.1 5.8 %copy-start.16 = (bf16[128,256]{1,0:T(8,128)(2,1)}, bf16[128,256]{1,0:T(8,128)(2,1)S(1)}, u32[]{:S(2)}) copy-start(bf16[128,256]{1,0:T(8,128)(2,1)S(1)} %collective-permute-done.2.refs_3_) | copy-start | bytes 196612
  41.1 5.8 %collective-permute-start.11 = (bf16[1056,128]{1,0:T(8,128)(2,1)S(1)}, bf16[1056,128]{1,0:T(8,128)(2,1)S(1)}, u32[]{:S(2)}, u32[]{:S(2)}) collective-permute-start(bf16[1056,128]{1,0:T(8,128)(2,1)S(1)} %constant_dynamic-update-slice_fusion.refs_6_), channel_id=1, source_target_pairs={{0,1},{1,0},{2,3},{3,2},{4,5},{5,4},{6,7},{7,6},{8,9},{9,8},{10,11... | collective-permute-start | bytes 811016 | tf_op jit(solution)/shard_map/ppermute | solution.py:232
  41.1 5.8 %copy-start.2 = (bf16[1056,128]{1,0:T(8,128)(2,1)}, bf16[1056,128]{1,0:T(8,128)(2,1)S(1)}, u32[]{:S(2)}) copy-start(bf16[1056,128]{1,0:T(8,128)(2,1)S(1)} %collective-permute-done.8.refs_9_) | copy-start | bytes 811012
  41.2 5.7 %collective-permute-start.14 = (bf16[1056,128]{1,0:T(8,128)(2,1)S(1)}, bf16[1056,128]{1,0:T(8,128)(2,1)S(1)}, u32[]{:S(2)}, u32[]{:S(2)}) collective-permute-start(bf16[1056,128]{1,0:T(8,128)(2,1)S(1)} %collective-permute-done.8.refs_9_), channel_id=1, source_target_pairs={{0,1},{1,0},{2,3},{3,2},{4,5},{5,4},{6,7},{7,6},{8,9},{9,8},{10,11... | collective-permute-start | bytes 811016 | tf_op jit(solution)/shard_map/ppermute | solution.py:232
  41.6 5.3 %copy-start.8 = (bf16[528,128]{1,0:T(8,128)(2,1)}, bf16[528,128]{1,0:T(8,128)(2,1)S(1)}, u32[]{:S(2)}) copy-start(bf16[528,128]{1,0:T(8,128)(2,1)S(1)} %collective-permute-done.9.refs_10_) | copy-start | bytes 405508
  41.6 3.8 %collective-permute-start.10 = (bf16[528,128]{1,0:T(8,128)(2,1)S(1)}, bf16[528,128]{1,0:T(8,128)(2,1)S(1)}, u32[]{:S(2)}, u32[]{:S(2)}) collective-permute-start(bf16[528,128]{1,0:T(8,128)(2,1)S(1)} %collective-permute-done.3.refs_5_), channel_id=1, source_target_pairs={{0,1},{1,0},{2,3},{3,2},{4,5},{5,4},{6,7},{7,6},{8,9},{9,8},{10,11... | collective-permute-start | bytes 405512 | tf_op jit(solution)/shard_map/ppermute | solution.py:232
  44.0 2.9 %copy-start.9 = (bf16[528,128]{1,0:T(8,128)(2,1)}, bf16[528,128]{1,0:T(8,128)(2,1)S(1)}, u32[]{:S(2)}) copy-start(bf16[528,128]{1,0:T(8,128)(2,1)S(1)} %collective-permute-done.6.refs_7_) | copy-start | bytes 405508
  44.0 1.5 %collective-permute-start.12 = (bf16[528,128]{1,0:T(8,128)(2,1)S(1)}, bf16[528,128]{1,0:T(8,128)(2,1)S(1)}, u32[]{:S(2)}, u32[]{:S(2)}) collective-permute-start(bf16[528,128]{1,0:T(8,128)(2,1)S(1)} %collective-permute-done.6.refs_7_), channel_id=1, source_target_pairs={{0,1},{1,0},{2,3},{3,2},{4,5},{5,4},{6,7},{7,6},{8,9},{9,8},{10,11... | collective-permute-start | bytes 405512 | tf_op jit(solution)/shard_map/ppermute | solution.py:232
  45.5 1.5 %copy-start.10 = (bf16[528,128]{1,0:T(8,128)(2,1)}, bf16[528,128]{1,0:T(8,128)(2,1)S(1)}, u32[]{:S(2)}) copy-start(bf16[528,128]{1,0:T(8,128)(2,1)S(1)} %collective-permute-done.7.refs_8_) | copy-start | bytes 405508
  45.5 1.4 %collective-permute-start.13 = (bf16[528,128]{1,0:T(8,128)(2,1)S(1)}, bf16[528,128]{1,0:T(8,128)(2,1)S(1)}, u32[]{:S(2)}, u32[]{:S(2)}) collective-permute-start(bf16[528,128]{1,0:T(8,128)(2,1)S(1)} %collective-permute-done.7.refs_8_), channel_id=1, source_target_pairs={{0,1},{1,0},{2,3},{3,2},{4,5},{5,4},{6,7},{7,6},{8,9},{9,8},{10,11... | collective-permute-start | bytes 405512 | tf_op jit(solution)/shard_map/ppermute | solution.py:232
  45.5 1.5 %copy-start.11 = (bf16[528,128]{1,0:T(8,128)(2,1)}, bf16[528,128]{1,0:T(8,128)(2,1)S(1)}, u32[]{:S(2)}) copy-start(bf16[528,128]{1,0:T(8,128)(2,1)S(1)} %collective-permute-done.10.refs_11_) | copy-start | bytes 405508
  45.5 1.4 %copy-start.12 = (bf16[528,128]{1,0:T(8,128)(2,1)}, bf16[528,128]{1,0:T(8,128)(2,1)S(1)}, u32[]{:S(2)}) copy-start(bf16[528,128]{1,0:T(8,128)(2,1)S(1)} %collective-permute-done.12.refs_13_) | copy-start | bytes 405508
  60.3 5.3 %collective-permute-start.15 = (bf16[128,256]{1,0:T(8,128)(2,1)}, bf16[128,256]{1,0:T(8,128)(2,1)S(1)}, u32[]{:S(2)}, u32[]{:S(2)}) collective-permute-start(bf16[128,256]{1,0:T(8,128)(2,1)} %get-tuple-element.28), channel_id=1, source_target_pairs={{0,4},{1,5},{2,6},{3,7},{4,0},{5,1},{6,2},{7,3},{8,12},{9,13},{10,... | collective-permute-start | bytes 196616 | tf_op jit(solution)/shard_map/ppermute | solution.py:232
  60.8 7.5 %collective-permute-start.16 = (bf16[128,256]{1,0:T(8,128)(2,1)}, bf16[128,256]{1,0:T(8,128)(2,1)S(1)}, u32[]{:S(2)}, u32[]{:S(2)}) collective-permute-start(bf16[128,256]{1,0:T(8,128)(2,1)} %get-tuple-element.29), channel_id=1, source_target_pairs={{0,8},{1,9},{2,10},{3,11},{4,12},{5,13},{6,14},{7,15},{8,0},{9,1},... | collective-permute-start | bytes 196616 | tf_op jit(solution)/shard_map/ppermute | solution.py:232
  64.0 6.4 %collective-permute-start.17 = (bf16[128,256]{1,0:T(8,128)(2,1)}, bf16[128,256]{1,0:T(8,128)(2,1)S(1)}, u32[]{:S(2)}, u32[]{:S(2)}) collective-permute-start(bf16[128,256]{1,0:T(8,128)(2,1)} %get-tuple-element.30), channel_id=1, source_target_pairs={{0,12},{1,13},{2,14},{3,15},{4,8},{5,9},{6,10},{7,11},{8,4},{9,5},... | collective-permute-start | bytes 196616 | tf_op jit(solution)/shard_map/ppermute | solution.py:232
  70.4 3.2 %copy-start.1 = (bf16[512,256]{1,0:T(8,128)(2,1)}, bf16[512,256]{1,0:T(8,128)(2,1)S(1)}, u32[]{:S(2)}) copy-start(bf16[512,256]{1,0:T(8,128)(2,1)S(1)} %constant_dynamic-update-slice_fusion.2.pieces_ref) | copy-start | bytes 786436
  70.4 6.7 %collective-permute-start.18 = (bf16[512,256]{1,0:T(8,128)(2,1)S(1)}, bf16[512,256]{1,0:T(8,128)(2,1)S(1)}, u32[]{:S(2)}, u32[]{:S(2)}) collective-permute-start(bf16[512,256]{1,0:T(8,128)(2,1)S(1)} %constant_dynamic-update-slice_fusion.2.pieces_ref), channel_id=1, source_target_pairs={{0,16},{16,0},{1,17},{17,1},{2,18},{18,2},{3,19},{19,3},{4,20},{20... | collective-permute-start | bytes 786440 | tf_op jit(solution)/shard_map/ppermute | solution.py:289
  (4 other events, 3.0 us)

commit v3 on v2

--- a/solution.py
+++ b/solution.py
@@ -107,13 +107,17 @@
             slots[slot][:, at] = normed * jnp.asarray(head ** (-0.5), jnp.bfloat16)
 
 
-def attention_kernel(*refs, held, head):
+def attention_kernel(*refs, held, head, earlier):
     queries, refs = refs[:WAYS], refs[WAYS:]
     pieces, refs = refs[:held], refs[held:]
-    outs, (k_all, v_all, b_all, q_all, o_all) = refs[:WAYS], refs[WAYS:]
+    if earlier:
+        before, *outs, k_all, v_all, b_all, q_all, o_all = refs
+    else:
+        o_all, k_all, v_all, b_all, q_all = refs
     rows, width = queries[0].shape
     heads = width // head
     tiles = width // LANES
+    deep = head + EXTRA
     size = tiles * rows + EXTRA + width
     biases = []
     for g in range(held):
@@ -149,27 +153,29 @@
             scores = lax.dot_general(k_all[...], masked, (((1,), (1,)), ((), ())), preferred_element_type=jnp.float32)
             bias = b_all[...]
             scores = scores + jnp.concatenate([bias] * (span // LANES), axis=-1)
-            expo = jnp.exp(scores - jnp.max(scores, axis=0, keepdims=True)).astype(jnp.bfloat16)
+            highest = jnp.max(scores, axis=0, keepdims=True)
+            expo = jnp.exp(scores - highest).astype(jnp.bfloat16)
             numer = jnp.dot(v_all[h], expo, preferred_element_type=jnp.float32)
-            columns.append(numer[:head, :] / numer[head : head + 1, :])
-        o_all[index] = jnp.concatenate(columns, axis=0)
+            at = h * deep
+            if earlier:
+                highest_before = before[index, at + head + 8 : at + head + 9, :]
+                most = jnp.maximum(highest, highest_before)
+                now, then = jnp.exp(highest - most), jnp.exp(highest_before - most)
+                total = numer[head : head + 1, :] * now + before[index, at + head : at + head + 1, :] * then
+                both = numer[:head, :] * now + before[index, at : at + head, :] * then
+                columns.append(both / total)
+            else:
+                o_all[index, at : at + head + 8, :] = numer[: head + 8, :]
+                o_all[index, at + head + 8 : at + deep, :] = jnp.broadcast_to(highest, (deep - head - 8, span))
+        if earlier:
+            o_all[index] = jnp.concatenate(columns, axis=0)
         return 0
 
     lax.fori_loop(0, WAYS // 2, one_block, 0)
-    for slot in range(WAYS):
-        at = (slot % 2) * rows
-        outs[slot][...] = o_all[slot // 2, :, at : at + rows].T.astype(jnp.bfloat16)
-
-
-def project(pieces_ref, w_ref, way, start, span):
-    width = pieces_ref.shape[1]
-    rows = pieces_ref.shape[0] // WAYS
-    total = jnp.zeros((rows, span), jnp.float32)
-    for slot in range(WAYS):
-        at = pl.multiple_of((way ^ slot) * width, width)
-        w = w_ref[pl.ds(at, width), pl.ds(start, span)]
-        total += jnp.dot(pieces_ref[slot * rows : (slot + 1) * rows, :], w, preferred_element_type=jnp.float32)
-    return total
+    if earlier:
+        for slot in range(WAYS):
+            at = (slot % 2) * rows
+            outs[slot][...] = o_all[slot // 2, :, at : at + rows].T.astype(jnp.bfloat16)
 
 
 def half_of(half):
@@ -185,23 +191,24 @@
     copy.wait()
 
 
-def project(pieces_ref, w_ref, way):
-    width = pieces_ref.shape[1]
-    rows = pieces_ref.shape[0] // WAYS
+def project(pieces, w_ref, way):
+    rows, width = pieces[0].shape
     total = jnp.zeros((rows, w_ref.shape[1]), jnp.float32)
-    for slot in range(WAYS):
+    for slot, piece in enumerate(pieces):
         w = w_ref[pl.ds(pl.multiple_of((way ^ slot) * width, width), width), :]
-        total += jnp.dot(pieces_ref[slot * rows : (slot + 1) * rows, :], w, preferred_element_type=jnp.float32)
+        total += jnp.dot(piece[...], w, preferred_element_type=jnp.float32)
     return total
 
 
-def own_kernel(pieces_ref, w_ref, out_ref, *, groups):
-    out_ref[...] = project(pieces_ref, w_ref, lax.axis_index("seq") // groups)
-
-
-def final_kernel(block_ref, pieces_ref, own_ref, w_ref, modulation_ref, out_ref, *, groups, half):
+def own_kernel(*refs, groups):
+    *pieces, w_ref, out_ref = refs
+    out_ref[...] = project(pieces, w_ref, lax.axis_index("seq") // groups)
+
+
+def final_kernel(block_ref, *refs, groups, half):
+    *pieces, own_ref, w_ref, modulation_ref, out_ref = refs
     spare, span, start = half_of(half)
-    total = project(pieces_ref, w_ref, lax.axis_index("seq") // groups)
+    total = project(pieces, w_ref, lax.axis_index("seq") // groups)
     is_text = text_rows(block_ref[0], total.shape[0])
     table = modulation_ref[:, pl.ds(start, span)]
     gate = jnp.where(is_text, table[5:6, :], table[2:3, :])
@@ -225,7 +232,14 @@
     bf16 = jnp.bfloat16
     smem = pl.BlockSpec(memory_space=pltpu.SMEM)
     vmem = pl.BlockSpec(memory_space=pltpu.VMEM)
-    hbm = pl.BlockSpec(memory_space=pl.ANY)
+    hbm = pl.BlockSpec(memory_space=pltpu.HBM)
+
+    def limit(mib):
+        return pltpu.CompilerParams(vmem_limit_bytes=min(mib, 60) * 2**20)
+
+    w_qkv, w_out, states, modulation = (
+        pltpu.with_memory_space_constraint(x, pltpu.HBM) for x in (w_qkv, w_out, states, modulation)
+    )
     held_in = functools.partial(pltpu.with_memory_space_constraint, memory_space=pltpu.VMEM)
 
     def exchange(x, bits):
@@ -236,10 +250,11 @@
         return [slots[0]] + [far[s] for s in range(1, WAYS)]
 
     size = (width // LANES) * rows + EXTRA + width
-    kv_piece = jax.ShapeDtypeStruct((size, LANES), bf16)
-    piece = jax.ShapeDtypeStruct((rows, width), bf16)
+    kv_piece = pltpu.VMEM((size, LANES), bf16)
+    piece = pltpu.VMEM((rows, width), bf16)
     *kv_slots, modded = pl.pallas_call(
         functools.partial(key_value_kernel, head=head, groups=groups),
+        compiler_params=limit(16),
         in_specs=[smem, smem, hbm, hbm, hbm, vmem],
         out_shape=[kv_piece] * WAYS + [pltpu.VMEM((rows, features), bf16)],
         scratch_shapes=[
@@ -252,6 +267,7 @@
     kv = spread(kv_slots)
     q_slots = pl.pallas_call(
         functools.partial(query_kernel, head=head, groups=groups),
+        compiler_params=limit(10),
         in_specs=[vmem, hbm, vmem],
         out_shape=[piece] * WAYS,
         scratch_shapes=[pltpu.VMEM((features, inner), bf16), pltpu.SemaphoreType.DMA],
@@ -261,42 +277,65 @@
     span = half + half % LANES
     w_half = pl.pallas_call(
         fetch_kernel,
+        compiler_params=limit(2),
         in_specs=[hbm],
         out_shape=pltpu.VMEM((inner, span), bf16),
         scratch_shapes=[pltpu.SemaphoreType.DMA],
     )(w_out)
-    held = [kv[0], kv[1], jnp.concatenate(kv[2:], axis=0)]
-    bit = groups // 2
-    while bit:
-        held = held + [exchange(x, bit) for x in held]
-        bit //= 2
-
-    keys = count * rows
-    o_slots = pl.pallas_call(
-        functools.partial(attention_kernel, held=len(held), head=head),
-        in_specs=[vmem] * (WAYS + len(held)),
-        out_shape=[piece] * WAYS,
-        scratch_shapes=[
-            pltpu.VMEM((keys, width), bf16),
-            pltpu.VMEM((width // head, head + EXTRA, keys), bf16),
-            pltpu.VMEM((keys, LANES), jnp.float32),
-            pltpu.VMEM((WAYS * rows, width), bf16),
-            pltpu.VMEM((WAYS // 2, width, 2 * rows), jnp.float32),
-        ],
-    )(*queries, *held)
-    attended = jnp.concatenate(spread(o_slots), axis=0)
+    top = groups // 2
+
+    def gathered(held):
+        bit = top // 2
+        while bit:
+            held = held + [exchange(x, bit) for x in held]
+            bit //= 2
+        return held
+
+    near = gathered(kv)
+    order = [0, 1, 3, 2]
+    crossed = {i: exchange(kv[i], top) for i in order}
+    far = gathered([crossed[i] for i in order])
+    keys = count * rows // 2
+    deep = head + EXTRA
+    roomy = count * rows <= 4096
+
+    def attend(pieces, before, out_shape, scratch):
+        ins = [held_in(x) if roomy else x for x in [*queries, *pieces]] + before
+        return pl.pallas_call(
+            functools.partial(attention_kernel, held=len(pieces), head=head, earlier=bool(before)),
+            compiler_params=limit(8 + keys // 96),
+            in_specs=[vmem] * len(ins),
+            out_shape=out_shape,
+            scratch_shapes=[
+                pltpu.VMEM((keys, width), bf16),
+                pltpu.VMEM((width // head, deep, keys), bf16),
+                pltpu.VMEM((keys, LANES), jnp.float32),
+                pltpu.VMEM((WAYS * rows, width), bf16),
+            ]
+            + scratch,
+        )(*ins)
+
+    part = pltpu.VMEM((WAYS // 2, deep * (width // head), 2 * rows), jnp.float32)
+    before = attend(near, [], part, [])
+    merged = pltpu.VMEM((WAYS // 2, width, 2 * rows), jnp.float32)
+    o_slots = attend(far, [held_in(before)], [piece] * WAYS, [merged])
+    attended = spread(o_slots)
     cfg_count = lax.axis_size("cfg")
-    partner = lax.ppermute(attended, "cfg", [(i, i ^ 1) for i in range(cfg_count)])
+    partner = []
+    for x in attended:
+        partner.append(lax.ppermute(x, "cfg", [(j, j ^ 1) for j in range(cfg_count)]))
     own = pl.pallas_call(
         functools.partial(own_kernel, groups=groups),
-        in_specs=[vmem] * 2,
+        compiler_params=limit(6),
+        in_specs=[vmem] * (WAYS + 1),
         out_shape=pltpu.VMEM((rows, span), jnp.float32),
-    )(attended, held_in(w_half))
+    )(*map(held_in, attended), held_in(w_half))
     guided = pl.pallas_call(
         functools.partial(final_kernel, groups=groups, half=half),
-        in_specs=[smem] + [vmem] * 4,
+        compiler_params=limit(8),
+        in_specs=[smem] + [vmem] * (WAYS + 3),
         out_shape=jax.ShapeDtypeStruct((half, rows), jnp.float32),
-    )(block_order, partner, held_in(own), held_in(w_half), modulation)
+    )(block_order, *map(held_in, partner), held_in(own), held_in(w_half), modulation)
     return guided.T
 
 

time: 80.5 us -> 69 us (0.86)
  waiting for transfers between devices: 25 us -> 18.4 us
  Pallas kernels: 28.2 us -> 23 us
  starting transfers between devices: 23 us -> 25.2 us
  local copies, waits for them, and re-layouts: 2.39 us -> 0.65 us
    ppermute x18 -> x21, waiting for transfers between devices: 22.9 us -> 17.7 us  [exchange(): return lax.ppermute(x, 'seq', [(i, i ^ bits) for i in range(count)])]
    ppermute x1 -> x4, starting transfers between devices: 1.55 us -> 5 us  [block(): lax.ppermute(x, 'cfg', [(j, j ^ 1) for j in range(cfg_count)])]
    pallas_call x3 -> x4, Pallas kernels: 15.6 us -> 13.2 us  [the longest x2 11.1 us: attend(): pl.pallas_call(functools.partial(attention_kernel, held=len(pieces), head...]
    unnamed x38 -> x4, local copies, waits for them, and re-layouts: 2.36 us -> 0.65 us
    ppermute x1 -> x4, waiting for transfers between devices: 2.14 us -> 0.67 us  [block(): lax.ppermute(x, 'cfg', [(j, j ^ 1) for j in range(cfg_count)])]
    pallas_call x1, Pallas kernels: 5.73 us -> 4.37 us  [block(): pl.pallas_call(functools.partial(key_value_kernel, head=head, groups=grou...]
    pallas_call x1, Pallas kernels: 4.57 us -> 3.23 us  [block(): pl.pallas_call(functools.partial(query_kernel, head=head, groups=groups),...]
    ppermute x18 -> x21, starting transfers between devices: 21.4 us -> 20.2 us  [exchange(): return lax.ppermute(x, 'seq', [(i, i ^ bits) for i in range(count)])]
  transfers between devices with their start and end apart: 19 -> 25, of which waited for: 9 -> 8; matrix products, arithmetic and copies ran while one was open for 1% -> 0% of each run, Pallas kernels for 9% -> 11%
where the time goes in v3:
time: 69 us; the launch traced here: 68.7 us
  starting transfers between devices  25.2 us (37%)
  Pallas kernels  23 us (33%)
  waiting for transfers between devices  18.4 us (27%)
  between operations  1.44 us (2%)
    ppermute x21, starting transfers between devices, exchange(): return lax.ppermute(x, 'seq', [(i, i ^ bits) for i in range(count)])  20.2 us
    ppermute x21, waiting for transfers between devices, exchange(): return lax.ppermute(x, 'seq', [(i, i ^ bits) for i in range(count)])  17.7 us
    pallas_call x2, Pallas kernels, attend(): pl.pallas_call(functools.partial(attention_kernel, held=len(pieces), head...  11.1 us
    ppermute x4, starting transfers between devices, block(): lax.ppermute(x, 'cfg', [(j, j ^ 1) for j in range(cfg_count)])  5 us
    pallas_call x1, Pallas kernels, block(): pl.pallas_call(functools.partial(key_value_kernel, head=head, groups=grou...  4.37 us
    pallas_call x1, Pallas kernels, block(): pl.pallas_call(functools.partial(query_kernel, head=head, groups=groups),...  3.23 us
    pallas_call x1, Pallas kernels, block(): pl.pallas_call(functools.partial(final_kernel, groups=groups, half=half),...  2.21 us
    pallas_call x1, Pallas kernels, block(): pl.pallas_call(fetch_kernel, compiler_params=limit(2), in_specs=[hbm], ou...  1.6 us
  transfers between devices with their start and end apart: 25, of which 8 were waited for; matrix products, arithmetic and copies ran while one was open for 0% of the time, Pallas kernels for 11%

profile of v3, /device:TPU:0, one launch (start us, length us, event | category | flops | bytes accessed | tf_op | source)
XLA Modules:
  0.0 68.7 jit_solution(10510638985711519097)
XLA Ops:
  1.3 0.6 copy-done
  2.0 4.4 %shard_map.82 = (bf16[528,128]{1,0:T(8,128)(2,1)S(1)}, bf16[528,128]{1,0:T(8,128)(2,1)S(1)}, bf16[528,128]{1,0:T(8,128)(2,1)S(1)}, bf16[528,128]{1,0:T(8,128)(2,1)S(1)}, bf16[128,1920]{1,0:T(8,128)(2,1)S(1)}) custom-call(s32[1]{0:T(128)S(6)} %copy.10.block_ref, s32[1]{0:T(128)S(6)} %copy.9.count_ref, bf16[128,1920]{1,0:T(8,128)(2,1)} %bitcast.6, ...), custom_call_target="tpu_custom_call" | custom-call | tf_op jit(solution)/shard_map/pallas_call | solution.py:255
  6.3 3.2 %shard_map.83 = (bf16[128,256]{1,0:T(8,128)(2,1)S(1)}, bf16[128,256]{1,0:T(8,128)(2,1)S(1)}, bf16[128,256]{1,0:T(8,128)(2,1)S(1)}, bf16[128,256]{1,0:T(8,128)(2,1)S(1)}) custom-call(bf16[128,1920]{1,0:T(8,128)(2,1)S(1)} %get-tuple-element.18.modded_ref, bf16[3,1920,1024]{2,1,0:T(8,128)(2,1)} %w_ref.4, f32[1,64]{1,0:T(1,128)S(1)} %bitcast.5), custom_call_target="tpu_custom_call" | custom-call | tf_op jit(solution)/shard_map/pallas_call | solution.py:268
  9.6 3.1 %collective-permute-start = (bf16[128,256]{1,0:T(8,128)(2,1)S(1)}, bf16[128,256]{1,0:T(8,128)(2,1)S(1)}, u32[]{:S(2)}, u32[]{:S(2)}) collective-permute-start(bf16[128,256]{1,0:T(8,128)(2,1)S(1)} %get-tuple-element.20), channel_id=1, source_target_pairs={{0,4},{1,5},{2,6},{3,7},{4,0},{5,1},{6,2},{7,3},{8,12},{9,13},{10,... | collective-permute-start | bytes 196616 | tf_op jit(solution)/shard_map/ppermute | solution.py:246
  12.7 2.6 %collective-permute-start.1 = (bf16[128,256]{1,0:T(8,128)(2,1)S(1)}, bf16[128,256]{1,0:T(8,128)(2,1)S(1)}, u32[]{:S(2)}, u32[]{:S(2)}) collective-permute-start(bf16[128,256]{1,0:T(8,128)(2,1)S(1)} %get-tuple-element.21), channel_id=1, source_target_pairs={{0,8},{1,9},{2,10},{3,11},{4,12},{5,13},{6,14},{7,15},{8,0},{9,1},... | collective-permute-start | bytes 196616 | tf_op jit(solution)/shard_map/ppermute | solution.py:246
  15.3 0.9 %collective-permute-start.4 = (bf16[528,128]{1,0:T(8,128)(2,1)S(1)}, bf16[528,128]{1,0:T(8,128)(2,1)S(1)}, u32[]{:S(2)}, u32[]{:S(2)}) collective-permute-start(bf16[528,128]{1,0:T(8,128)(2,1)S(1)} %get-tuple-element.24), channel_id=1, source_target_pairs={{0,4},{1,5},{2,6},{3,7},{4,0},{5,1},{6,2},{7,3},{8,12},{9,13},{10,... | collective-permute-start | bytes 405512 | tf_op jit(solution)/shard_map/ppermute | solution.py:246
  16.2 2.9 %collective-permute-start.6 = (bf16[528,128]{1,0:T(8,128)(2,1)S(1)}, bf16[528,128]{1,0:T(8,128)(2,1)S(1)}, u32[]{:S(2)}, u32[]{:S(2)}) collective-permute-start(bf16[528,128]{1,0:T(8,128)(2,1)S(1)} %get-tuple-element.25), channel_id=1, source_target_pairs={{0,12},{1,13},{2,14},{3,15},{4,8},{5,9},{6,10},{7,11},{8,4},{9,5},... | collective-permute-start | bytes 405512 | tf_op jit(solution)/shard_map/ppermute | solution.py:246
  19.1 0.6 collective-permute-start.8
  20.0 2.1 %collective-permute-done.2.refs_3_ = bf16[128,256]{1,0:T(8,128)(2,1)S(1)} collective-permute-done((bf16[128,256]{1,0:T(8,128)(2,1)S(1)}, bf16[128,256]{1,0:T(8,128)(2,1)S(1)}, u32[]{:S(2)}, u32[]{:S(2)}) %collective-permute-start.2) | collective-permute-done | bytes 65568 | tf_op jit(solution)/shard_map/ppermute | solution.py:246
  22.2 1.5 %collective-permute-start.3 = (bf16[528,128]{1,0:T(8,128)(2,1)S(1)}, bf16[528,128]{1,0:T(8,128)(2,1)S(1)}, u32[]{:S(2)}, u32[]{:S(2)}) collective-permute-start(bf16[528,128]{1,0:T(8,128)(2,1)S(1)} %get-tuple-element.23.refs_4_), channel_id=1, source_target_pairs={{0,2},{1,3},{2,0},{3,1},{4,6},{5,7},{6,4},{7,5},{8,10},{9,11},{10,... | collective-permute-start | bytes 405512 | tf_op jit(solution)/shard_map/ppermute | solution.py:246
  23.7 3.9 %collective-permute-done.6.refs_7_ = bf16[528,128]{1,0:T(8,128)(2,1)S(1)} collective-permute-done((bf16[528,128]{1,0:T(8,128)(2,1)S(1)}, bf16[528,128]{1,0:T(8,128)(2,1)S(1)}, u32[]{:S(2)}, u32[]{:S(2)}) %collective-permute-start.6) | collective-permute-done | bytes 135200 | tf_op jit(solution)/shard_map/ppermute | solution.py:246
  27.6 1.5 %collective-permute-start.5 = (bf16[528,128]{1,0:T(8,128)(2,1)S(1)}, bf16[528,128]{1,0:T(8,128)(2,1)S(1)}, u32[]{:S(2)}, u32[]{:S(2)}) collective-permute-start(bf16[528,128]{1,0:T(8,128)(2,1)S(1)} %collective-permute-done.4.refs_5_), channel_id=1, source_target_pairs={{0,2},{1,3},{2,0},{3,1},{4,6},{5,7},{6,4},{7,5},{8,10},{9,11},{10,... | collective-permute-start | bytes 405512 | tf_op jit(solution)/shard_map/ppermute | solution.py:246
  29.1 3.8 %collective-permute-done.8.refs_6_ = bf16[528,128]{1,0:T(8,128)(2,1)S(1)} collective-permute-done((bf16[528,128]{1,0:T(8,128)(2,1)S(1)}, bf16[528,128]{1,0:T(8,128)(2,1)S(1)}, u32[]{:S(2)}, u32[]{:S(2)}) %collective-permute-start.8) | collective-permute-done | bytes 135200 | tf_op jit(solution)/shard_map/ppermute | solution.py:246
  33.0 1.5 %collective-permute-start.7 = (bf16[528,128]{1,0:T(8,128)(2,1)S(1)}, bf16[528,128]{1,0:T(8,128)(2,1)S(1)}, u32[]{:S(2)}, u32[]{:S(2)}) collective-permute-start(bf16[528,128]{1,0:T(8,128)(2,1)S(1)} %collective-permute-done.6.refs_7_), channel_id=1, source_target_pairs={{0,2},{1,3},{2,0},{3,1},{4,6},{5,7},{6,4},{7,5},{8,10},{9,11},{10,... | collective-permute-start | bytes 405512 | tf_op jit(solution)/shard_map/ppermute | solution.py:246
  34.5 0.5 collective-permute-start.9
  35.0 0.5 collective-permute-start.10
  35.6 3.8 %collective-permute-done.7.refs_6_ = bf16[528,128]{1,0:T(8,128)(2,1)S(1)} collective-permute-done((bf16[528,128]{1,0:T(8,128)(2,1)S(1)}, bf16[528,128]{1,0:T(8,128)(2,1)S(1)}, u32[]{:S(2)}, u32[]{:S(2)}) %collective-permute-start.7) | collective-permute-done | bytes 135200 | tf_op jit(solution)/shard_map/ppermute | solution.py:246
  39.4 2.4 %collective-permute-done.9.refs_7_ = bf16[528,128]{1,0:T(8,128)(2,1)S(1)} collective-permute-done((bf16[528,128]{1,0:T(8,128)(2,1)S(1)}, bf16[528,128]{1,0:T(8,128)(2,1)S(1)}, u32[]{:S(2)}, u32[]{:S(2)}) %collective-permute-start.9) | collective-permute-done | bytes 135200 | tf_op jit(solution)/shard_map/ppermute | solution.py:246
  41.9 5.4 %shard_map.84.refs_12_ = f32[2,320,256]{2,1,0:T(8,128)S(1)} custom-call(bf16[128,256]{1,0:T(8,128)(2,1)S(1)} %get-tuple-element.19.refs_0_, bf16[128,256]{1,0:T(8,128)(2,1)S(1)} %collective-permute-done.refs_1_, bf16[128,256]{1,0:T(8,128)(2,1)S(1)} %collective-permute-done.1.refs_2_, bf16[128,256]{1,0:T(8,128)(2,1)S(1)} %collective-permute-done.2.refs_3_, ...), custom_call_target="tpu_custom_call" | custom-call | tf_op jit(solution)/shard_map/pallas_call | solution.py:304
  47.3 5.7 %shard_map.85 = (bf16[128,256]{1,0:T(8,128)(2,1)S(1)}, bf16[128,256]{1,0:T(8,128)(2,1)S(1)}, bf16[128,256]{1,0:T(8,128)(2,1)S(1)}, bf16[128,256]{1,0:T(8,128)(2,1)S(1)}) custom-call(bf16[128,256]{1,0:T(8,128)(2,1)S(1)} %get-tuple-element.19.refs_0_, bf16[128,256]{1,0:T(8,128)(2,1)S(1)} %collective-permute-done.refs_1_, ...), custom_call_target="tpu_custom_call" | custom-call | tf_op jit(solution)/shard_map/pallas_call | solution.py:304
  53.1 0.4 collective-permute-start.19
  53.4 2.7 %collective-permute-start.21 = (bf16[128,256]{1,0:T(8,128)(2,1)S(1)}, bf16[128,256]{1,0:T(8,128)(2,1)S(1)}, u32[]{:S(2)}, u32[]{:S(2)}) collective-permute-start(bf16[128,256]{1,0:T(8,128)(2,1)S(1)} %get-tuple-element.29), channel_id=1, source_target_pairs={{0,8},{1,9},{2,10},{3,11},{4,12},{5,13},{6,14},{7,15},{8,0},{9,1},... | collective-permute-start | bytes 196616 | tf_op jit(solution)/shard_map/ppermute | solution.py:246
  56.2 1.3 %collective-permute-start.23 = (bf16[128,256]{1,0:T(8,128)(2,1)S(1)}, bf16[128,256]{1,0:T(8,128)(2,1)S(1)}, u32[]{:S(2)}, u32[]{:S(2)}) collective-permute-start(bf16[128,256]{1,0:T(8,128)(2,1)S(1)} %get-tuple-element.30), channel_id=1, source_target_pairs={{0,12},{1,13},{2,14},{3,15},{4,8},{5,9},{6,10},{7,11},{8,4},{9,5},... | collective-permute-start | bytes 196616 | tf_op jit(solution)/shard_map/ppermute | solution.py:246
  57.5 1.5 %collective-permute-start.18 = (bf16[128,256]{1,0:T(8,128)(2,1)S(1)}, bf16[128,256]{1,0:T(8,128)(2,1)S(1)}, u32[]{:S(2)}, u32[]{:S(2)}) collective-permute-start(bf16[128,256]{1,0:T(8,128)(2,1)S(1)} %get-tuple-element.27.refs_0_), channel_id=1, source_target_pairs={{0,16},{16,0},{1,17},{17,1},{2,18},{18,2},{3,19},{19,3},{4,20},{20... | collective-permute-start | bytes 196616 | tf_op jit(solution)/shard_map/ppermute | solution.py:326
  59.0 1.4 %collective-permute-start.20 = (bf16[128,256]{1,0:T(8,128)(2,1)S(1)}, bf16[128,256]{1,0:T(8,128)(2,1)S(1)}, u32[]{:S(2)}, u32[]{:S(2)}) collective-permute-start(bf16[128,256]{1,0:T(8,128)(2,1)S(1)} %collective-permute-done.19.refs_1_), channel_id=1, source_target_pairs={{0,16},{16,0},{1,17},{17,1},{2,18},{18,2},{3,19},{19,3},{4,20},{20... | collective-permute-start | bytes 196616 | tf_op jit(solution)/shard_map/ppermute | solution.py:326
  60.4 0.6 collective-permute-start.22
  61.0 1.2 %collective-permute-done.23.refs_3_ = bf16[128,256]{1,0:T(8,128)(2,1)S(1)} collective-permute-done((bf16[128,256]{1,0:T(8,128)(2,1)S(1)}, bf16[128,256]{1,0:T(8,128)(2,1)S(1)}, u32[]{:S(2)}, u32[]{:S(2)}) %collective-permute-start.23) | collective-permute-done | bytes 65568 | tf_op jit(solution)/shard_map/ppermute | solution.py:246
  62.2 1.5 %collective-permute-start.24 = (bf16[128,256]{1,0:T(8,128)(2,1)S(1)}, bf16[128,256]{1,0:T(8,128)(2,1)S(1)}, u32[]{:S(2)}, u32[]{:S(2)}) collective-permute-start(bf16[128,256]{1,0:T(8,128)(2,1)S(1)} %collective-permute-done.23.refs_3_), channel_id=1, source_target_pairs={{0,16},{16,0},{1,17},{17,1},{2,18},{18,2},{3,19},{19,3},{4,20},{20... | collective-permute-start | bytes 196616 | tf_op jit(solution)/shard_map/ppermute | solution.py:326
  63.7 1.6 %shard_map.86.refs_4_.refs_5_ = bf16[1024,1024]{1,0:T(8,128)(2,1)S(1)} custom-call(bf16[1024,1920]{1,0:T(8,128)(2,1)} %w_ref.5), custom_call_target="tpu_custom_call" | custom-call | tf_op jit(solution)/shard_map/pallas_call | solution.py:278
  65.3 0.5 shard_map.87.refs_4_
  65.8 0.7 collective-permute-done.24.refs_3_
  66.5 2.2 %shard_map.88 = f32[960,128]{1,0:T(8,128)} custom-call(s32[1]{0:T(128)S(6)} %copy.10.block_ref, bf16[128,256]{1,0:T(8,128)(2,1)S(1)} %collective-permute-done.18.refs_0_, bf16[128,256]{1,0:T(8,128)(2,1)S(1)} %collective-permute-done.20.refs_1_, bf16[128,256]{1,0:T(8,128)(2,1)S(1)} %collective-permute-done.22.refs_2_, ...), custom_call_target="tpu_custom_call" | custom-call | tf_op jit(solution)/shard_map/pallas_call | solution.py:333
  (29 shorter events, 0.5 us)
Async XLA Ops:
  1.3 0.7 copy-start
  2.0 4.4 %copy-start.1 = (f32[64]{0:T(128)S(1)}, f32[64]{0:T(128)}, u32[]{:S(2)}) copy-start(f32[64]{0:T(128)} %param.11) | copy-start | bytes 772
  9.6 9.5 %collective-permute-start = (bf16[128,256]{1,0:T(8,128)(2,1)S(1)}, bf16[128,256]{1,0:T(8,128)(2,1)S(1)}, u32[]{:S(2)}, u32[]{:S(2)}) collective-permute-start(bf16[128,256]{1,0:T(8,128)(2,1)S(1)} %get-tuple-element.20), channel_id=1, source_target_pairs={{0,4},{1,5},{2,6},{3,7},{4,0},{5,1},{6,2},{7,3},{8,12},{9,13},{10,... | collective-permute-start | bytes 196616 | tf_op jit(solution)/shard_map/ppermute | solution.py:246
  12.7 7.3 %collective-permute-start.1 = (bf16[128,256]{1,0:T(8,128)(2,1)S(1)}, bf16[128,256]{1,0:T(8,128)(2,1)S(1)}, u32[]{:S(2)}, u32[]{:S(2)}) collective-permute-start(bf16[128,256]{1,0:T(8,128)(2,1)S(1)} %get-tuple-element.21), channel_id=1, source_target_pairs={{0,8},{1,9},{2,10},{3,11},{4,12},{5,13},{6,14},{7,15},{8,0},{9,1},... | collective-permute-start | bytes 196616 | tf_op jit(solution)/shard_map/ppermute | solution.py:246
  15.3 6.9 %collective-permute-start.2 = (bf16[128,256]{1,0:T(8,128)(2,1)S(1)}, bf16[128,256]{1,0:T(8,128)(2,1)S(1)}, u32[]{:S(2)}, u32[]{:S(2)}) collective-permute-start(bf16[128,256]{1,0:T(8,128)(2,1)S(1)} %get-tuple-element.22), channel_id=1, source_target_pairs={{0,12},{1,13},{2,14},{3,15},{4,8},{5,9},{6,10},{7,11},{8,4},{9,5},... | collective-permute-start | bytes 196616 | tf_op jit(solution)/shard_map/ppermute | solution.py:246
  15.3 8.4 %collective-permute-start.4 = (bf16[528,128]{1,0:T(8,128)(2,1)S(1)}, bf16[528,128]{1,0:T(8,128)(2,1)S(1)}, u32[]{:S(2)}, u32[]{:S(2)}) collective-permute-start(bf16[528,128]{1,0:T(8,128)(2,1)S(1)} %get-tuple-element.24), channel_id=1, source_target_pairs={{0,4},{1,5},{2,6},{3,7},{4,0},{5,1},{6,2},{7,3},{8,12},{9,13},{10,... | collective-permute-start | bytes 405512 | tf_op jit(solution)/shard_map/ppermute | solution.py:246
  16.2 11.4 %collective-permute-start.6 = (bf16[528,128]{1,0:T(8,128)(2,1)S(1)}, bf16[528,128]{1,0:T(8,128)(2,1)S(1)}, u32[]{:S(2)}, u32[]{:S(2)}) collective-permute-start(bf16[528,128]{1,0:T(8,128)(2,1)S(1)} %get-tuple-element.25), channel_id=1, source_target_pairs={{0,12},{1,13},{2,14},{3,15},{4,8},{5,9},{6,10},{7,11},{8,4},{9,5},... | collective-permute-start | bytes 405512 | tf_op jit(solution)/shard_map/ppermute | solution.py:246
  19.1 13.8 %collective-permute-start.8 = (bf16[528,128]{1,0:T(8,128)(2,1)S(1)}, bf16[528,128]{1,0:T(8,128)(2,1)S(1)}, u32[]{:S(2)}, u32[]{:S(2)}) collective-permute-start(bf16[528,128]{1,0:T(8,128)(2,1)S(1)} %get-tuple-element.26), channel_id=1, source_target_pairs={{0,8},{1,9},{2,10},{3,11},{4,12},{5,13},{6,14},{7,15},{8,0},{9,1},... | collective-permute-start | bytes 405512 | tf_op jit(solution)/shard_map/ppermute | solution.py:246
  20.0 12.9 %collective-permute-start.14 = (bf16[528,128]{1,0:T(8,128)(2,1)S(1)}, bf16[528,128]{1,0:T(8,128)(2,1)S(1)}, u32[]{:S(2)}, u32[]{:S(2)}) collective-permute-start(bf16[528,128]{1,0:T(8,128)(2,1)S(1)} %get-tuple-element.23.refs_4_), channel_id=1, source_target_pairs={{0,1},{1,0},{2,3},{3,2},{4,5},{5,4},{6,7},{7,6},{8,9},{9,8},{10,11... | collective-permute-start | bytes 405512 | tf_op jit(solution)/shard_map/ppermute | solution.py:246
  22.2 12.3 %collective-permute-start.3 = (bf16[528,128]{1,0:T(8,128)(2,1)S(1)}, bf16[528,128]{1,0:T(8,128)(2,1)S(1)}, u32[]{:S(2)}, u32[]{:S(2)}) collective-permute-start(bf16[528,128]{1,0:T(8,128)(2,1)S(1)} %get-tuple-element.23.refs_4_), channel_id=1, source_target_pairs={{0,2},{1,3},{2,0},{3,1},{4,6},{5,7},{6,4},{7,5},{8,10},{9,11},{10,... | collective-permute-start | bytes 405512 | tf_op jit(solution)/shard_map/ppermute | solution.py:246
  23.7 11.3 %collective-permute-start.15 = (bf16[528,128]{1,0:T(8,128)(2,1)S(1)}, bf16[528,128]{1,0:T(8,128)(2,1)S(1)}, u32[]{:S(2)}, u32[]{:S(2)}) collective-permute-start(bf16[528,128]{1,0:T(8,128)(2,1)S(1)} %collective-permute-done.4.refs_5_), channel_id=1, source_target_pairs={{0,1},{1,0},{2,3},{3,2},{4,5},{5,4},{6,7},{7,6},{8,9},{9,8},{10,11... | collective-permute-start | bytes 405512 | tf_op jit(solution)/shard_map/ppermute | solution.py:246
  27.6 7.4 %collective-permute-start.5 = (bf16[528,128]{1,0:T(8,128)(2,1)S(1)}, bf16[528,128]{1,0:T(8,128)(2,1)S(1)}, u32[]{:S(2)}, u32[]{:S(2)}) collective-permute-start(bf16[528,128]{1,0:T(8,128)(2,1)S(1)} %collective-permute-done.4.refs_5_), channel_id=1, source_target_pairs={{0,2},{1,3},{2,0},{3,1},{4,6},{5,7},{6,4},{7,5},{8,10},{9,11},{10,... | collective-permute-start | bytes 405512 | tf_op jit(solution)/shard_map/ppermute | solution.py:246
  33.0 2.6 %collective-permute-start.17 = (bf16[528,128]{1,0:T(8,128)(2,1)S(1)}, bf16[528,128]{1,0:T(8,128)(2,1)S(1)}, u32[]{:S(2)}, u32[]{:S(2)}) collective-permute-start(bf16[528,128]{1,0:T(8,128)(2,1)S(1)} %collective-permute-done.6.refs_7_), channel_id=1, source_target_pairs={{0,1},{1,0},{2,3},{3,2},{4,5},{5,4},{6,7},{7,6},{8,9},{9,8},{10,11... | collective-permute-start | bytes 405512 | tf_op jit(solution)/shard_map/ppermute | solution.py:246
  33.0 6.5 %collective-permute-start.7 = (bf16[528,128]{1,0:T(8,128)(2,1)S(1)}, bf16[528,128]{1,0:T(8,128)(2,1)S(1)}, u32[]{:S(2)}, u32[]{:S(2)}) collective-permute-start(bf16[528,128]{1,0:T(8,128)(2,1)S(1)} %collective-permute-done.6.refs_7_), channel_id=1, source_target_pairs={{0,2},{1,3},{2,0},{3,1},{4,6},{5,7},{6,4},{7,5},{8,10},{9,11},{10,... | collective-permute-start | bytes 405512 | tf_op jit(solution)/shard_map/ppermute | solution.py:246
  34.5 7.4 %collective-permute-start.9 = (bf16[528,128]{1,0:T(8,128)(2,1)S(1)}, bf16[528,128]{1,0:T(8,128)(2,1)S(1)}, u32[]{:S(2)}, u32[]{:S(2)}) collective-permute-start(bf16[528,128]{1,0:T(8,128)(2,1)S(1)} %collective-permute-done.8.refs_6_), channel_id=1, source_target_pairs={{0,2},{1,3},{2,0},{3,1},{4,6},{5,7},{6,4},{7,5},{8,10},{9,11},{10,... | collective-permute-start | bytes 405512 | tf_op jit(solution)/shard_map/ppermute | solution.py:246
  35.0 6.9 %collective-permute-start.16 = (bf16[528,128]{1,0:T(8,128)(2,1)S(1)}, bf16[528,128]{1,0:T(8,128)(2,1)S(1)}, u32[]{:S(2)}, u32[]{:S(2)}) collective-permute-start(bf16[528,128]{1,0:T(8,128)(2,1)S(1)} %collective-permute-done.8.refs_6_), channel_id=1, source_target_pairs={{0,1},{1,0},{2,3},{3,2},{4,5},{5,4},{6,7},{7,6},{8,9},{9,8},{10,11... | collective-permute-start | bytes 405512 | tf_op jit(solution)/shard_map/ppermute | solution.py:246
  35.0 12.3 %collective-permute-start.10 = (bf16[528,128]{1,0:T(8,128)(2,1)S(1)}, bf16[528,128]{1,0:T(8,128)(2,1)S(1)}, u32[]{:S(2)}, u32[]{:S(2)}) collective-permute-start(bf16[528,128]{1,0:T(8,128)(2,1)S(1)} %collective-permute-done.3.refs_4_), channel_id=1, source_target_pairs={{0,1},{1,0},{2,3},{3,2},{4,5},{5,4},{6,7},{7,6},{8,9},{9,8},{10,11... | collective-permute-start | bytes 405512 | tf_op jit(solution)/shard_map/ppermute | solution.py:246
  35.5 11.8 %collective-permute-start.11 = (bf16[528,128]{1,0:T(8,128)(2,1)S(1)}, bf16[528,128]{1,0:T(8,128)(2,1)S(1)}, u32[]{:S(2)}, u32[]{:S(2)}) collective-permute-start(bf16[528,128]{1,0:T(8,128)(2,1)S(1)} %collective-permute-done.5.refs_5_), channel_id=1, source_target_pairs={{0,1},{1,0},{2,3},{3,2},{4,5},{5,4},{6,7},{7,6},{8,9},{9,8},{10,11... | collective-permute-start | bytes 405512 | tf_op jit(solution)/shard_map/ppermute | solution.py:246
  39.4 7.9 %collective-permute-start.12 = (bf16[528,128]{1,0:T(8,128)(2,1)S(1)}, bf16[528,128]{1,0:T(8,128)(2,1)S(1)}, u32[]{:S(2)}, u32[]{:S(2)}) collective-permute-start(bf16[528,128]{1,0:T(8,128)(2,1)S(1)} %collective-permute-done.7.refs_6_), channel_id=1, source_target_pairs={{0,1},{1,0},{2,3},{3,2},{4,5},{5,4},{6,7},{7,6},{8,9},{9,8},{10,11... | collective-permute-start | bytes 405512 | tf_op jit(solution)/shard_map/ppermute | solution.py:246
  41.9 5.4 %collective-permute-start.13 = (bf16[528,128]{1,0:T(8,128)(2,1)S(1)}, bf16[528,128]{1,0:T(8,128)(2,1)S(1)}, u32[]{:S(2)}, u32[]{:S(2)}) collective-permute-start(bf16[528,128]{1,0:T(8,128)(2,1)S(1)} %collective-permute-done.9.refs_7_), channel_id=1, source_target_pairs={{0,1},{1,0},{2,3},{3,2},{4,5},{5,4},{6,7},{7,6},{8,9},{9,8},{10,11... | collective-permute-start | bytes 405512 | tf_op jit(solution)/shard_map/ppermute | solution.py:246
  53.1 5.9 %collective-permute-start.19 = (bf16[128,256]{1,0:T(8,128)(2,1)S(1)}, bf16[128,256]{1,0:T(8,128)(2,1)S(1)}, u32[]{:S(2)}, u32[]{:S(2)}) collective-permute-start(bf16[128,256]{1,0:T(8,128)(2,1)S(1)} %get-tuple-element.28), channel_id=1, source_target_pairs={{0,4},{1,5},{2,6},{3,7},{4,0},{5,1},{6,2},{7,3},{8,12},{9,13},{10,... | collective-permute-start | bytes 196616 | tf_op jit(solution)/shard_map/ppermute | solution.py:246
  53.4 7.0 %collective-permute-start.21 = (bf16[128,256]{1,0:T(8,128)(2,1)S(1)}, bf16[128,256]{1,0:T(8,128)(2,1)S(1)}, u32[]{:S(2)}, u32[]{:S(2)}) collective-permute-start(bf16[128,256]{1,0:T(8,128)(2,1)S(1)} %get-tuple-element.29), channel_id=1, source_target_pairs={{0,8},{1,9},{2,10},{3,11},{4,12},{5,13},{6,14},{7,15},{8,0},{9,1},... | collective-permute-start | bytes 196616 | tf_op jit(solution)/shard_map/ppermute | solution.py:246
  56.2 6.1 %collective-permute-start.23 = (bf16[128,256]{1,0:T(8,128)(2,1)S(1)}, bf16[128,256]{1,0:T(8,128)(2,1)S(1)}, u32[]{:S(2)}, u32[]{:S(2)}) collective-permute-start(bf16[128,256]{1,0:T(8,128)(2,1)S(1)} %get-tuple-element.30), channel_id=1, source_target_pairs={{0,12},{1,13},{2,14},{3,15},{4,8},{5,9},{6,10},{7,11},{8,4},{9,5},... | collective-permute-start | bytes 196616 | tf_op jit(solution)/shard_map/ppermute | solution.py:246
  57.5 8.3 %collective-permute-start.18 = (bf16[128,256]{1,0:T(8,128)(2,1)S(1)}, bf16[128,256]{1,0:T(8,128)(2,1)S(1)}, u32[]{:S(2)}, u32[]{:S(2)}) collective-permute-start(bf16[128,256]{1,0:T(8,128)(2,1)S(1)} %get-tuple-element.27.refs_0_), channel_id=1, source_target_pairs={{0,16},{16,0},{1,17},{17,1},{2,18},{18,2},{3,19},{19,3},{4,20},{20... | collective-permute-start | bytes 196616 | tf_op jit(solution)/shard_map/ppermute | solution.py:326
  59.0 6.8 %collective-permute-start.20 = (bf16[128,256]{1,0:T(8,128)(2,1)S(1)}, bf16[128,256]{1,0:T(8,128)(2,1)S(1)}, u32[]{:S(2)}, u32[]{:S(2)}) collective-permute-start(bf16[128,256]{1,0:T(8,128)(2,1)S(1)} %collective-permute-done.19.refs_1_), channel_id=1, source_target_pairs={{0,16},{16,0},{1,17},{17,1},{2,18},{18,2},{3,19},{19,3},{4,20},{20... | collective-permute-start | bytes 196616 | tf_op jit(solution)/shard_map/ppermute | solution.py:326
  60.4 5.4 %collective-permute-start.22 = (bf16[128,256]{1,0:T(8,128)(2,1)S(1)}, bf16[128,256]{1,0:T(8,128)(2,1)S(1)}, u32[]{:S(2)}, u32[]{:S(2)}) collective-permute-start(bf16[128,256]{1,0:T(8,128)(2,1)S(1)} %collective-permute-done.21.refs_2_), channel_id=1, source_target_pairs={{0,16},{16,0},{1,17},{17,1},{2,18},{18,2},{3,19},{19,3},{4,20},{20... | collective-permute-start | bytes 196616 | tf_op jit(solution)/shard_map/ppermute | solution.py:326
  62.2 4.3 %collective-permute-start.24 = (bf16[128,256]{1,0:T(8,128)(2,1)S(1)}, bf16[128,256]{1,0:T(8,128)(2,1)S(1)}, u32[]{:S(2)}, u32[]{:S(2)}) collective-permute-start(bf16[128,256]{1,0:T(8,128)(2,1)S(1)} %collective-permute-done.23.refs_3_), channel_id=1, source_target_pairs={{0,16},{16,0},{1,17},{17,1},{2,18},{18,2},{3,19},{19,3},{4,20},{20... | collective-permute-start | bytes 196616 | tf_op jit(solution)/shard_map/ppermute | solution.py:326

commit v4 on v3

--- a/solution.py
+++ b/solution.py
@@ -104,17 +104,17 @@
         for tile in range(width // LANES):
             at = slice(tile * LANES, (tile + 1) * LANES)
             normed = head_normal(query[:, at], gain, head).astype(jnp.bfloat16)
-            slots[slot][:, at] = normed * jnp.asarray(head ** (-0.5), jnp.bfloat16)
+            slots[slot][at, :] = (normed * jnp.asarray(head ** (-0.5), jnp.bfloat16)).T
 
 
 def attention_kernel(*refs, held, head, earlier):
     queries, refs = refs[:WAYS], refs[WAYS:]
     pieces, refs = refs[:held], refs[held:]
     if earlier:
-        before, *outs, k_all, v_all, b_all, q_all, o_all = refs
+        before, *outs, k_all, v_all, b_all, s_all, o_all = refs
     else:
-        o_all, k_all, v_all, b_all, q_all = refs
-    rows, width = queries[0].shape
+        o_all, k_all, v_all, b_all, s_all = refs
+    width, rows = queries[0].shape
     heads = width // head
     tiles = width // LANES
     deep = head + EXTRA
@@ -139,39 +139,53 @@
         for i in range(len(some)):
             to = (first + i) * rows
             b_all[to : to + rows, :] = jnp.broadcast_to(columns[:, i : i + 1], (rows, LANES))
-    for slot in range(WAYS):
-        q_all[slot * rows : (slot + 1) * rows, :] = queries[slot][...]
-    lane = lax.broadcasted_iota(jnp.int32, (1, width), 1)
     span = 2 * rows
-
-    def one_block(index, _):
-        query = q_all[pl.ds(pl.multiple_of(index * span, span), span), :]
-        columns = []
-        for h in range(heads):
-            inside = (lane >= h * head) & (lane < (h + 1) * head)
-            masked = jnp.where(inside, query, jnp.zeros_like(query))
-            scores = lax.dot_general(k_all[...], masked, (((1,), (1,)), ((), ())), preferred_element_type=jnp.float32)
-            bias = b_all[...]
-            scores = scores + jnp.concatenate([bias] * (span // LANES), axis=-1)
-            highest = jnp.max(scores, axis=0, keepdims=True)
-            expo = jnp.exp(scores - highest).astype(jnp.bfloat16)
-            numer = jnp.dot(v_all[h], expo, preferred_element_type=jnp.float32)
-            at = h * deep
-            if earlier:
-                highest_before = before[index, at + head + 8 : at + head + 9, :]
-                most = jnp.maximum(highest, highest_before)
-                now, then = jnp.exp(highest - most), jnp.exp(highest_before - most)
-                total = numer[head : head + 1, :] * now + before[index, at + head : at + head + 1, :] * then
-                both = numer[:head, :] * now + before[index, at : at + head, :] * then
-                columns.append(both / total)
-            else:
-                o_all[index, at : at + head + 8, :] = numer[: head + 8, :]
-                o_all[index, at + head + 8 : at + deep, :] = jnp.broadcast_to(highest, (deep - head - 8, span))
+    chunk = 2 * rows
+    chunks = k_all.shape[0] // chunk
+    steps = [(index, h) for index in range(WAYS // 2) for h in range(heads)]
+
+    def one_head(step):
+        index, h = steps[step]
+        query = jnp.concatenate([queries[2 * index + i][h * head : (h + 1) * head, :] for i in range(2)], axis=1)
+        sides = [jnp.zeros((n * head, span), jnp.bfloat16) for n in (h, heads - 1 - h)]
+        return jnp.concatenate([x for x in (sides[0], query, sides[1]) if x.shape[0]], axis=0)
+
+    def score(step, at, query, highest):
+        scores = jnp.dot(k_all[at : at + chunk, :], query, preferred_element_type=jnp.float32)
+        scores = scores + jnp.concatenate([b_all[at : at + chunk, :]] * (span // LANES), axis=-1)
+        s_all[step % 2, at : at + chunk, :] = scores
+        most = jnp.max(scores, axis=0, keepdims=True)
+        return most if highest is None else jnp.maximum(highest, most)
+
+    def finish(step, highest, numer):
+        index, h = steps[step]
+        at = h * deep
         if earlier:
-            o_all[index] = jnp.concatenate(columns, axis=0)
-        return 0
-
-    lax.fori_loop(0, WAYS // 2, one_block, 0)
+            highest_before = before[index, at + head + 8 : at + head + 9, :]
+            most = jnp.maximum(highest, highest_before)
+            now, then = jnp.exp(highest - most), jnp.exp(highest_before - most)
+            total = numer[head : head + 1, :] * now + before[index, at + head : at + head + 1, :] * then
+            both = numer[:head, :] * now + before[index, at : at + head, :] * then
+            o_all[index, h * head : (h + 1) * head, :] = both / total
+        else:
+            o_all[index, at : at + head + 8, :] = numer[: head + 8, :]
+            o_all[index, at + head + 8 : at + deep, :] = jnp.broadcast_to(highest, (deep - head - 8, span))
+
+    highest = None
+    for step in range(len(steps) + 1):
+        ready, highest = highest, None
+        query = one_head(step) if step < len(steps) else None
+        numer = jnp.zeros((deep, span), jnp.float32)
+        for c in range(chunks):
+            at = c * chunk
+            if query is not None:
+                highest = score(step, at, query, highest)
+            if step:
+                expo = jnp.exp(s_all[(step - 1) % 2, at : at + chunk, :] - ready).astype(jnp.bfloat16)
+                values = v_all[steps[step - 1][1], :, at : at + chunk]
+                numer += jnp.dot(values, expo, preferred_element_type=jnp.float32)
+        if step:
+            finish(step - 1, ready, numer)
     if earlier:
         for slot in range(WAYS):
             at = (slot % 2) * rows
@@ -269,7 +283,7 @@
         functools.partial(query_kernel, head=head, groups=groups),
         compiler_params=limit(10),
         in_specs=[vmem, hbm, vmem],
-        out_shape=[piece] * WAYS,
+        out_shape=[pltpu.VMEM((width, rows), bf16)] * WAYS,
         scratch_shapes=[pltpu.VMEM((features, inner), bf16), pltpu.SemaphoreType.DMA],
     )(held_in(modded), w_qkv, q_gain[None, :])
     queries = spread(q_slots)
@@ -310,7 +324,7 @@
                 pltpu.VMEM((keys, width), bf16),
                 pltpu.VMEM((width // head, deep, keys), bf16),
                 pltpu.VMEM((keys, LANES), jnp.float32),
-                pltpu.VMEM((WAYS * rows, width), bf16),
+                pltpu.VMEM((2, keys, 2 * rows), jnp.float32),
             ]
             + scratch,
         )(*ins)

time: 69 us -> 64.7 us (0.938)
  Pallas kernels: 23 us -> 18.8 us
    pallas_call x2, Pallas kernels: 11.1 us -> 6.7 us  [attend(): pl.pallas_call(functools.partial(attention_kernel, held=len(pieces), head...]
  transfers between devices with their start and end apart: 25 -> 25, of which waited for: 8 -> 8; matrix products, arithmetic and copies ran while one was open for 0% -> 0% of each run, Pallas kernels for 11% -> 8%
where the time goes in v4:
time: 64.7 us; the launch traced here: 64.5 us
  starting transfers between devices  25.2 us (39%)
  Pallas kernels  18.8 us (29%)
  waiting for transfers between devices  18.4 us (28%)
  between operations  1.44 us (2%)
  local copies, waits for them, and re-layouts  0.65 us (1%)
    ppermute x21, starting transfers between devices, exchange(): return lax.ppermute(x, 'seq', [(i, i ^ bits) for i in range(count)])  20.2 us
    ppermute x21, waiting for transfers between devices, exchange(): return lax.ppermute(x, 'seq', [(i, i ^ bits) for i in range(count)])  17.7 us
    pallas_call x2, Pallas kernels, attend(): pl.pallas_call(functools.partial(attention_kernel, held=len(pieces), head...  6.7 us
    ppermute x4, starting transfers between devices, block(): lax.ppermute(x, 'cfg', [(j, j ^ 1) for j in range(cfg_count)])  5.01 us
    pallas_call x1, Pallas kernels, block(): pl.pallas_call(functools.partial(key_value_kernel, head=head, groups=grou...  4.37 us
    pallas_call x1, Pallas kernels, block(): pl.pallas_call(functools.partial(query_kernel, head=head, groups=groups),...  3.45 us
    pallas_call x1, Pallas kernels, block(): pl.pallas_call(functools.partial(final_kernel, groups=groups, half=half),...  2.21 us
    pallas_call x1, Pallas kernels, block(): pl.pallas_call(fetch_kernel, compiler_params=limit(2), in_specs=[hbm], ou...  1.6 us
  transfers between devices with their start and end apart: 25, of which 8 were waited for; matrix products, arithmetic and copies ran while one was open for 0% of the time, Pallas kernels for 8%

profile of v4, /device:TPU:0, one launch (start us, length us, event | category | flops | bytes accessed | tf_op | source)
XLA Modules:
  0.0 64.5 jit_solution(14898969299930674829)
XLA Ops:
  1.3 0.6 %copy-done = f32[64]{0:T(128)S(1)} copy-done((f32[64]{0:T(128)S(1)}, f32[64]{0:T(128)}, u32[]{:S(2)}) %copy-start) | copy-done | bytes 280
  2.0 4.4 %shard_map.82 = (bf16[528,128]{1,0:T(8,128)(2,1)S(1)}, bf16[528,128]{1,0:T(8,128)(2,1)S(1)}, bf16[528,128]{1,0:T(8,128)(2,1)S(1)}, bf16[528,128]{1,0:T(8,128)(2,1)S(1)}, bf16[128,1920]{1,0:T(8,128)(2,1)S(1)}) custom-call(s32[1]{0:T(128)S(6)} %copy.10.block_ref, s32[1]{0:T(128)S(6)} %copy.9.count_ref, bf16[128,1920]{1,0:T(8,128)(2,1)} %bitcast.6, ...), custom_call_target="tpu_custom_call" | custom-call | tf_op jit(solution)/shard_map/pallas_call | solution.py:269
  6.3 3.4 %shard_map.83 = (bf16[256,128]{1,0:T(8,128)(2,1)S(1)}, bf16[256,128]{1,0:T(8,128)(2,1)S(1)}, bf16[256,128]{1,0:T(8,128)(2,1)S(1)}, bf16[256,128]{1,0:T(8,128)(2,1)S(1)}) custom-call(bf16[128,1920]{1,0:T(8,128)(2,1)S(1)} %get-tuple-element.18.modded_ref, bf16[3,1920,1024]{2,1,0:T(8,128)(2,1)} %w_ref.4, f32[1,64]{1,0:T(1,128)S(1)} %bitcast.5), custom_call_target="tpu_custom_call" | custom-call | tf_op jit(solution)/shard_map/pallas_call | solution.py:282
  9.8 3.1 %collective-permute-start = (bf16[256,128]{1,0:T(8,128)(2,1)S(1)}, bf16[256,128]{1,0:T(8,128)(2,1)S(1)}, u32[]{:S(2)}, u32[]{:S(2)}) collective-permute-start(bf16[256,128]{1,0:T(8,128)(2,1)S(1)} %get-tuple-element.20), channel_id=1, source_target_pairs={{0,4},{1,5},{2,6},{3,7},{4,0},{5,1},{6,2},{7,3},{8,12},{9,13},{10,... | collective-permute-start | bytes 196616 | tf_op jit(solution)/shard_map/ppermute | solution.py:260
  12.9 2.6 %collective-permute-start.1 = (bf16[256,128]{1,0:T(8,128)(2,1)S(1)}, bf16[256,128]{1,0:T(8,128)(2,1)S(1)}, u32[]{:S(2)}, u32[]{:S(2)}) collective-permute-start(bf16[256,128]{1,0:T(8,128)(2,1)S(1)} %get-tuple-element.21), channel_id=1, source_target_pairs={{0,8},{1,9},{2,10},{3,11},{4,12},{5,13},{6,14},{7,15},{8,0},{9,1},... | collective-permute-start | bytes 196616 | tf_op jit(solution)/shard_map/ppermute | solution.py:260
  15.5 0.9 %collective-permute-start.4 = (bf16[528,128]{1,0:T(8,128)(2,1)S(1)}, bf16[528,128]{1,0:T(8,128)(2,1)S(1)}, u32[]{:S(2)}, u32[]{:S(2)}) collective-permute-start(bf16[528,128]{1,0:T(8,128)(2,1)S(1)} %get-tuple-element.24), channel_id=1, source_target_pairs={{0,4},{1,5},{2,6},{3,7},{4,0},{5,1},{6,2},{7,3},{8,12},{9,13},{10,... | collective-permute-start | bytes 405512 | tf_op jit(solution)/shard_map/ppermute | solution.py:260
  16.4 2.9 %collective-permute-start.6 = (bf16[528,128]{1,0:T(8,128)(2,1)S(1)}, bf16[528,128]{1,0:T(8,128)(2,1)S(1)}, u32[]{:S(2)}, u32[]{:S(2)}) collective-permute-start(bf16[528,128]{1,0:T(8,128)(2,1)S(1)} %get-tuple-element.25), channel_id=1, source_target_pairs={{0,12},{1,13},{2,14},{3,15},{4,8},{5,9},{6,10},{7,11},{8,4},{9,5},... | collective-permute-start | bytes 405512 | tf_op jit(solution)/shard_map/ppermute | solution.py:260
  19.3 0.6 collective-permute-start.8
  20.2 2.1 %collective-permute-done.2.refs_3_ = bf16[256,128]{1,0:T(8,128)(2,1)S(1)} collective-permute-done((bf16[256,128]{1,0:T(8,128)(2,1)S(1)}, bf16[256,128]{1,0:T(8,128)(2,1)S(1)}, u32[]{:S(2)}, u32[]{:S(2)}) %collective-permute-start.2) | collective-permute-done | bytes 65568 | tf_op jit(solution)/shard_map/ppermute | solution.py:260
  22.4 1.5 %collective-permute-start.3 = (bf16[528,128]{1,0:T(8,128)(2,1)S(1)}, bf16[528,128]{1,0:T(8,128)(2,1)S(1)}, u32[]{:S(2)}, u32[]{:S(2)}) collective-permute-start(bf16[528,128]{1,0:T(8,128)(2,1)S(1)} %get-tuple-element.23.refs_4_), channel_id=1, source_target_pairs={{0,2},{1,3},{2,0},{3,1},{4,6},{5,7},{6,4},{7,5},{8,10},{9,11},{10,... | collective-permute-start | bytes 405512 | tf_op jit(solution)/shard_map/ppermute | solution.py:260
  23.9 3.9 %collective-permute-done.6.refs_7_ = bf16[528,128]{1,0:T(8,128)(2,1)S(1)} collective-permute-done((bf16[528,128]{1,0:T(8,128)(2,1)S(1)}, bf16[528,128]{1,0:T(8,128)(2,1)S(1)}, u32[]{:S(2)}, u32[]{:S(2)}) %collective-permute-start.6) | collective-permute-done | bytes 135200 | tf_op jit(solution)/shard_map/ppermute | solution.py:260
  27.8 1.5 %collective-permute-start.5 = (bf16[528,128]{1,0:T(8,128)(2,1)S(1)}, bf16[528,128]{1,0:T(8,128)(2,1)S(1)}, u32[]{:S(2)}, u32[]{:S(2)}) collective-permute-start(bf16[528,128]{1,0:T(8,128)(2,1)S(1)} %collective-permute-done.4.refs_5_), channel_id=1, source_target_pairs={{0,2},{1,3},{2,0},{3,1},{4,6},{5,7},{6,4},{7,5},{8,10},{9,11},{10,... | collective-permute-start | bytes 405512 | tf_op jit(solution)/shard_map/ppermute | solution.py:260
  29.4 3.8 %collective-permute-done.8.refs_6_ = bf16[528,128]{1,0:T(8,128)(2,1)S(1)} collective-permute-done((bf16[528,128]{1,0:T(8,128)(2,1)S(1)}, bf16[528,128]{1,0:T(8,128)(2,1)S(1)}, u32[]{:S(2)}, u32[]{:S(2)}) %collective-permute-start.8) | collective-permute-done | bytes 135200 | tf_op jit(solution)/shard_map/ppermute | solution.py:260
  33.2 1.5 %collective-permute-start.7 = (bf16[528,128]{1,0:T(8,128)(2,1)S(1)}, bf16[528,128]{1,0:T(8,128)(2,1)S(1)}, u32[]{:S(2)}, u32[]{:S(2)}) collective-permute-start(bf16[528,128]{1,0:T(8,128)(2,1)S(1)} %collective-permute-done.6.refs_7_), channel_id=1, source_target_pairs={{0,2},{1,3},{2,0},{3,1},{4,6},{5,7},{6,4},{7,5},{8,10},{9,11},{10,... | collective-permute-start | bytes 405512 | tf_op jit(solution)/shard_map/ppermute | solution.py:260
  34.7 0.5 collective-permute-start.9
  35.2 0.5 collective-permute-start.10
  35.8 3.8 %collective-permute-done.7.refs_6_ = bf16[528,128]{1,0:T(8,128)(2,1)S(1)} collective-permute-done((bf16[528,128]{1,0:T(8,128)(2,1)S(1)}, bf16[528,128]{1,0:T(8,128)(2,1)S(1)}, u32[]{:S(2)}, u32[]{:S(2)}) %collective-permute-start.7) | collective-permute-done | bytes 135200 | tf_op jit(solution)/shard_map/ppermute | solution.py:260
  39.6 2.4 %collective-permute-done.9.refs_7_ = bf16[528,128]{1,0:T(8,128)(2,1)S(1)} collective-permute-done((bf16[528,128]{1,0:T(8,128)(2,1)S(1)}, bf16[528,128]{1,0:T(8,128)(2,1)S(1)}, u32[]{:S(2)}, u32[]{:S(2)}) %collective-permute-start.9) | collective-permute-done | bytes 135200 | tf_op jit(solution)/shard_map/ppermute | solution.py:260
  42.1 3.2 %shard_map.84.refs_12_ = f32[2,320,256]{2,1,0:T(8,128)S(1)} custom-call(bf16[256,128]{1,0:T(8,128)(2,1)S(1)} %get-tuple-element.19.refs_0_, bf16[256,128]{1,0:T(8,128)(2,1)S(1)} %collective-permute-done.refs_1_, bf16[256,128]{1,0:T(8,128)(2,1)S(1)} %collective-permute-done.1.refs_2_, bf16[256,128]{1,0:T(8,128)(2,1)S(1)} %collective-permute-done.2.refs_3_, ...), custom_call_target="tpu_custom_call" | custom-call | tf_op jit(solution)/shard_map/pallas_call | solution.py:318
  45.3 3.5 %shard_map.85 = (bf16[128,256]{1,0:T(8,128)(2,1)S(1)}, bf16[128,256]{1,0:T(8,128)(2,1)S(1)}, bf16[128,256]{1,0:T(8,128)(2,1)S(1)}, bf16[128,256]{1,0:T(8,128)(2,1)S(1)}) custom-call(bf16[256,128]{1,0:T(8,128)(2,1)S(1)} %get-tuple-element.19.refs_0_, bf16[256,128]{1,0:T(8,128)(2,1)S(1)} %collective-permute-done.refs_1_, ...), custom_call_target="tpu_custom_call" | custom-call | tf_op jit(solution)/shard_map/pallas_call | solution.py:318
  48.8 0.4 collective-permute-start.19
  49.2 2.7 %collective-permute-start.21 = (bf16[128,256]{1,0:T(8,128)(2,1)S(1)}, bf16[128,256]{1,0:T(8,128)(2,1)S(1)}, u32[]{:S(2)}, u32[]{:S(2)}) collective-permute-start(bf16[128,256]{1,0:T(8,128)(2,1)S(1)} %get-tuple-element.29), channel_id=1, source_target_pairs={{0,8},{1,9},{2,10},{3,11},{4,12},{5,13},{6,14},{7,15},{8,0},{9,1},... | collective-permute-start | bytes 196616 | tf_op jit(solution)/shard_map/ppermute | solution.py:260
  51.9 1.3 %collective-permute-start.23 = (bf16[128,256]{1,0:T(8,128)(2,1)S(1)}, bf16[128,256]{1,0:T(8,128)(2,1)S(1)}, u32[]{:S(2)}, u32[]{:S(2)}) collective-permute-start(bf16[128,256]{1,0:T(8,128)(2,1)S(1)} %get-tuple-element.30), channel_id=1, source_target_pairs={{0,12},{1,13},{2,14},{3,15},{4,8},{5,9},{6,10},{7,11},{8,4},{9,5},... | collective-permute-start | bytes 196616 | tf_op jit(solution)/shard_map/ppermute | solution.py:260
  53.3 1.5 %collective-permute-start.18 = (bf16[128,256]{1,0:T(8,128)(2,1)S(1)}, bf16[128,256]{1,0:T(8,128)(2,1)S(1)}, u32[]{:S(2)}, u32[]{:S(2)}) collective-permute-start(bf16[128,256]{1,0:T(8,128)(2,1)S(1)} %get-tuple-element.27.refs_0_), channel_id=1, source_target_pairs={{0,16},{16,0},{1,17},{17,1},{2,18},{18,2},{3,19},{19,3},{4,20},{20... | collective-permute-start | bytes 196616 | tf_op jit(solution)/shard_map/ppermute | solution.py:340
  54.8 1.4 %collective-permute-start.20 = (bf16[128,256]{1,0:T(8,128)(2,1)S(1)}, bf16[128,256]{1,0:T(8,128)(2,1)S(1)}, u32[]{:S(2)}, u32[]{:S(2)}) collective-permute-start(bf16[128,256]{1,0:T(8,128)(2,1)S(1)} %collective-permute-done.19.refs_1_), channel_id=1, source_target_pairs={{0,16},{16,0},{1,17},{17,1},{2,18},{18,2},{3,19},{19,3},{4,20},{20... | collective-permute-start | bytes 196616 | tf_op jit(solution)/shard_map/ppermute | solution.py:340
  56.2 0.6 collective-permute-start.22
  56.8 1.2 %collective-permute-done.23.refs_3_ = bf16[128,256]{1,0:T(8,128)(2,1)S(1)} collective-permute-done((bf16[128,256]{1,0:T(8,128)(2,1)S(1)}, bf16[128,256]{1,0:T(8,128)(2,1)S(1)}, u32[]{:S(2)}, u32[]{:S(2)}) %collective-permute-start.23) | collective-permute-done | bytes 65568 | tf_op jit(solution)/shard_map/ppermute | solution.py:260
  58.0 1.5 %collective-permute-start.24 = (bf16[128,256]{1,0:T(8,128)(2,1)S(1)}, bf16[128,256]{1,0:T(8,128)(2,1)S(1)}, u32[]{:S(2)}, u32[]{:S(2)}) collective-permute-start(bf16[128,256]{1,0:T(8,128)(2,1)S(1)} %collective-permute-done.23.refs_3_), channel_id=1, source_target_pairs={{0,16},{16,0},{1,17},{17,1},{2,18},{18,2},{3,19},{19,3},{4,20},{20... | collective-permute-start | bytes 196616 | tf_op jit(solution)/shard_map/ppermute | solution.py:340
  59.5 1.6 %shard_map.86.refs_4_.refs_5_ = bf16[1024,1024]{1,0:T(8,128)(2,1)S(1)} custom-call(bf16[1024,1920]{1,0:T(8,128)(2,1)} %w_ref.5), custom_call_target="tpu_custom_call" | custom-call | tf_op jit(solution)/shard_map/pallas_call | solution.py:292
  61.1 0.5 shard_map.87.refs_4_
  61.6 0.7 %collective-permute-done.24.refs_3_ = bf16[128,256]{1,0:T(8,128)(2,1)S(1)} collective-permute-done((bf16[128,256]{1,0:T(8,128)(2,1)S(1)}, bf16[128,256]{1,0:T(8,128)(2,1)S(1)}, u32[]{:S(2)}, u32[]{:S(2)}) %collective-permute-start.24) | collective-permute-done | bytes 65568 | tf_op jit(solution)/shard_map/ppermute | solution.py:340
  62.3 2.2 %shard_map.88 = f32[960,128]{1,0:T(8,128)} custom-call(s32[1]{0:T(128)S(6)} %copy.10.block_ref, bf16[128,256]{1,0:T(8,128)(2,1)S(1)} %collective-permute-done.18.refs_0_, bf16[128,256]{1,0:T(8,128)(2,1)S(1)} %collective-permute-done.20.refs_1_, bf16[128,256]{1,0:T(8,128)(2,1)S(1)} %collective-permute-done.22.refs_2_, ...), custom_call_target="tpu_custom_call" | custom-call | tf_op jit(solution)/shard_map/pallas_call | solution.py:347
  (29 shorter events, 0.5 us)
Async XLA Ops:
  1.3 0.7 %copy-start = (f32[64]{0:T(128)S(1)}, f32[64]{0:T(128)}, u32[]{:S(2)}) copy-start(f32[64]{0:T(128)} %param.12) | copy-start | bytes 772
  2.0 4.4 %copy-start.1 = (f32[64]{0:T(128)S(1)}, f32[64]{0:T(128)}, u32[]{:S(2)}) copy-start(f32[64]{0:T(128)} %param.11) | copy-start | bytes 772
  9.8 9.5 %collective-permute-start = (bf16[256,128]{1,0:T(8,128)(2,1)S(1)}, bf16[256,128]{1,0:T(8,128)(2,1)S(1)}, u32[]{:S(2)}, u32[]{:S(2)}) collective-permute-start(bf16[256,128]{1,0:T(8,128)(2,1)S(1)} %get-tuple-element.20), channel_id=1, source_target_pairs={{0,4},{1,5},{2,6},{3,7},{4,0},{5,1},{6,2},{7,3},{8,12},{9,13},{10,... | collective-permute-start | bytes 196616 | tf_op jit(solution)/shard_map/ppermute | solution.py:260
  12.9 7.3 %collective-permute-start.1 = (bf16[256,128]{1,0:T(8,128)(2,1)S(1)}, bf16[256,128]{1,0:T(8,128)(2,1)S(1)}, u32[]{:S(2)}, u32[]{:S(2)}) collective-permute-start(bf16[256,128]{1,0:T(8,128)(2,1)S(1)} %get-tuple-element.21), channel_id=1, source_target_pairs={{0,8},{1,9},{2,10},{3,11},{4,12},{5,13},{6,14},{7,15},{8,0},{9,1},... | collective-permute-start | bytes 196616 | tf_op jit(solution)/shard_map/ppermute | solution.py:260
  15.5 6.9 %collective-permute-start.2 = (bf16[256,128]{1,0:T(8,128)(2,1)S(1)}, bf16[256,128]{1,0:T(8,128)(2,1)S(1)}, u32[]{:S(2)}, u32[]{:S(2)}) collective-permute-start(bf16[256,128]{1,0:T(8,128)(2,1)S(1)} %get-tuple-element.22), channel_id=1, source_target_pairs={{0,12},{1,13},{2,14},{3,15},{4,8},{5,9},{6,10},{7,11},{8,4},{9,5},... | collective-permute-start | bytes 196616 | tf_op jit(solution)/shard_map/ppermute | solution.py:260
  15.5 8.4 %collective-permute-start.4 = (bf16[528,128]{1,0:T(8,128)(2,1)S(1)}, bf16[528,128]{1,0:T(8,128)(2,1)S(1)}, u32[]{:S(2)}, u32[]{:S(2)}) collective-permute-start(bf16[528,128]{1,0:T(8,128)(2,1)S(1)} %get-tuple-element.24), channel_id=1, source_target_pairs={{0,4},{1,5},{2,6},{3,7},{4,0},{5,1},{6,2},{7,3},{8,12},{9,13},{10,... | collective-permute-start | bytes 405512 | tf_op jit(solution)/shard_map/ppermute | solution.py:260
  16.4 11.4 %collective-permute-start.6 = (bf16[528,128]{1,0:T(8,128)(2,1)S(1)}, bf16[528,128]{1,0:T(8,128)(2,1)S(1)}, u32[]{:S(2)}, u32[]{:S(2)}) collective-permute-start(bf16[528,128]{1,0:T(8,128)(2,1)S(1)} %get-tuple-element.25), channel_id=1, source_target_pairs={{0,12},{1,13},{2,14},{3,15},{4,8},{5,9},{6,10},{7,11},{8,4},{9,5},... | collective-permute-start | bytes 405512 | tf_op jit(solution)/shard_map/ppermute | solution.py:260
  19.3 13.8 %collective-permute-start.8 = (bf16[528,128]{1,0:T(8,128)(2,1)S(1)}, bf16[528,128]{1,0:T(8,128)(2,1)S(1)}, u32[]{:S(2)}, u32[]{:S(2)}) collective-permute-start(bf16[528,128]{1,0:T(8,128)(2,1)S(1)} %get-tuple-element.26), channel_id=1, source_target_pairs={{0,8},{1,9},{2,10},{3,11},{4,12},{5,13},{6,14},{7,15},{8,0},{9,1},... | collective-permute-start | bytes 405512 | tf_op jit(solution)/shard_map/ppermute | solution.py:260
  20.2 12.9 %collective-permute-start.14 = (bf16[528,128]{1,0:T(8,128)(2,1)S(1)}, bf16[528,128]{1,0:T(8,128)(2,1)S(1)}, u32[]{:S(2)}, u32[]{:S(2)}) collective-permute-start(bf16[528,128]{1,0:T(8,128)(2,1)S(1)} %get-tuple-element.23.refs_4_), channel_id=1, source_target_pairs={{0,1},{1,0},{2,3},{3,2},{4,5},{5,4},{6,7},{7,6},{8,9},{9,8},{10,11... | collective-permute-start | bytes 405512 | tf_op jit(solution)/shard_map/ppermute | solution.py:260
  22.4 12.3 %collective-permute-start.3 = (bf16[528,128]{1,0:T(8,128)(2,1)S(1)}, bf16[528,128]{1,0:T(8,128)(2,1)S(1)}, u32[]{:S(2)}, u32[]{:S(2)}) collective-permute-start(bf16[528,128]{1,0:T(8,128)(2,1)S(1)} %get-tuple-element.23.refs_4_), channel_id=1, source_target_pairs={{0,2},{1,3},{2,0},{3,1},{4,6},{5,7},{6,4},{7,5},{8,10},{9,11},{10,... | collective-permute-start | bytes 405512 | tf_op jit(solution)/shard_map/ppermute | solution.py:260
  23.9 11.3 %collective-permute-start.15 = (bf16[528,128]{1,0:T(8,128)(2,1)S(1)}, bf16[528,128]{1,0:T(8,128)(2,1)S(1)}, u32[]{:S(2)}, u32[]{:S(2)}) collective-permute-start(bf16[528,128]{1,0:T(8,128)(2,1)S(1)} %collective-permute-done.4.refs_5_), channel_id=1, source_target_pairs={{0,1},{1,0},{2,3},{3,2},{4,5},{5,4},{6,7},{7,6},{8,9},{9,8},{10,11... | collective-permute-start | bytes 405512 | tf_op jit(solution)/shard_map/ppermute | solution.py:260
  27.8 7.4 %collective-permute-start.5 = (bf16[528,128]{1,0:T(8,128)(2,1)S(1)}, bf16[528,128]{1,0:T(8,128)(2,1)S(1)}, u32[]{:S(2)}, u32[]{:S(2)}) collective-permute-start(bf16[528,128]{1,0:T(8,128)(2,1)S(1)} %collective-permute-done.4.refs_5_), channel_id=1, source_target_pairs={{0,2},{1,3},{2,0},{3,1},{4,6},{5,7},{6,4},{7,5},{8,10},{9,11},{10,... | collective-permute-start | bytes 405512 | tf_op jit(solution)/shard_map/ppermute | solution.py:260
  33.2 2.6 %collective-permute-start.17 = (bf16[528,128]{1,0:T(8,128)(2,1)S(1)}, bf16[528,128]{1,0:T(8,128)(2,1)S(1)}, u32[]{:S(2)}, u32[]{:S(2)}) collective-permute-start(bf16[528,128]{1,0:T(8,128)(2,1)S(1)} %collective-permute-done.6.refs_7_), channel_id=1, source_target_pairs={{0,1},{1,0},{2,3},{3,2},{4,5},{5,4},{6,7},{7,6},{8,9},{9,8},{10,11... | collective-permute-start | bytes 405512 | tf_op jit(solution)/shard_map/ppermute | solution.py:260
  33.2 6.5 %collective-permute-start.7 = (bf16[528,128]{1,0:T(8,128)(2,1)S(1)}, bf16[528,128]{1,0:T(8,128)(2,1)S(1)}, u32[]{:S(2)}, u32[]{:S(2)}) collective-permute-start(bf16[528,128]{1,0:T(8,128)(2,1)S(1)} %collective-permute-done.6.refs_7_), channel_id=1, source_target_pairs={{0,2},{1,3},{2,0},{3,1},{4,6},{5,7},{6,4},{7,5},{8,10},{9,11},{10,... | collective-permute-start | bytes 405512 | tf_op jit(solution)/shard_map/ppermute | solution.py:260
  34.7 7.4 %collective-permute-start.9 = (bf16[528,128]{1,0:T(8,128)(2,1)S(1)}, bf16[528,128]{1,0:T(8,128)(2,1)S(1)}, u32[]{:S(2)}, u32[]{:S(2)}) collective-permute-start(bf16[528,128]{1,0:T(8,128)(2,1)S(1)} %collective-permute-done.8.refs_6_), channel_id=1, source_target_pairs={{0,2},{1,3},{2,0},{3,1},{4,6},{5,7},{6,4},{7,5},{8,10},{9,11},{10,... | collective-permute-start | bytes 405512 | tf_op jit(solution)/shard_map/ppermute | solution.py:260
  35.2 6.9 %collective-permute-start.16 = (bf16[528,128]{1,0:T(8,128)(2,1)S(1)}, bf16[528,128]{1,0:T(8,128)(2,1)S(1)}, u32[]{:S(2)}, u32[]{:S(2)}) collective-permute-start(bf16[528,128]{1,0:T(8,128)(2,1)S(1)} %collective-permute-done.8.refs_6_), channel_id=1, source_target_pairs={{0,1},{1,0},{2,3},{3,2},{4,5},{5,4},{6,7},{7,6},{8,9},{9,8},{10,11... | collective-permute-start | bytes 405512 | tf_op jit(solution)/shard_map/ppermute | solution.py:260
  35.2 10.1 %collective-permute-start.10 = (bf16[528,128]{1,0:T(8,128)(2,1)S(1)}, bf16[528,128]{1,0:T(8,128)(2,1)S(1)}, u32[]{:S(2)}, u32[]{:S(2)}) collective-permute-start(bf16[528,128]{1,0:T(8,128)(2,1)S(1)} %collective-permute-done.3.refs_4_), channel_id=1, source_target_pairs={{0,1},{1,0},{2,3},{3,2},{4,5},{5,4},{6,7},{7,6},{8,9},{9,8},{10,11... | collective-permute-start | bytes 405512 | tf_op jit(solution)/shard_map/ppermute | solution.py:260
  35.7 9.6 %collective-permute-start.11 = (bf16[528,128]{1,0:T(8,128)(2,1)S(1)}, bf16[528,128]{1,0:T(8,128)(2,1)S(1)}, u32[]{:S(2)}, u32[]{:S(2)}) collective-permute-start(bf16[528,128]{1,0:T(8,128)(2,1)S(1)} %collective-permute-done.5.refs_5_), channel_id=1, source_target_pairs={{0,1},{1,0},{2,3},{3,2},{4,5},{5,4},{6,7},{7,6},{8,9},{9,8},{10,11... | collective-permute-start | bytes 405512 | tf_op jit(solution)/shard_map/ppermute | solution.py:260
  39.6 5.7 %collective-permute-start.12 = (bf16[528,128]{1,0:T(8,128)(2,1)S(1)}, bf16[528,128]{1,0:T(8,128)(2,1)S(1)}, u32[]{:S(2)}, u32[]{:S(2)}) collective-permute-start(bf16[528,128]{1,0:T(8,128)(2,1)S(1)} %collective-permute-done.7.refs_6_), channel_id=1, source_target_pairs={{0,1},{1,0},{2,3},{3,2},{4,5},{5,4},{6,7},{7,6},{8,9},{9,8},{10,11... | collective-permute-start | bytes 405512 | tf_op jit(solution)/shard_map/ppermute | solution.py:260
  42.1 3.3 %collective-permute-start.13 = (bf16[528,128]{1,0:T(8,128)(2,1)S(1)}, bf16[528,128]{1,0:T(8,128)(2,1)S(1)}, u32[]{:S(2)}, u32[]{:S(2)}) collective-permute-start(bf16[528,128]{1,0:T(8,128)(2,1)S(1)} %collective-permute-done.9.refs_7_), channel_id=1, source_target_pairs={{0,1},{1,0},{2,3},{3,2},{4,5},{5,4},{6,7},{7,6},{8,9},{9,8},{10,11... | collective-permute-start | bytes 405512 | tf_op jit(solution)/shard_map/ppermute | solution.py:260
  48.8 5.9 %collective-permute-start.19 = (bf16[128,256]{1,0:T(8,128)(2,1)S(1)}, bf16[128,256]{1,0:T(8,128)(2,1)S(1)}, u32[]{:S(2)}, u32[]{:S(2)}) collective-permute-start(bf16[128,256]{1,0:T(8,128)(2,1)S(1)} %get-tuple-element.28), channel_id=1, source_target_pairs={{0,4},{1,5},{2,6},{3,7},{4,0},{5,1},{6,2},{7,3},{8,12},{9,13},{10,... | collective-permute-start | bytes 196616 | tf_op jit(solution)/shard_map/ppermute | solution.py:260
  49.2 7.0 %collective-permute-start.21 = (bf16[128,256]{1,0:T(8,128)(2,1)S(1)}, bf16[128,256]{1,0:T(8,128)(2,1)S(1)}, u32[]{:S(2)}, u32[]{:S(2)}) collective-permute-start(bf16[128,256]{1,0:T(8,128)(2,1)S(1)} %get-tuple-element.29), channel_id=1, source_target_pairs={{0,8},{1,9},{2,10},{3,11},{4,12},{5,13},{6,14},{7,15},{8,0},{9,1},... | collective-permute-start | bytes 196616 | tf_op jit(solution)/shard_map/ppermute | solution.py:260
  51.9 6.1 %collective-permute-start.23 = (bf16[128,256]{1,0:T(8,128)(2,1)S(1)}, bf16[128,256]{1,0:T(8,128)(2,1)S(1)}, u32[]{:S(2)}, u32[]{:S(2)}) collective-permute-start(bf16[128,256]{1,0:T(8,128)(2,1)S(1)} %get-tuple-element.30), channel_id=1, source_target_pairs={{0,12},{1,13},{2,14},{3,15},{4,8},{5,9},{6,10},{7,11},{8,4},{9,5},... | collective-permute-start | bytes 196616 | tf_op jit(solution)/shard_map/ppermute | solution.py:260
  53.3 8.3 %collective-permute-start.18 = (bf16[128,256]{1,0:T(8,128)(2,1)S(1)}, bf16[128,256]{1,0:T(8,128)(2,1)S(1)}, u32[]{:S(2)}, u32[]{:S(2)}) collective-permute-start(bf16[128,256]{1,0:T(8,128)(2,1)S(1)} %get-tuple-element.27.refs_0_), channel_id=1, source_target_pairs={{0,16},{16,0},{1,17},{17,1},{2,18},{18,2},{3,19},{19,3},{4,20},{20... | collective-permute-start | bytes 196616 | tf_op jit(solution)/shard_map/ppermute | solution.py:340
  54.8 6.8 %collective-permute-start.20 = (bf16[128,256]{1,0:T(8,128)(2,1)S(1)}, bf16[128,256]{1,0:T(8,128)(2,1)S(1)}, u32[]{:S(2)}, u32[]{:S(2)}) collective-permute-start(bf16[128,256]{1,0:T(8,128)(2,1)S(1)} %collective-permute-done.19.refs_1_), channel_id=1, source_target_pairs={{0,16},{16,0},{1,17},{17,1},{2,18},{18,2},{3,19},{19,3},{4,20},{20... | collective-permute-start | bytes 196616 | tf_op jit(solution)/shard_map/ppermute | solution.py:340
  56.2 5.4 %collective-permute-start.22 = (bf16[128,256]{1,0:T(8,128)(2,1)S(1)}, bf16[128,256]{1,0:T(8,128)(2,1)S(1)}, u32[]{:S(2)}, u32[]{:S(2)}) collective-permute-start(bf16[128,256]{1,0:T(8,128)(2,1)S(1)} %collective-permute-done.21.refs_2_), channel_id=1, source_target_pairs={{0,16},{16,0},{1,17},{17,1},{2,18},{18,2},{3,19},{19,3},{4,20},{20... | collective-permute-start | bytes 196616 | tf_op jit(solution)/shard_map/ppermute | solution.py:340
  58.0 4.3 %collective-permute-start.24 = (bf16[128,256]{1,0:T(8,128)(2,1)S(1)}, bf16[128,256]{1,0:T(8,128)(2,1)S(1)}, u32[]{:S(2)}, u32[]{:S(2)}) collective-permute-start(bf16[128,256]{1,0:T(8,128)(2,1)S(1)} %collective-permute-done.23.refs_3_), channel_id=1, source_target_pairs={{0,16},{16,0},{1,17},{17,1},{2,18},{18,2},{3,19},{19,3},{4,20},{20... | collective-permute-start | bytes 196616 | tf_op jit(solution)/shard_map/ppermute | solution.py:340

commit v5 on v4

--- a/solution.py
+++ b/solution.py
@@ -54,10 +54,11 @@
 
 
 def key_value_kernel(block_ref, count_ref, hidden_ref, modulation_ref, w_ref, gain_ref, *refs, head, groups):
-    slots, (modded_ref, states, table, w_all, sems) = refs[:WAYS], refs[WAYS:]
+    slots, (modded_ref, states, table, gains, w_all, sems) = refs[:WAYS], refs[WAYS:]
     first = [
         pltpu.make_async_copy(hidden_ref, states, sems.at[2]),
         pltpu.make_async_copy(modulation_ref, table, sems.at[3]),
+        pltpu.make_async_copy(gain_ref, gains, sems.at[4]),
     ]
     copies = [pltpu.make_async_copy(w_ref.at[1 + i], w_all.at[i], sems.at[i]) for i in range(2)]
     for copy in first + copies:
@@ -68,7 +69,7 @@
     modded_ref[...] = modulate(block, states[...].astype(jnp.float32), table)
     rows = modded_ref.shape[0]
     width = w_all.shape[2] // WAYS
-    gain = wide(gain_ref[...])
+    gain = wide(gains[...])
     way = lax.axis_index("seq") // groups
     position = block * rows + lax.broadcasted_iota(jnp.int32, (EXTRA, rows), 1)
     keep = (position >= TXT) | (position < count_ref[0])
@@ -91,11 +92,14 @@
 
 
 def query_kernel(modded_ref, w_ref, gain_ref, *refs, head, groups):
-    slots, (w_all, sem) = refs[:WAYS], refs[WAYS:]
-    copy = pltpu.make_async_copy(w_ref.at[0], w_all, sem)
+    slots, (gains, w_all, sems) = refs[:WAYS], refs[WAYS:]
+    copy = pltpu.make_async_copy(w_ref.at[0], w_all, sems.at[0])
     copy.start()
+    small = pltpu.make_async_copy(gain_ref, gains, sems.at[1])
+    small.start()
+    small.wait()
     width = w_all.shape[1] // WAYS
-    gain = wide(gain_ref[...])
+    gain = wide(gains[...])
     way = lax.axis_index("seq") // groups
     copy.wait()
     for slot in range(WAYS):
@@ -107,13 +111,18 @@
             slots[slot][at, :] = (normed * jnp.asarray(head ** (-0.5), jnp.bfloat16)).T
 
 
-def attention_kernel(*refs, held, head, earlier):
-    queries, refs = refs[:WAYS], refs[WAYS:]
+def attention_kernel(*refs, queries, held, outs, head, earlier):
+    queries, refs = refs[:queries], refs[queries:]
     pieces, refs = refs[:held], refs[held:]
-    if earlier:
-        before, *outs, k_all, v_all, b_all, s_all, o_all = refs
+    if earlier is not None:
+        before, refs = refs[0], refs[1:]
+    if earlier is None:
+        o_all, k_all, v_all, b_all, s_all = refs
+    elif held:
+        outs, (k_all, v_all, b_all, s_all, o_all) = refs[:outs], refs[outs:]
     else:
-        o_all, k_all, v_all, b_all, s_all = refs
+        (k_all, v_all, b_all), refs = refs[:3], refs[3:]
+        outs, (s_all, o_all) = refs[:outs], refs[outs:]
     width, rows = queries[0].shape
     heads = width // head
     tiles = width // LANES
@@ -130,7 +139,7 @@
             at += EXTRA
             for h in range(heads):
                 v_all[h, :head, to : to + rows] = pieces[g][at + h * head : at + (h + 1) * head, :]
-    for h in range(heads):
+    for h in range(heads if held else 0):
         v_all[h, head:, :] = jnp.ones((EXTRA, v_all.shape[2]), jnp.bfloat16)
     for first in range(0, len(biases), LANES):
         some = biases[first : first + LANES]
@@ -142,7 +151,7 @@
     span = 2 * rows
     chunk = 2 * rows
     chunks = k_all.shape[0] // chunk
-    steps = [(index, h) for index in range(WAYS // 2) for h in range(heads)]
+    steps = [(index, h) for index in range(len(queries) // 2) for h in range(heads)]
 
     def one_head(step):
         index, h = steps[step]
@@ -160,12 +169,13 @@
     def finish(step, highest, numer):
         index, h = steps[step]
         at = h * deep
-        if earlier:
-            highest_before = before[index, at + head + 8 : at + head + 9, :]
+        if earlier is not None:
+            past = earlier + index
+            highest_before = before[past, at + head + 8 : at + head + 9, :]
             most = jnp.maximum(highest, highest_before)
             now, then = jnp.exp(highest - most), jnp.exp(highest_before - most)
-            total = numer[head : head + 1, :] * now + before[index, at + head : at + head + 1, :] * then
-            both = numer[:head, :] * now + before[index, at : at + head, :] * then
+            total = numer[head : head + 1, :] * now + before[past, at + head : at + head + 1, :] * then
+            both = numer[:head, :] * now + before[past, at : at + head, :] * then
             o_all[index, h * head : (h + 1) * head, :] = both / total
         else:
             o_all[index, at : at + head + 8, :] = numer[: head + 8, :]
@@ -186,8 +196,8 @@
                 numer += jnp.dot(values, expo, preferred_element_type=jnp.float32)
         if step:
             finish(step - 1, ready, numer)
-    if earlier:
-        for slot in range(WAYS):
+    if earlier is not None:
+        for slot in range(len(queries)):
             at = (slot % 2) * rows
             outs[slot][...] = o_all[slot // 2, :, at : at + rows].T.astype(jnp.bfloat16)
 
@@ -198,10 +208,16 @@
     return spare, span, pl.multiple_of(lax.axis_index("cfg") * (half - spare), LANES)
 
 
-def fetch_kernel(w_ref, out_ref, sem):
+def fetch_kernel(block_ref, w_ref, modulation_ref, out_ref, gate_ref, table, sems):
     _, span, start = half_of(w_ref.shape[1] // 2)
-    copy = pltpu.make_async_copy(w_ref.at[:, pl.ds(start, span)], out_ref, sem)
+    small = pltpu.make_async_copy(modulation_ref, table, sems.at[0])
+    copy = pltpu.make_async_copy(w_ref.at[:, pl.ds(start, span)], out_ref, sems.at[1])
+    small.start()
     copy.start()
+    small.wait()
+    is_text = text_rows(block_ref[0], gate_ref.shape[0])
+    gates = table[:, pl.ds(start, span)]
+    gate_ref[...] = jnp.where(is_text, gates[5:6, :], gates[2:3, :])
     copy.wait()
 
 
@@ -215,19 +231,15 @@
 
 
 def own_kernel(*refs, groups):
-    *pieces, w_ref, out_ref = refs
-    out_ref[...] = project(pieces, w_ref, lax.axis_index("seq") // groups)
-
-
-def final_kernel(block_ref, *refs, groups, half):
-    *pieces, own_ref, w_ref, modulation_ref, out_ref = refs
-    spare, span, start = half_of(half)
-    total = project(pieces, w_ref, lax.axis_index("seq") // groups)
-    is_text = text_rows(block_ref[0], total.shape[0])
-    table = modulation_ref[:, pl.ds(start, span)]
-    gate = jnp.where(is_text, table[5:6, :], table[2:3, :])
-    other = gate * total
-    own = gate * own_ref[...]
+    *pieces, gate_ref, w_ref, out_ref = refs
+    out_ref[...] = gate_ref[...] * project(pieces, w_ref, lax.axis_index("seq") // groups)
+
+
+def final_kernel(*refs, groups, half):
+    *pieces, own_ref, gate_ref, w_ref, out_ref = refs
+    spare = half_of(half)[0]
+    other = gate_ref[...] * project(pieces, w_ref, lax.axis_index("seq") // groups)
+    own = own_ref[...]
     is_first = lax.axis_index("cfg") == 0
     cond = jnp.where(is_first, own, other)
     uncond = jnp.where(is_first, other, own)
@@ -251,9 +263,8 @@
     def limit(mib):
         return pltpu.CompilerParams(vmem_limit_bytes=min(mib, 60) * 2**20)
 
-    w_qkv, w_out, states, modulation = (
-        pltpu.with_memory_space_constraint(x, pltpu.HBM) for x in (w_qkv, w_out, states, modulation)
-    )
+    in_hbm = functools.partial(pltpu.with_memory_space_constraint, memory_space=pltpu.HBM)
+    w_qkv, w_out, states, modulation = map(in_hbm, (w_qkv, w_out, states, modulation))
     held_in = functools.partial(pltpu.with_memory_space_constraint, memory_space=pltpu.VMEM)
 
     def exchange(x, bits):
@@ -269,33 +280,38 @@
     *kv_slots, modded = pl.pallas_call(
         functools.partial(key_value_kernel, head=head, groups=groups),
         compiler_params=limit(16),
-        in_specs=[smem, smem, hbm, hbm, hbm, vmem],
+        in_specs=[smem, smem, hbm, hbm, hbm, hbm],
         out_shape=[kv_piece] * WAYS + [pltpu.VMEM((rows, features), bf16)],
         scratch_shapes=[
             pltpu.VMEM((rows, features), bf16),
             pltpu.VMEM(modulation.shape, jnp.float32),
+            pltpu.VMEM((1, head), jnp.float32),
             pltpu.VMEM((2, features, inner), bf16),
-            pltpu.SemaphoreType.DMA((4,)),
+            pltpu.SemaphoreType.DMA((5,)),
         ],
-    )(block_order, text_count, states, modulation, w_qkv, k_gain[None, :])
+    )(block_order, text_count, states, modulation, w_qkv, in_hbm(k_gain[None, :]))
     kv = spread(kv_slots)
     q_slots = pl.pallas_call(
         functools.partial(query_kernel, head=head, groups=groups),
         compiler_params=limit(10),
-        in_specs=[vmem, hbm, vmem],
+        in_specs=[vmem, hbm, hbm],
         out_shape=[pltpu.VMEM((width, rows), bf16)] * WAYS,
-        scratch_shapes=[pltpu.VMEM((features, inner), bf16), pltpu.SemaphoreType.DMA],
-    )(held_in(modded), w_qkv, q_gain[None, :])
+        scratch_shapes=[
+            pltpu.VMEM((1, head), jnp.float32),
+            pltpu.VMEM((features, inner), bf16),
+            pltpu.SemaphoreType.DMA((2,)),
+        ],
+    )(held_in(modded), w_qkv, in_hbm(q_gain[None, :]))
     queries = spread(q_slots)
     half = w_out.shape[1] // 2
     span = half + half % LANES
-    w_half = pl.pallas_call(
+    w_half, gate = pl.pallas_call(
         fetch_kernel,
-        compiler_params=limit(2),
-        in_specs=[hbm],
-        out_shape=pltpu.VMEM((inner, span), bf16),
-        scratch_shapes=[pltpu.SemaphoreType.DMA],
-    )(w_out)
+        compiler_params=limit(3),
+        in_specs=[smem, hbm, hbm],
+        out_shape=[pltpu.VMEM((inner, span), bf16), pltpu.VMEM((rows, span), jnp.float32)],
+        scratch_shapes=[pltpu.VMEM(modulation.shape, jnp.float32), pltpu.SemaphoreType.DMA((2,))],
+    )(block_order, w_out, modulation)
     top = groups // 2
 
     def gathered(held):
@@ -313,27 +329,33 @@
     deep = head + EXTRA
     roomy = count * rows <= 4096
 
-    def attend(pieces, before, out_shape, scratch):
-        ins = [held_in(x) if roomy else x for x in [*queries, *pieces]] + before
+    laid = [
+        pltpu.VMEM((keys, width), bf16),
+        pltpu.VMEM((width // head, deep, keys), bf16),
+        pltpu.VMEM((keys, LANES), jnp.float32),
+    ]
+    scores = pltpu.VMEM((2, keys, 2 * rows), jnp.float32)
+
+    def attend(slots, pieces, more, earlier, outs, out_shape, scratch):
+        ins = [held_in(x) if roomy else x for x in [*slots, *pieces]] + more
         return pl.pallas_call(
-            functools.partial(attention_kernel, held=len(pieces), head=head, earlier=bool(before)),
+            functools.partial(
+                attention_kernel, queries=len(slots), held=len(pieces), outs=outs, head=head, earlier=earlier
+            ),
             compiler_params=limit(8 + keys // 96),
             in_specs=[vmem] * len(ins),
             out_shape=out_shape,
-            scratch_shapes=[
-                pltpu.VMEM((keys, width), bf16),
-                pltpu.VMEM((width // head, deep, keys), bf16),
-                pltpu.VMEM((keys, LANES), jnp.float32),
-                pltpu.VMEM((2, keys, 2 * rows), jnp.float32),
-            ]
-            + scratch,
+            scratch_shapes=scratch,
         )(*ins)
 
     part = pltpu.VMEM((WAYS // 2, deep * (width // head), 2 * rows), jnp.float32)
-    before = attend(near, [], part, [])
-    merged = pltpu.VMEM((WAYS // 2, width, 2 * rows), jnp.float32)
-    o_slots = attend(far, [held_in(before)], [piece] * WAYS, [merged])
-    attended = spread(o_slots)
+    merged = pltpu.VMEM((1, width, 2 * rows), jnp.float32)
+    before = held_in(attend(queries, near, [], None, 0, [part], laid + [scores])[0])
+    *o_far, k_all, v_all, b_all = attend(
+        queries[2:], far, [before], 1, 2, [piece] * 2 + laid, [scores, merged])
+    o_near = attend(
+        queries[:2], [], [before, held_in(k_all), held_in(v_all), held_in(b_all)], 0, 2, [piece] * 2, [scores, merged])
+    attended = spread([*o_near, *o_far])
     cfg_count = lax.axis_size("cfg")
     partner = []
     for x in attended:
@@ -341,15 +363,15 @@
     own = pl.pallas_call(
         functools.partial(own_kernel, groups=groups),
         compiler_params=limit(6),
-        in_specs=[vmem] * (WAYS + 1),
+        in_specs=[vmem] * (WAYS + 2),
         out_shape=pltpu.VMEM((rows, span), jnp.float32),
-    )(*map(held_in, attended), held_in(w_half))
+    )(*map(held_in, [*attended, gate, w_half]))
     guided = pl.pallas_call(
         functools.partial(final_kernel, groups=groups, half=half),
         compiler_params=limit(8),
-        in_specs=[smem] + [vmem] * (WAYS + 3),
+        in_specs=[vmem] * (WAYS + 3),
         out_shape=jax.ShapeDtypeStruct((half, rows), jnp.float32),
-    )(block_order, *map(held_in, partner), held_in(own), held_in(w_half), modulation)
+    )(*map(held_in, [*partner, own, gate, w_half]))
     return guided.T
 
 

time: 64.7 us -> 63.6 us (0.983)
  Pallas kernels: 18.8 us -> 18.1 us
  local copies, waits for them, and re-layouts: 0.65 us -> 0 us
    ppermute x4, waiting for transfers between devices: 0.67 us -> 1.62 us  [block(): lax.ppermute(x, 'cfg', [(j, j ^ 1) for j in range(cfg_count)])]
    ppermute x4, starting transfers between devices: 5.01 us -> 4.05 us  [block(): lax.ppermute(x, 'cfg', [(j, j ^ 1) for j in range(cfg_count)])]
    pallas_call x1, Pallas kernels: 2.21 us -> 1.38 us  [block(): pl.pallas_call(functools.partial(final_kernel, groups=groups, half=half),...]
    unnamed x4 -> x0, local copies, waits for them, and re-layouts: 0.65 us -> none
    pallas_call x3 -> x4, Pallas kernels: 8.29 us -> 8.43 us  [the longest x3 6.79 us: attend(): pl.pallas_call(functools.partial(attention_kernel, queries=len(slots), he...]
  transfers between devices with their start and end apart: 25 -> 25, of which waited for: 8 -> 9; matrix products, arithmetic and copies ran while one was open for 0% -> 0% of each run, Pallas kernels for 8% -> 8%
where the time goes in v5:
time: 63.6 us; the launch traced here: 63.5 us
  starting transfers between devices  24.9 us (39%)
  waiting for transfers between devices  19 us (30%)
  Pallas kernels  18.1 us (28%)
  between operations  1.42 us (2%)
    ppermute x21, starting transfers between devices, exchange(): return lax.ppermute(x, 'seq', [(i, i ^ bits) for i in range(count)])  20.8 us
    ppermute x21, waiting for transfers between devices, exchange(): return lax.ppermute(x, 'seq', [(i, i ^ bits) for i in range(count)])  17.4 us
    pallas_call x3, Pallas kernels, attend(): pl.pallas_call(functools.partial(attention_kernel, queries=len(slots), he...  6.79 us
    pallas_call x1, Pallas kernels, block(): pl.pallas_call(functools.partial(key_value_kernel, head=head, groups=grou...  4.41 us
    ppermute x4, starting transfers between devices, block(): lax.ppermute(x, 'cfg', [(j, j ^ 1) for j in range(cfg_count)])  4.05 us
    pallas_call x1, Pallas kernels, block(): pl.pallas_call(functools.partial(query_kernel, head=head, groups=groups),...  3.46 us
    pallas_call x1, Pallas kernels, block(): pl.pallas_call(fetch_kernel, compiler_params=limit(3), in_specs=[smem, hb...  1.64 us
    ppermute x4, waiting for transfers between devices, block(): lax.ppermute(x, 'cfg', [(j, j ^ 1) for j in range(cfg_count)])  1.62 us
  transfers between devices with their start and end apart: 25, of which 9 were waited for; matrix products, arithmetic and copies ran while one was open for 0% of the time, Pallas kernels for 8%

profile of v5, /device:TPU:0, one launch (start us, length us, event | category | flops | bytes accessed | tf_op | source)
XLA Modules:
  0.0 63.5 jit_solution(17210248369388732862)
XLA Ops:
  1.3 4.4 %shard_map.82 = (bf16[528,128]{1,0:T(8,128)(2,1)S(1)}, bf16[528,128]{1,0:T(8,128)(2,1)S(1)}, bf16[528,128]{1,0:T(8,128)(2,1)S(1)}, bf16[528,128]{1,0:T(8,128)(2,1)S(1)}, bf16[128,1920]{1,0:T(8,128)(2,1)S(1)}) custom-call(s32[1]{0:T(128)S(6)} %copy.10.block_ref, s32[1]{0:T(128)S(6)} %copy.9.count_ref, bf16[128,1920]{1,0:T(8,128)(2,1)} %bitcast.4, ...), custom_call_target="tpu_custom_call" | custom-call | tf_op jit(solution)/shard_map/pallas_call | solution.py:280
  5.7 3.5 %shard_map.83 = (bf16[256,128]{1,0:T(8,128)(2,1)S(1)}, bf16[256,128]{1,0:T(8,128)(2,1)S(1)}, bf16[256,128]{1,0:T(8,128)(2,1)S(1)}, bf16[256,128]{1,0:T(8,128)(2,1)S(1)}) custom-call(bf16[128,1920]{1,0:T(8,128)(2,1)S(1)} %get-tuple-element.23.modded_ref, bf16[3,1920,1024]{2,1,0:T(8,128)(2,1)} %w_ref.4, f32[1,64]{1,0:T(1,128)} %bitcast.6), custom_call_target="tpu_custom_call" | custom-call | tf_op jit(solution)/shard_map/pallas_call | solution.py:294
  9.2 3.1 %collective-permute-start = (bf16[256,128]{1,0:T(8,128)(2,1)S(1)}, bf16[256,128]{1,0:T(8,128)(2,1)S(1)}, u32[]{:S(2)}, u32[]{:S(2)}) collective-permute-start(bf16[256,128]{1,0:T(8,128)(2,1)S(1)} %get-tuple-element.25), channel_id=1, source_target_pairs={{0,4},{1,5},{2,6},{3,7},{4,0},{5,1},{6,2},{7,3},{8,12},{9,13},{10,... | collective-permute-start | bytes 196616 | tf_op jit(solution)/shard_map/ppermute | solution.py:271
  12.3 2.6 %collective-permute-start.1 = (bf16[256,128]{1,0:T(8,128)(2,1)S(1)}, bf16[256,128]{1,0:T(8,128)(2,1)S(1)}, u32[]{:S(2)}, u32[]{:S(2)}) collective-permute-start(bf16[256,128]{1,0:T(8,128)(2,1)S(1)} %get-tuple-element.26), channel_id=1, source_target_pairs={{0,8},{1,9},{2,10},{3,11},{4,12},{5,13},{6,14},{7,15},{8,0},{9,1},... | collective-permute-start | bytes 196616 | tf_op jit(solution)/shard_map/ppermute | solution.py:271
  14.9 0.9 %collective-permute-start.3 = (bf16[528,128]{1,0:T(8,128)(2,1)S(1)}, bf16[528,128]{1,0:T(8,128)(2,1)S(1)}, u32[]{:S(2)}, u32[]{:S(2)}) collective-permute-start(bf16[528,128]{1,0:T(8,128)(2,1)S(1)} %get-tuple-element.29), channel_id=1, source_target_pairs={{0,4},{1,5},{2,6},{3,7},{4,0},{5,1},{6,2},{7,3},{8,12},{9,13},{10,... | collective-permute-start | bytes 405512 | tf_op jit(solution)/shard_map/ppermute | solution.py:271
  15.8 3.5 %collective-permute-start.4 = (bf16[528,128]{1,0:T(8,128)(2,1)S(1)}, bf16[528,128]{1,0:T(8,128)(2,1)S(1)}, u32[]{:S(2)}, u32[]{:S(2)}) collective-permute-start(bf16[528,128]{1,0:T(8,128)(2,1)S(1)} %get-tuple-element.30), channel_id=1, source_target_pairs={{0,8},{1,9},{2,10},{3,11},{4,12},{5,13},{6,14},{7,15},{8,0},{9,1},... | collective-permute-start | bytes 405512 | tf_op jit(solution)/shard_map/ppermute | solution.py:271
  19.6 1.5 %collective-permute-start.10 = (bf16[528,128]{1,0:T(8,128)(2,1)S(1)}, bf16[528,128]{1,0:T(8,128)(2,1)S(1)}, u32[]{:S(2)}, u32[]{:S(2)}) collective-permute-start(bf16[528,128]{1,0:T(8,128)(2,1)S(1)} %get-tuple-element.28.refs_4_), channel_id=1, source_target_pairs={{0,2},{1,3},{2,0},{3,1},{4,6},{5,7},{6,4},{7,5},{8,10},{9,11},{10,... | collective-permute-start | bytes 405512 | tf_op jit(solution)/shard_map/ppermute | solution.py:271
  21.1 0.6 collective-permute-done.2.refs_3_.refs_1_
  21.8 1.0 %collective-permute-done.3.refs_5_ = bf16[528,128]{1,0:T(8,128)(2,1)S(1)} collective-permute-done((bf16[528,128]{1,0:T(8,128)(2,1)S(1)}, bf16[528,128]{1,0:T(8,128)(2,1)S(1)}, u32[]{:S(2)}, u32[]{:S(2)}) %collective-permute-start.3) | collective-permute-done | bytes 135200 | tf_op jit(solution)/shard_map/ppermute | solution.py:271
  22.7 1.5 %collective-permute-start.11 = (bf16[528,128]{1,0:T(8,128)(2,1)S(1)}, bf16[528,128]{1,0:T(8,128)(2,1)S(1)}, u32[]{:S(2)}, u32[]{:S(2)}) collective-permute-start(bf16[528,128]{1,0:T(8,128)(2,1)S(1)} %collective-permute-done.3.refs_5_), channel_id=1, source_target_pairs={{0,2},{1,3},{2,0},{3,1},{4,6},{5,7},{6,4},{7,5},{8,10},{9,11},{10,... | collective-permute-start | bytes 405512 | tf_op jit(solution)/shard_map/ppermute | solution.py:271
  24.2 6.2 %collective-permute-done.4.refs_6_ = bf16[528,128]{1,0:T(8,128)(2,1)S(1)} collective-permute-done((bf16[528,128]{1,0:T(8,128)(2,1)S(1)}, bf16[528,128]{1,0:T(8,128)(2,1)S(1)}, u32[]{:S(2)}, u32[]{:S(2)}) %collective-permute-start.4) | collective-permute-done | bytes 135200 | tf_op jit(solution)/shard_map/ppermute | solution.py:271
  30.4 1.5 %collective-permute-start.13 = (bf16[528,128]{1,0:T(8,128)(2,1)S(1)}, bf16[528,128]{1,0:T(8,128)(2,1)S(1)}, u32[]{:S(2)}, u32[]{:S(2)}) collective-permute-start(bf16[528,128]{1,0:T(8,128)(2,1)S(1)} %collective-permute-done.4.refs_6_), channel_id=1, source_target_pairs={{0,2},{1,3},{2,0},{3,1},{4,6},{5,7},{6,4},{7,5},{8,10},{9,11},{10,... | collective-permute-start | bytes 405512 | tf_op jit(solution)/shard_map/ppermute | solution.py:271
  32.2 0.5 collective-permute-start.12
  32.7 0.5 collective-permute-start.14
  33.2 3.7 %collective-permute-done.13.refs_5_ = bf16[528,128]{1,0:T(8,128)(2,1)S(1)} collective-permute-done((bf16[528,128]{1,0:T(8,128)(2,1)S(1)}, bf16[528,128]{1,0:T(8,128)(2,1)S(1)}, u32[]{:S(2)}, u32[]{:S(2)}) %collective-permute-start.13) | collective-permute-done | bytes 135200 | tf_op jit(solution)/shard_map/ppermute | solution.py:271
  36.9 0.5 collective-permute-start.17
  37.4 1.9 %collective-permute-done.12.refs_4_ = bf16[528,128]{1,0:T(8,128)(2,1)S(1)} collective-permute-done((bf16[528,128]{1,0:T(8,128)(2,1)S(1)}, bf16[528,128]{1,0:T(8,128)(2,1)S(1)}, u32[]{:S(2)}, u32[]{:S(2)}) %collective-permute-start.12) | collective-permute-done | bytes 135200 | tf_op jit(solution)/shard_map/ppermute | solution.py:271
  39.3 3.2 %shard_map.84.refs_10_.refs_2_ = f32[2,320,256]{2,1,0:T(8,128)S(1)} custom-call(bf16[256,128]{1,0:T(8,128)(2,1)S(1)} %get-tuple-element.24.refs_0_, bf16[256,128]{1,0:T(8,128)(2,1)S(1)} %collective-permute-done.refs_1_, bf16[256,128]{1,0:T(8,128)(2,1)S(1)} %collective-permute-done.1.refs_2_.refs_0_, ...), custom_call_target="tpu_custom_call" | custom-call | tf_op jit(solution)/shard_map/pallas_call | solution.py:341
  42.6 1.8 %shard_map.85 = (bf16[128,256]{1,0:T(8,128)(2,1)S(1)}, bf16[128,256]{1,0:T(8,128)(2,1)S(1)}, bf16[1024,256]{1,0:T(8,128)(2,1)S(1)}, bf16[4,80,1024]{2,1,0:T(8,128)(2,1)S(1)}, f32[1024,128]{1,0:T(8,128)S(1)}) custom-call(bf16[256,128]{1,0:T(8,128)(2,1)S(1)} %collective-permute-done.1.refs_2_.refs_0_, ...), custom_call_target="tpu_custom_call" | custom-call | tf_op jit(solution)/shard_map/pallas_call | solution.py:341
  44.4 1.7 %shard_map.86 = (bf16[128,256]{1,0:T(8,128)(2,1)S(1)}, bf16[128,256]{1,0:T(8,128)(2,1)S(1)}) custom-call(bf16[256,128]{1,0:T(8,128)(2,1)S(1)} %get-tuple-element.24.refs_0_, bf16[256,128]{1,0:T(8,128)(2,1)S(1)} %collective-permute-done.refs_1_, f32[2,320,256]{2,1,0:T(8,128)S(1)} %shard_map.84.refs_10_.refs_2_, ...), custom_call_target="tpu_custom_call" | custom-call | tf_op jit(solution)/shard_map/pallas_call | solution.py:341
  46.2 1.8 %collective-permute-start.19 = (bf16[128,256]{1,0:T(8,128)(2,1)S(1)}, bf16[128,256]{1,0:T(8,128)(2,1)S(1)}, u32[]{:S(2)}, u32[]{:S(2)}) collective-permute-start(bf16[128,256]{1,0:T(8,128)(2,1)S(1)} %get-tuple-element.36), channel_id=1, source_target_pairs={{0,4},{1,5},{2,6},{3,7},{4,0},{5,1},{6,2},{7,3},{8,12},{9,13},{10,... | collective-permute-start | bytes 196616 | tf_op jit(solution)/shard_map/ppermute | solution.py:271
  48.0 1.7 %collective-permute-start.21 = (bf16[128,256]{1,0:T(8,128)(2,1)S(1)}, bf16[128,256]{1,0:T(8,128)(2,1)S(1)}, u32[]{:S(2)}, u32[]{:S(2)}) collective-permute-start(bf16[128,256]{1,0:T(8,128)(2,1)S(1)} %get-tuple-element.37), channel_id=1, source_target_pairs={{0,8},{1,9},{2,10},{3,11},{4,12},{5,13},{6,14},{7,15},{8,0},{9,1},... | collective-permute-start | bytes 196616 | tf_op jit(solution)/shard_map/ppermute | solution.py:271
  49.7 1.0 %collective-permute-start.23 = (bf16[128,256]{1,0:T(8,128)(2,1)S(1)}, bf16[128,256]{1,0:T(8,128)(2,1)S(1)}, u32[]{:S(2)}, u32[]{:S(2)}) collective-permute-start(bf16[128,256]{1,0:T(8,128)(2,1)S(1)} %get-tuple-element.38), channel_id=1, source_target_pairs={{0,12},{1,13},{2,14},{3,15},{4,8},{5,9},{6,10},{7,11},{8,4},{9,5},... | collective-permute-start | bytes 196616 | tf_op jit(solution)/shard_map/ppermute | solution.py:271
  50.6 1.5 %collective-permute-start.18 = (bf16[128,256]{1,0:T(8,128)(2,1)S(1)}, bf16[128,256]{1,0:T(8,128)(2,1)S(1)}, u32[]{:S(2)}, u32[]{:S(2)}) collective-permute-start(bf16[128,256]{1,0:T(8,128)(2,1)S(1)} %get-tuple-element.35.refs_0_), channel_id=1, source_target_pairs={{0,16},{16,0},{1,17},{17,1},{2,18},{18,2},{3,19},{19,3},{4,20},{20... | collective-permute-start | bytes 196616 | tf_op jit(solution)/shard_map/ppermute | solution.py:362
  52.1 0.5 collective-permute-start.20
  52.6 3.7 %collective-permute-done.21.refs_2_ = bf16[128,256]{1,0:T(8,128)(2,1)S(1)} collective-permute-done((bf16[128,256]{1,0:T(8,128)(2,1)S(1)}, bf16[128,256]{1,0:T(8,128)(2,1)S(1)}, u32[]{:S(2)}, u32[]{:S(2)}) %collective-permute-start.21) | collective-permute-done | bytes 65568 | tf_op jit(solution)/shard_map/ppermute | solution.py:271
  56.3 1.5 %collective-permute-start.22 = (bf16[128,256]{1,0:T(8,128)(2,1)S(1)}, bf16[128,256]{1,0:T(8,128)(2,1)S(1)}, u32[]{:S(2)}, u32[]{:S(2)}) collective-permute-start(bf16[128,256]{1,0:T(8,128)(2,1)S(1)} %collective-permute-done.21.refs_2_), channel_id=1, source_target_pairs={{0,16},{16,0},{1,17},{17,1},{2,18},{18,2},{3,19},{19,3},{4,20},{20... | collective-permute-start | bytes 196616 | tf_op jit(solution)/shard_map/ppermute | solution.py:362
  57.8 0.5 collective-permute-start.24
  58.3 1.6 %shard_map.87 = (bf16[1024,1024]{1,0:T(8,128)(2,1)S(1)}, f32[128,1024]{1,0:T(8,128)S(1)}) custom-call(s32[1]{0:T(128)S(6)} %copy.10.block_ref, bf16[1024,1920]{1,0:T(8,128)(2,1)} %w_ref.5, f32[6,1920]{1,0:T(8,128)} %modulation_ref.3), custom_call_target="tpu_custom_call" | custom-call | tf_op jit(solution)/shard_map/pallas_call | solution.py:308
  60.0 0.5 shard_map.88.refs_4_
  60.6 1.5 %collective-permute-done.24.refs_3_ = bf16[128,256]{1,0:T(8,128)(2,1)S(1)} collective-permute-done((bf16[128,256]{1,0:T(8,128)(2,1)S(1)}, bf16[128,256]{1,0:T(8,128)(2,1)S(1)}, u32[]{:S(2)}, u32[]{:S(2)}) %collective-permute-start.24) | collective-permute-done | bytes 65568 | tf_op jit(solution)/shard_map/ppermute | solution.py:362
  62.1 1.4 %shard_map.89 = f32[960,128]{1,0:T(8,128)} custom-call(bf16[128,256]{1,0:T(8,128)(2,1)S(1)} %collective-permute-done.18.refs_0_, bf16[128,256]{1,0:T(8,128)(2,1)S(1)} %collective-permute-done.20.refs_1_, bf16[128,256]{1,0:T(8,128)(2,1)S(1)} %collective-permute-done.22.refs_2_, bf16[128,256]{1,0:T(8,128)(2,1)S(1)} %collective-permute-done.24.refs_3_, ...), custom_call_target="tpu_custom_call" | custom-call | tf_op jit(solution)/shard_map/pallas_call | solution.py:369
  (26 shorter events, 0.7 us)
Async XLA Ops:
  9.2 10.1 %collective-permute-start = (bf16[256,128]{1,0:T(8,128)(2,1)S(1)}, bf16[256,128]{1,0:T(8,128)(2,1)S(1)}, u32[]{:S(2)}, u32[]{:S(2)}) collective-permute-start(bf16[256,128]{1,0:T(8,128)(2,1)S(1)} %get-tuple-element.25), channel_id=1, source_target_pairs={{0,4},{1,5},{2,6},{3,7},{4,0},{5,1},{6,2},{7,3},{8,12},{9,13},{10,... | collective-permute-start | bytes 196616 | tf_op jit(solution)/shard_map/ppermute | solution.py:271
  12.3 7.3 %collective-permute-start.1 = (bf16[256,128]{1,0:T(8,128)(2,1)S(1)}, bf16[256,128]{1,0:T(8,128)(2,1)S(1)}, u32[]{:S(2)}, u32[]{:S(2)}) collective-permute-start(bf16[256,128]{1,0:T(8,128)(2,1)S(1)} %get-tuple-element.26), channel_id=1, source_target_pairs={{0,8},{1,9},{2,10},{3,11},{4,12},{5,13},{6,14},{7,15},{8,0},{9,1},... | collective-permute-start | bytes 196616 | tf_op jit(solution)/shard_map/ppermute | solution.py:271
  14.9 6.9 %collective-permute-start.2 = (bf16[256,128]{1,0:T(8,128)(2,1)S(1)}, bf16[256,128]{1,0:T(8,128)(2,1)S(1)}, u32[]{:S(2)}, u32[]{:S(2)}) collective-permute-start(bf16[256,128]{1,0:T(8,128)(2,1)S(1)} %get-tuple-element.27), channel_id=1, source_target_pairs={{0,12},{1,13},{2,14},{3,15},{4,8},{5,9},{6,10},{7,11},{8,4},{9,5},... | collective-permute-start | bytes 196616 | tf_op jit(solution)/shard_map/ppermute | solution.py:271
  14.9 7.8 %collective-permute-start.3 = (bf16[528,128]{1,0:T(8,128)(2,1)S(1)}, bf16[528,128]{1,0:T(8,128)(2,1)S(1)}, u32[]{:S(2)}, u32[]{:S(2)}) collective-permute-start(bf16[528,128]{1,0:T(8,128)(2,1)S(1)} %get-tuple-element.29), channel_id=1, source_target_pairs={{0,4},{1,5},{2,6},{3,7},{4,0},{5,1},{6,2},{7,3},{8,12},{9,13},{10,... | collective-permute-start | bytes 405512 | tf_op jit(solution)/shard_map/ppermute | solution.py:271
  15.8 14.6 %collective-permute-start.4 = (bf16[528,128]{1,0:T(8,128)(2,1)S(1)}, bf16[528,128]{1,0:T(8,128)(2,1)S(1)}, u32[]{:S(2)}, u32[]{:S(2)}) collective-permute-start(bf16[528,128]{1,0:T(8,128)(2,1)S(1)} %get-tuple-element.30), channel_id=1, source_target_pairs={{0,8},{1,9},{2,10},{3,11},{4,12},{5,13},{6,14},{7,15},{8,0},{9,1},... | collective-permute-start | bytes 405512 | tf_op jit(solution)/shard_map/ppermute | solution.py:271
  19.3 11.1 %collective-permute-start.5 = (bf16[528,128]{1,0:T(8,128)(2,1)S(1)}, bf16[528,128]{1,0:T(8,128)(2,1)S(1)}, u32[]{:S(2)}, u32[]{:S(2)}) collective-permute-start(bf16[528,128]{1,0:T(8,128)(2,1)S(1)} %get-tuple-element.31), channel_id=1, source_target_pairs={{0,12},{1,13},{2,14},{3,15},{4,8},{5,9},{6,10},{7,11},{8,4},{9,5},... | collective-permute-start | bytes 405512 | tf_op jit(solution)/shard_map/ppermute | solution.py:271
  19.6 12.3 %collective-permute-start.10 = (bf16[528,128]{1,0:T(8,128)(2,1)S(1)}, bf16[528,128]{1,0:T(8,128)(2,1)S(1)}, u32[]{:S(2)}, u32[]{:S(2)}) collective-permute-start(bf16[528,128]{1,0:T(8,128)(2,1)S(1)} %get-tuple-element.28.refs_4_), channel_id=1, source_target_pairs={{0,2},{1,3},{2,0},{3,1},{4,6},{5,7},{6,4},{7,5},{8,10},{9,11},{10,... | collective-permute-start | bytes 405512 | tf_op jit(solution)/shard_map/ppermute | solution.py:271
  21.7 10.4 %collective-permute-start.6 = (bf16[528,128]{1,0:T(8,128)(2,1)S(1)}, bf16[528,128]{1,0:T(8,128)(2,1)S(1)}, u32[]{:S(2)}, u32[]{:S(2)}) collective-permute-start(bf16[528,128]{1,0:T(8,128)(2,1)S(1)} %get-tuple-element.28.refs_4_), channel_id=1, source_target_pairs={{0,1},{1,0},{2,3},{3,2},{4,5},{5,4},{6,7},{7,6},{8,9},{9,8},{10,11... | collective-permute-start | bytes 405512 | tf_op jit(solution)/shard_map/ppermute | solution.py:271
  22.7 10.0 %collective-permute-start.11 = (bf16[528,128]{1,0:T(8,128)(2,1)S(1)}, bf16[528,128]{1,0:T(8,128)(2,1)S(1)}, u32[]{:S(2)}, u32[]{:S(2)}) collective-permute-start(bf16[528,128]{1,0:T(8,128)(2,1)S(1)} %collective-permute-done.3.refs_5_), channel_id=1, source_target_pairs={{0,2},{1,3},{2,0},{3,1},{4,6},{5,7},{6,4},{7,5},{8,10},{9,11},{10,... | collective-permute-start | bytes 405512 | tf_op jit(solution)/shard_map/ppermute | solution.py:271
  30.4 2.3 %collective-permute-start.7 = (bf16[528,128]{1,0:T(8,128)(2,1)S(1)}, bf16[528,128]{1,0:T(8,128)(2,1)S(1)}, u32[]{:S(2)}, u32[]{:S(2)}) collective-permute-start(bf16[528,128]{1,0:T(8,128)(2,1)S(1)} %collective-permute-done.3.refs_5_), channel_id=1, source_target_pairs={{0,1},{1,0},{2,3},{3,2},{4,5},{5,4},{6,7},{7,6},{8,9},{9,8},{10,11... | collective-permute-start | bytes 405512 | tf_op jit(solution)/shard_map/ppermute | solution.py:271
  30.4 6.5 %collective-permute-start.13 = (bf16[528,128]{1,0:T(8,128)(2,1)S(1)}, bf16[528,128]{1,0:T(8,128)(2,1)S(1)}, u32[]{:S(2)}, u32[]{:S(2)}) collective-permute-start(bf16[528,128]{1,0:T(8,128)(2,1)S(1)} %collective-permute-done.4.refs_6_), channel_id=1, source_target_pairs={{0,2},{1,3},{2,0},{3,1},{4,6},{5,7},{6,4},{7,5},{8,10},{9,11},{10,... | collective-permute-start | bytes 405512 | tf_op jit(solution)/shard_map/ppermute | solution.py:271
  31.9 4.9 %collective-permute-start.8 = (bf16[528,128]{1,0:T(8,128)(2,1)S(1)}, bf16[528,128]{1,0:T(8,128)(2,1)S(1)}, u32[]{:S(2)}, u32[]{:S(2)}) collective-permute-start(bf16[528,128]{1,0:T(8,128)(2,1)S(1)} %collective-permute-done.4.refs_6_), channel_id=1, source_target_pairs={{0,1},{1,0},{2,3},{3,2},{4,5},{5,4},{6,7},{7,6},{8,9},{9,8},{10,11... | collective-permute-start | bytes 405512 | tf_op jit(solution)/shard_map/ppermute | solution.py:271
  32.2 7.1 %collective-permute-start.12 = (bf16[528,128]{1,0:T(8,128)(2,1)S(1)}, bf16[528,128]{1,0:T(8,128)(2,1)S(1)}, u32[]{:S(2)}, u32[]{:S(2)}) collective-permute-start(bf16[528,128]{1,0:T(8,128)(2,1)S(1)} %collective-permute-done.5.refs_7_), channel_id=1, source_target_pairs={{0,2},{1,3},{2,0},{3,1},{4,6},{5,7},{6,4},{7,5},{8,10},{9,11},{10,... | collective-permute-start | bytes 405512 | tf_op jit(solution)/shard_map/ppermute | solution.py:271
  32.7 6.6 %collective-permute-start.9 = (bf16[528,128]{1,0:T(8,128)(2,1)S(1)}, bf16[528,128]{1,0:T(8,128)(2,1)S(1)}, u32[]{:S(2)}, u32[]{:S(2)}) collective-permute-start(bf16[528,128]{1,0:T(8,128)(2,1)S(1)} %collective-permute-done.5.refs_7_), channel_id=1, source_target_pairs={{0,1},{1,0},{2,3},{3,2},{4,5},{5,4},{6,7},{7,6},{8,9},{9,8},{10,11... | collective-permute-start | bytes 405512 | tf_op jit(solution)/shard_map/ppermute | solution.py:271
  32.7 9.8 %collective-permute-start.14 = (bf16[528,128]{1,0:T(8,128)(2,1)S(1)}, bf16[528,128]{1,0:T(8,128)(2,1)S(1)}, u32[]{:S(2)}, u32[]{:S(2)}) collective-permute-start(bf16[528,128]{1,0:T(8,128)(2,1)S(1)} %collective-permute-done.10.refs_2_), channel_id=1, source_target_pairs={{0,1},{1,0},{2,3},{3,2},{4,5},{5,4},{6,7},{7,6},{8,9},{9,8},{10,11... | collective-permute-start | bytes 405512 | tf_op jit(solution)/shard_map/ppermute | solution.py:271
  36.9 5.7 %collective-permute-start.15 = (bf16[528,128]{1,0:T(8,128)(2,1)S(1)}, bf16[528,128]{1,0:T(8,128)(2,1)S(1)}, u32[]{:S(2)}, u32[]{:S(2)}) collective-permute-start(bf16[528,128]{1,0:T(8,128)(2,1)S(1)} %collective-permute-done.11.refs_3_), channel_id=1, source_target_pairs={{0,1},{1,0},{2,3},{3,2},{4,5},{5,4},{6,7},{7,6},{8,9},{9,8},{10,11... | collective-permute-start | bytes 405512 | tf_op jit(solution)/shard_map/ppermute | solution.py:271
  36.9 5.7 %collective-permute-start.17 = (bf16[528,128]{1,0:T(8,128)(2,1)S(1)}, bf16[528,128]{1,0:T(8,128)(2,1)S(1)}, u32[]{:S(2)}, u32[]{:S(2)}) collective-permute-start(bf16[528,128]{1,0:T(8,128)(2,1)S(1)} %collective-permute-done.13.refs_5_), channel_id=1, source_target_pairs={{0,1},{1,0},{2,3},{3,2},{4,5},{5,4},{6,7},{7,6},{8,9},{9,8},{10,11... | collective-permute-start | bytes 405512 | tf_op jit(solution)/shard_map/ppermute | solution.py:271
  39.3 3.3 %collective-permute-start.16 = (bf16[528,128]{1,0:T(8,128)(2,1)S(1)}, bf16[528,128]{1,0:T(8,128)(2,1)S(1)}, u32[]{:S(2)}, u32[]{:S(2)}) collective-permute-start(bf16[528,128]{1,0:T(8,128)(2,1)S(1)} %collective-permute-done.12.refs_4_), channel_id=1, source_target_pairs={{0,1},{1,0},{2,3},{3,2},{4,5},{5,4},{6,7},{7,6},{8,9},{9,8},{10,11... | collective-permute-start | bytes 405512 | tf_op jit(solution)/shard_map/ppermute | solution.py:271
  46.2 5.9 %collective-permute-start.19 = (bf16[128,256]{1,0:T(8,128)(2,1)S(1)}, bf16[128,256]{1,0:T(8,128)(2,1)S(1)}, u32[]{:S(2)}, u32[]{:S(2)}) collective-permute-start(bf16[128,256]{1,0:T(8,128)(2,1)S(1)} %get-tuple-element.36), channel_id=1, source_target_pairs={{0,4},{1,5},{2,6},{3,7},{4,0},{5,1},{6,2},{7,3},{8,12},{9,13},{10,... | collective-permute-start | bytes 196616 | tf_op jit(solution)/shard_map/ppermute | solution.py:271
  48.0 8.4 %collective-permute-start.21 = (bf16[128,256]{1,0:T(8,128)(2,1)S(1)}, bf16[128,256]{1,0:T(8,128)(2,1)S(1)}, u32[]{:S(2)}, u32[]{:S(2)}) collective-permute-start(bf16[128,256]{1,0:T(8,128)(2,1)S(1)} %get-tuple-element.37), channel_id=1, source_target_pairs={{0,8},{1,9},{2,10},{3,11},{4,12},{5,13},{6,14},{7,15},{8,0},{9,1},... | collective-permute-start | bytes 196616 | tf_op jit(solution)/shard_map/ppermute | solution.py:271
  49.7 8.2 %collective-permute-start.23 = (bf16[128,256]{1,0:T(8,128)(2,1)S(1)}, bf16[128,256]{1,0:T(8,128)(2,1)S(1)}, u32[]{:S(2)}, u32[]{:S(2)}) collective-permute-start(bf16[128,256]{1,0:T(8,128)(2,1)S(1)} %get-tuple-element.38), channel_id=1, source_target_pairs={{0,12},{1,13},{2,14},{3,15},{4,8},{5,9},{6,10},{7,11},{8,4},{9,5},... | collective-permute-start | bytes 196616 | tf_op jit(solution)/shard_map/ppermute | solution.py:271
  50.6 9.9 %collective-permute-start.18 = (bf16[128,256]{1,0:T(8,128)(2,1)S(1)}, bf16[128,256]{1,0:T(8,128)(2,1)S(1)}, u32[]{:S(2)}, u32[]{:S(2)}) collective-permute-start(bf16[128,256]{1,0:T(8,128)(2,1)S(1)} %get-tuple-element.35.refs_0_), channel_id=1, source_target_pairs={{0,16},{16,0},{1,17},{17,1},{2,18},{18,2},{3,19},{19,3},{4,20},{20... | collective-permute-start | bytes 196616 | tf_op jit(solution)/shard_map/ppermute | solution.py:362
  52.1 8.4 %collective-permute-start.20 = (bf16[128,256]{1,0:T(8,128)(2,1)S(1)}, bf16[128,256]{1,0:T(8,128)(2,1)S(1)}, u32[]{:S(2)}, u32[]{:S(2)}) collective-permute-start(bf16[128,256]{1,0:T(8,128)(2,1)S(1)} %collective-permute-done.19.refs_1_), channel_id=1, source_target_pairs={{0,16},{16,0},{1,17},{17,1},{2,18},{18,2},{3,19},{19,3},{4,20},{20... | collective-permute-start | bytes 196616 | tf_op jit(solution)/shard_map/ppermute | solution.py:362
  56.3 4.3 %collective-permute-start.22 = (bf16[128,256]{1,0:T(8,128)(2,1)S(1)}, bf16[128,256]{1,0:T(8,128)(2,1)S(1)}, u32[]{:S(2)}, u32[]{:S(2)}) collective-permute-start(bf16[128,256]{1,0:T(8,128)(2,1)S(1)} %collective-permute-done.21.refs_2_), channel_id=1, source_target_pairs={{0,16},{16,0},{1,17},{17,1},{2,18},{18,2},{3,19},{19,3},{4,20},{20... | collective-permute-start | bytes 196616 | tf_op jit(solution)/shard_map/ppermute | solution.py:362
  57.8 4.3 %collective-permute-start.24 = (bf16[128,256]{1,0:T(8,128)(2,1)S(1)}, bf16[128,256]{1,0:T(8,128)(2,1)S(1)}, u32[]{:S(2)}, u32[]{:S(2)}) collective-permute-start(bf16[128,256]{1,0:T(8,128)(2,1)S(1)} %collective-permute-done.23.refs_3_), channel_id=1, source_target_pairs={{0,16},{16,0},{1,17},{17,1},{2,18},{18,2},{3,19},{19,3},{4,20},{20... | collective-permute-start | bytes 196616 | tf_op jit(solution)/shard_map/ppermute | solution.py:362
